TPU v7x, 8 devices: a whole 2x2x1 slice. The times are simulated.
8 devices in a mesh: rep: 1 (over z), mp: 2 (over y), tok: 4 (over x, core).
Axes of the slice: x: 2, y: 2, z: 1, core: 2. Of those that a mesh axis runs over, the one named last changes fastest.
Arguments:
- x_in: bfloat16 [2, 4096, 3584], P(None, ('rep', 'tok', 'mp'))
- seg_ids: int32 [2, 4096], P(None, ('rep', 'tok', 'mp'))
- g_attn: bfloat16 [2, 3584], replicated
- w_q: bfloat16 [2, 3584, 16, 256], P(None, 'tok', 'mp')
- w_k: bfloat16 [2, 3584, 8, 256], P(None, 'tok', 'mp')
- w_v: bfloat16 [2, 3584, 8, 256], P(None, 'tok', 'mp')
- w_o: bfloat16 [2, 16, 256, 3584], P(None, 'mp', None, 'tok')
- g_mlp: bfloat16 [2, 3584], replicated
- w_gate: bfloat16 [2, 3584, 14336], P(None, 'tok', 'mp')
- w_up: bfloat16 [2, 3584, 14336], P(None, 'tok', 'mp')
- w_down: bfloat16 [2, 14336, 3584], P(None, 'mp', 'tok')
Outputs:
- output: float32 [2, 4096, 3584], P(None, ('rep', 'tok', 'mp'))
All inputs are finite; a program needn't handle non-finite values.
Results may differ from a plain program's by a relative error of at most 0.00833919.
Values are sent between devices in bfloat16 or wider.
A program may use at most 1 GiB of HBM per device.

v0:
```python
import jax
import jax.numpy as jnp
from jax import lax
from jax.sharding import PartitionSpec as P

NORM_EPS = 1e-5
ROPE_BASE = 10000.0
NEG_BIG = -1e30


def rms_norm(resid, gain_vec):
    mean_sq = jnp.mean(resid * resid, axis=-1, keepdims=True)
    return (resid * lax.rsqrt(mean_sq + NORM_EPS) * gain_vec.astype(jnp.float32)).astype(jnp.bfloat16)


def seg_positions(seg_rows):
    positions = jnp.arange(seg_rows.shape[-1], dtype=jnp.int32)
    previous = jnp.concatenate([seg_rows[..., :1] - 1, seg_rows[..., :-1]], axis=-1)
    start_at = jnp.where(seg_rows != previous, positions, 0)
    return positions - lax.cummax(start_at, axis=seg_rows.ndim - 1)


def rope_tables(positions, head_dim):
    half_dim = head_dim // 2
    inv_freq = ROPE_BASE ** (-2.0 * jnp.arange(half_dim, dtype=jnp.float32) / head_dim)
    angles = positions.astype(jnp.float32)[..., None] * inv_freq
    return jnp.cos(angles), jnp.sin(angles)


def apply_rope(values, cos_t, sin_t):
    half_dim = values.shape[-1] // 2
    first_half = values[..., :half_dim]
    second_half = values[..., half_dim:]
    return jnp.concatenate([first_half * cos_t - second_half * sin_t, second_half * cos_t + first_half * sin_t], axis=-1)


def attend(q_rot, k_rot, v_val, allowed):
    scores = jnp.einsum('msngd,mtnd->mnsgt', q_rot, k_rot, preferred_element_type=jnp.float32) * q_rot.shape[-1] ** -0.5
    scores = jnp.where(allowed[:, None, :, None, :], scores, NEG_BIG)
    probs_bf = jax.nn.softmax(scores, axis=-1).astype(jnp.bfloat16)
    return jnp.einsum('mnsgt,mtnd->mnsgd', probs_bf, v_val, preferred_element_type=jnp.float32).astype(jnp.bfloat16)


def solution(mesh):
    act_spec = P(None, ('rep', 'tok', 'mp'), None)
    seg_spec = P(None, ('rep', 'tok', 'mp'))
    gain_spec = P(None, None)
    head_in = P(None, 'tok', 'mp', None)
    head_out = P(None, 'mp', None, 'tok')
    ffn_in = P(None, 'tok', 'mp')
    ffn_out = P(None, 'mp', 'tok')

    def device_fn(x_in, seg_ids, g_attn, w_q, w_k, w_v, w_o, g_mlp, w_gate, w_up, w_down):
        micro_n = x_in.shape[0]
        head_dim = w_q.shape[3]
        kv_heads = w_k.shape[2]
        groups = w_q.shape[2] // kv_heads
        seg_blk = lax.all_gather(seg_ids, 'mp', axis=1, tiled=True)
        blk_len = seg_blk.shape[1]
        tok_order = jnp.arange(blk_len)
        allowed = (seg_blk[:, :, None] == seg_blk[:, None, :]) & (tok_order[None, :] <= tok_order[:, None])
        cos_t, sin_t = rope_tables(seg_positions(seg_blk), head_dim)
        cos_t = cos_t[:, :, None, :]
        sin_t = sin_t[:, :, None, :]
        residual = x_in.astype(jnp.float32)
        for layer_idx in range(w_q.shape[0]):
            wq_full = lax.all_gather(w_q[layer_idx], 'tok', axis=0, tiled=True)
            wk_full = lax.all_gather(w_k[layer_idx], 'tok', axis=0, tiled=True)
            wv_full = lax.all_gather(w_v[layer_idx], 'tok', axis=0, tiled=True)
            wo_full = lax.all_gather(w_o[layer_idx], 'tok', axis=2, tiled=True)
            wg_full = lax.all_gather(w_gate[layer_idx], 'tok', axis=0, tiled=True)
            wu_full = lax.all_gather(w_up[layer_idx], 'tok', axis=0, tiled=True)
            wd_full = lax.all_gather(w_down[layer_idx], 'tok', axis=1, tiled=True)
            embed_dim = wo_full.shape[2]

            hidden = rms_norm(residual, g_attn[layer_idx])
            h_blk = lax.all_gather(hidden, 'mp', axis=1, tiled=True)
            q_lin = jnp.einsum('mse,end->msnd', h_blk, wq_full, preferred_element_type=jnp.float32)
            k_lin = jnp.einsum('mse,end->msnd', h_blk, wk_full, preferred_element_type=jnp.float32)
            v_val = jnp.einsum('mse,end->msnd', h_blk, wv_full, preferred_element_type=jnp.float32).astype(jnp.bfloat16)
            q_rot = apply_rope(q_lin, cos_t, sin_t).astype(jnp.bfloat16).reshape(micro_n, blk_len, kv_heads, groups, head_dim)
            k_rot = apply_rope(k_lin, cos_t, sin_t).astype(jnp.bfloat16)
            attn_out = attend(q_rot, k_rot, v_val, allowed)
            part_sum = jnp.einsum('mnsgd,ngde->mse', attn_out, wo_full.reshape(kv_heads, groups, head_dim, embed_dim), preferred_element_type=jnp.float32)
            residual = residual + lax.psum_scatter(part_sum, 'mp', scatter_dimension=1, tiled=True)

            hidden = rms_norm(residual, g_mlp[layer_idx])
            h_blk = lax.all_gather(hidden, 'mp', axis=1, tiled=True)
            gate_val = jnp.einsum('mse,ef->msf', h_blk, wg_full, preferred_element_type=jnp.float32)
            up_val = jnp.einsum('mse,ef->msf', h_blk, wu_full, preferred_element_type=jnp.float32)
            act_val = (jax.nn.silu(gate_val) * up_val).astype(jnp.bfloat16)
            part_sum = jnp.einsum('msf,fe->mse', act_val, wd_full, preferred_element_type=jnp.float32)
            residual = residual + lax.psum_scatter(part_sum, 'mp', scatter_dimension=1, tiled=True)
        return residual

    return jax.shard_map(
        device_fn,
        mesh=mesh,
        in_specs=(act_spec, seg_spec, gain_spec, head_in, head_in, head_in, head_out, gain_spec, ffn_in, ffn_in, ffn_out),
        out_specs=act_spec,
        check_vma=False,
    )
```

profile of v0, /device:TPU:0, one launch (start us, length us, event | category | flops | bytes accessed | tf_op | source)
XLA Modules:
  0.0 4906.6 jit_solution(12230433814980883262)
XLA Ops:
  6.5 4.5 fusion.96
  15.7 4.6 fusion.26
  20.3 8.9 fusion.28
  29.3 5.1 slice_bitcast_fusion
  34.4 6.5 fusion.94
  41.0 6.4 copy.76
  47.4 6.9 fusion.95
  54.8 5.9 all_gather.57
  64.5 3.7 multiply_cosine_fusion
  68.2 173.0 %all-gather.33.cloned.1.call-done = bf16[2,1024,3584]{2,1,0:T(8,128)(2,1)} async-done(((bf16[2,512,3584]{2,1,0:T(8,128)(2,1)}), bf16[2,1024,3584]{2,1,0:T(8,128)(2,1)}) %all-gather.33.cloned.1.call-update) | async-done | bytes 14680080 | tf_op jit(solution)/shard_map/all_gather | solution.py:77
  241.2 21.3 fusion.44
  265.5 27.0 all-gather.45.cloned.1.call-done
  292.5 21.0 fusion.140
  313.5 72.4 %all-gather.41.cloned.1.call-done = bf16[1,3584,8,256]{1,3,2,0:T(8,128)(2,1)} async-done(((bf16[1,896,8,256]{1,3,2,0:T(8,128)(2,1)}), bf16[1,3584,8,256]{1,3,2,0:T(8,128)(2,1)}) %all-gather.41.cloned.1.call-update) | async-done | bytes 14680080 | tf_op jit(solution)/shard_map/all_gather | solution.py:67
  385.9 38.8 fusion.46
  424.7 9.4 subtract_convert_fusion.1
  434.0 6.4 copy.35
  440.5 6.2 copy.36
  446.6 26.9 fusion.55
  473.5 67.1 %fusion.97 = (f32[2,4,1024,2]{2,3,1,0:T(2,128)S(1)}, f32[2,4,1024,2,1024]{2,4,3,1,0:T(8,128)}) fusion(f32[2,4,1024,2,1024]{2,4,3,1,0:T(8,128)} %fusion.55, pred[2,1024,1024]{1,2,0:T(8,128)(4,1)} %compare_and_fusion), kind=kOutput, calls=%fused_computation.140 | output fusion | flops 100664320 | bytes 136380416 | tf_op jit(solution)/shard_map/sub | solution.py:40
  540.6 28.5 fusion.18
  569.1 43.4 fusion.49
  612.7 19.3 fusion.92
  632.7 301.6 %reduce-scatter.5.cloned.1.call-done = f32[2,512,3584]{2,1,0:T(8,128)} async-done(((f32[2,1024,3584]{2,1,0:T(8,128)}), f32[2,512,3584]{2,1,0:T(8,128)}) %reduce-scatter.5.cloned.1.call-update) | async-done | bytes 14680080 | tf_op jit(solution)/shard_map/reduce_scatter | solution.py:85
  934.3 9.2 multiply_reduce_fusion.2
  943.6 10.7 multiply_convert_fusion.6
  954.3 19.3 fusion.91
  973.7 17.5 fusion.93
  991.3 247.2 %all-gather.51.cloned.1.call-done = bf16[1,3584,7168]{2,1,0:T(8,128)(2,1)} async-done(((bf16[1,896,7168]{2,1,0:T(8,128)(2,1)}), bf16[1,3584,7168]{2,1,0:T(8,128)(2,1)}) %all-gather.51.cloned.1.call-update) | async-done | bytes 51380240 | tf_op jit(solution)/shard_map/all_gather | solution.py:72
  1238.5 174.5 %all-gather.35.cloned.1.call-done = bf16[2,1024,3584]{2,1,0:T(8,128)(2,1)} async-done(((bf16[2,512,3584]{2,1,0:T(8,128)(2,1)}), bf16[2,1024,3584]{2,1,0:T(8,128)(2,1)}) %all-gather.35.cloned.1.call-update) | async-done | bytes 14680080 | tf_op jit(solution)/shard_map/all_gather | solution.py:88
  1412.9 117.5 %fusion.10 = f32[2,1024,7168]{2,1,0:T(8,128)} fusion(bf16[2,1024,3584]{2,1,0:T(8,128)(2,1)} %all-gather.35.cloned.1.call-done, bf16[1,3584,7168]{2,1,0:T(8,128)(2,1)} %all-gather.51.cloned.1.call-done), kind=kOutput, calls=%fused_computation.18 | convolution fusion | flops 105226698752 | bytes 124780544 | tf_op jit(solution)/shard_map/mse,ef->msf/dot_general | solution.py:90
  1530.4 186.7 %all-gather.49.cloned.1.call-done = bf16[1,3584,7168]{2,1,0:T(8,128)(2,1)} async-done(((bf16[1,896,7168]{2,1,0:T(8,128)(2,1)}), bf16[1,3584,7168]{2,1,0:T(8,128)(2,1)}) %all-gather.49.cloned.1.call-update) | async-done | bytes 51380240 | tf_op jit(solution)/shard_map/all_gather | solution.py:71
  1717.1 117.5 %fusion.12 = f32[2,1024,7168]{2,1,0:T(8,128)} fusion(bf16[2,1024,3584]{2,1,0:T(8,128)(2,1)} %all-gather.35.cloned.1.call-done, bf16[1,3584,7168]{2,1,0:T(8,128)(2,1)} %all-gather.49.cloned.1.call-done), kind=kOutput, calls=%fused_computation.20 | convolution fusion | flops 105226698752 | bytes 124780544 | tf_op jit(solution)/shard_map/mse,ef->msf/dot_general | solution.py:89
  1834.6 186.2 %all-gather.53.cloned.1.call-done = bf16[1,7168,3584]{2,1,0:T(8,128)(2,1)} async-done(((bf16[1,7168,896]{2,1,0:T(8,128)(2,1)}), bf16[1,7168,3584]{2,1,0:T(8,128)(2,1)}) %all-gather.53.cloned.1.call-update) | async-done | bytes 51380240 | tf_op jit(solution)/shard_map/all_gather | solution.py:73
  2020.8 127.0 %fusion.8 = f32[2,1024,3584]{2,1,0:T(8,128)} fusion(bf16[1,7168,3584]{2,1,0:T(8,128)(2,1)} %all-gather.53.cloned.1.call-done, f32[2,1024,7168]{2,1,0:T(8,128)} %fusion.10, f32[2,1024,7168]{2,1,0:T(8,128)} %fusion.12), kind=kOutput, calls=%fused_computation.16 | convolution fusion | flops 105314779136 | bytes 198180864 | tf_op jit(solution)/shard_map/msf,fe->mse/dot_general | solution.py:92
  2147.8 6.4 copy.79
  2154.3 315.2 %reduce-scatter.7.cloned.1.call-done = f32[2,512,3584]{2,1,0:T(8,128)} async-done(((f32[2,1024,3584]{2,1,0:T(8,128)}), f32[2,512,3584]{2,1,0:T(8,128)}) %reduce-scatter.7.cloned.1.call-update) | async-done | bytes 14680080 | tf_op jit(solution)/shard_map/reduce_scatter | solution.py:93
  2469.5 18.3 multiply_reduce_fusion.1
  2487.8 10.6 multiply_convert_fusion.5
  2502.9 60.1 %all-gather.55.cloned.1.call-done = bf16[1,3584,8,256]{1,3,2,0:T(8,128)(2,1)} async-done(((bf16[1,896,8,256]{1,3,2,0:T(8,128)(2,1)}), bf16[1,3584,8,256]{1,3,2,0:T(8,128)(2,1)}) %all-gather.55.cloned.1.call-update) | async-done | bytes 14680080 | tf_op jit(solution)/shard_map/all_gather | solution.py:67
  2562.9 174.5 %all-gather.37.cloned.1.call-done = bf16[2,1024,3584]{2,1,0:T(8,128)(2,1)} async-done(((bf16[2,512,3584]{2,1,0:T(8,128)(2,1)}), bf16[2,1024,3584]{2,1,0:T(8,128)(2,1)}) %all-gather.37.cloned.1.call-update) | async-done | bytes 14680080 | tf_op jit(solution)/shard_map/all_gather | solution.py:77
  2737.4 38.5 fusion.38
  2775.9 9.4 subtract_convert_fusion
  2785.3 6.2 copy.45
  2791.6 6.2 copy.46
  2797.8 21.3 fusion.36
  2822.0 17.4 all-gather.59.cloned.1.call-done
  2839.5 21.4 fusion.136
  2860.9 26.9 fusion.59
  2887.8 66.9 %fusion.98 = (f32[2,4,1024,2]{2,3,1,0:T(2,128)S(1)}, f32[2,4,1024,2,1024]{2,4,3,1,0:T(8,128)}) fusion(f32[2,4,1024,2,1024]{2,4,3,1,0:T(8,128)} %fusion.59, pred[2,1024,1024]{1,2,0:T(8,128)(4,1)} %compare_and_fusion), kind=kOutput, calls=%fused_computation.141 | output fusion | flops 100664320 | bytes 136380416 | tf_op jit(solution)/shard_map/sub | solution.py:40
  2954.8 28.5 fusion.16
  2983.3 43.4 fusion.52
  3027.3 321.1 %reduce-scatter.9.cloned.1.call-done = f32[2,512,3584]{2,1,0:T(8,128)} async-done(((f32[2,1024,3584]{2,1,0:T(8,128)}), f32[2,512,3584]{2,1,0:T(8,128)}) %reduce-scatter.9.cloned.1.call-update) | async-done | bytes 14680080 | tf_op jit(solution)/shard_map/reduce_scatter | solution.py:85
  3348.4 15.4 multiply_reduce_fusion
  3363.8 10.5 multiply_convert_fusion.4
  3375.7 276.7 %all-gather.63.cloned.1.call-done = bf16[1,3584,7168]{2,1,0:T(8,128)(2,1)} async-done(((bf16[1,896,7168]{2,1,0:T(8,128)(2,1)}), bf16[1,3584,7168]{2,1,0:T(8,128)(2,1)}) %all-gather.63.cloned.1.call-update) | async-done | bytes 51380240 | tf_op jit(solution)/shard_map/all_gather | solution.py:71
  3652.4 174.5 %all-gather.39.cloned.1.call-done = bf16[2,1024,3584]{2,1,0:T(8,128)(2,1)} async-done(((bf16[2,512,3584]{2,1,0:T(8,128)(2,1)}), bf16[2,1024,3584]{2,1,0:T(8,128)(2,1)}) %all-gather.39.cloned.1.call-update) | async-done | bytes 14680080 | tf_op jit(solution)/shard_map/all_gather | solution.py:88
  3826.9 117.4 %fusion.6 = f32[2,1024,7168]{2,1,0:T(8,128)} fusion(bf16[2,1024,3584]{2,1,0:T(8,128)(2,1)} %all-gather.39.cloned.1.call-done, bf16[1,3584,7168]{2,1,0:T(8,128)(2,1)} %all-gather.63.cloned.1.call-done), kind=kOutput, calls=%fused_computation.14 | convolution fusion | flops 105226698752 | bytes 124780544 | tf_op jit(solution)/shard_map/mse,ef->msf/dot_general | solution.py:89
  3944.3 186.6 %all-gather.65.cloned.1.call-done = bf16[1,3584,7168]{2,1,0:T(8,128)(2,1)} async-done(((bf16[1,896,7168]{2,1,0:T(8,128)(2,1)}), bf16[1,3584,7168]{2,1,0:T(8,128)(2,1)}) %all-gather.65.cloned.1.call-update) | async-done | bytes 51380240 | tf_op jit(solution)/shard_map/all_gather | solution.py:72
  4130.9 117.4 %fusion.4 = f32[2,1024,7168]{2,1,0:T(8,128)} fusion(bf16[2,1024,3584]{2,1,0:T(8,128)(2,1)} %all-gather.39.cloned.1.call-done, bf16[1,3584,7168]{2,1,0:T(8,128)(2,1)} %all-gather.65.cloned.1.call-done), kind=kOutput, calls=%fused_computation.12 | convolution fusion | flops 105226698752 | bytes 124780544 | tf_op jit(solution)/shard_map/mse,ef->msf/dot_general | solution.py:90
  4248.3 186.4 %all-gather.67.cloned.1.call-done = bf16[1,7168,3584]{2,1,0:T(8,128)(2,1)} async-done(((bf16[1,7168,896]{2,1,0:T(8,128)(2,1)}), bf16[1,7168,3584]{2,1,0:T(8,128)(2,1)}) %all-gather.67.cloned.1.call-update) | async-done | bytes 51380240 | tf_op jit(solution)/shard_map/all_gather | solution.py:73
  4434.7 127.1 %fusion.2 = f32[2,1024,3584]{2,1,0:T(8,128)} fusion(bf16[1,7168,3584]{2,1,0:T(8,128)(2,1)} %all-gather.67.cloned.1.call-done, f32[2,1024,7168]{2,1,0:T(8,128)} %fusion.4, f32[2,1024,7168]{2,1,0:T(8,128)} %fusion.6), kind=kOutput, calls=%fused_computation.10 | convolution fusion | flops 105314779136 | bytes 198180864 | tf_op jit(solution)/shard_map/msf,fe->mse/dot_general | solution.py:92
  4561.8 321.7 %reduce-scatter.11.cloned.1.call-done = f32[2,512,3584]{2,1,0:T(8,128)} async-done(((f32[2,1024,3584]{2,1,0:T(8,128)}), f32[2,512,3584]{2,1,0:T(8,128)}) %reduce-scatter.11.cloned.1.call-update) | async-done | bytes 14680080 | tf_op jit(solution)/shard_map/reduce_scatter | solution.py:93
  4883.5 15.8 add.85
  (91 shorter events, 22.4 us)
Async XLA Ops:
  6.5 61.7 %all-gather.43.cloned.1.call-start = ((), (), s32[]{:S(2)}) async-start(), calls=%async_computation.13 | async-start | bytes 9175040 | tf_op jit(solution)/shard_map/all_gather | solution.py:68
  14.2 227.1 %all-gather.33.cloned.1.call-start = ((), (), s32[]{:S(2)}) async-start(), calls=%async_computation.4 | async-start | bytes 22020096 | tf_op jit(solution)/shard_map/all_gather | solution.py:77
  29.2 263.3 %all-gather.45.cloned.1.call-start = ((), (), s32[]{:S(2)}) async-start(), calls=%async_computation.14 | async-start | bytes 9175040 | tf_op jit(solution)/shard_map/all_gather | solution.py:69
  34.4 351.5 %all-gather.41.cloned.1.call-start = ((), (), s32[]{:S(2)}) async-start(), calls=%async_computation.12 | async-start | bytes 18350080 | tf_op jit(solution)/shard_map/all_gather | solution.py:67
  41.0 13.8 copy-start.10
  47.4 521.8 %all-gather.47.cloned.1.call-start = ((), (), s32[]{:S(2)}) async-start(), calls=%async_computation.15 | async-start | bytes 18350080 | tf_op jit(solution)/shard_map/all_gather | solution.py:70
  54.4 879.9 %reduce-scatter.5.cloned.1.call-start = ((), (), s32[]{:S(2)}) async-start(), calls=%async_computation.5 | async-start | bytes 44040192 | tf_op jit(solution)/shard_map/reduce_scatter | solution.py:85
  68.2 356.5 %copy-start = (f32[2,1024,128]{1,2,0:T(8,128)}, f32[2,1024,128]{1,2,0:T(8,128)S(1)}, u32[]{:S(2)}) copy-start(f32[2,1024,128]{1,2,0:T(8,128)S(1)} %get-tuple-element.35) | copy-start | bytes 3145732
  68.2 356.5 %copy-start.2 = (f32[2,1024,128]{1,2,0:T(8,128)}, f32[2,1024,128]{1,2,0:T(8,128)S(1)}, u32[]{:S(2)}) copy-start(f32[2,1024,128]{1,2,0:T(8,128)S(1)} %get-tuple-element.36) | copy-start | bytes 3145732
  434.0 12.6 copy-start.4
  612.6 19.4 copy-start.9
  612.6 625.9 %all-gather.51.cloned.1.call-start = ((), (), s32[]{:S(2)}) async-start(), calls=%async_computation.17 | async-start | bytes 64225280 | tf_op jit(solution)/shard_map/all_gather | solution.py:72
  632.0 781.0 %all-gather.35.cloned.1.call-start = ((), (), s32[]{:S(2)}) async-start(), calls=%async_computation.6 | async-start | bytes 22020096 | tf_op jit(solution)/shard_map/all_gather | solution.py:88
  954.3 762.8 %all-gather.49.cloned.1.call-start = ((), (), s32[]{:S(2)}) async-start(), calls=%async_computation.16 | async-start | bytes 64225280 | tf_op jit(solution)/shard_map/all_gather | solution.py:71
  973.6 1047.1 %all-gather.53.cloned.1.call-start = ((), (), s32[]{:S(2)}) async-start(), calls=%async_computation.18 | async-start | bytes 64225280 | tf_op jit(solution)/shard_map/all_gather | solution.py:73
  991.2 1478.3 %reduce-scatter.7.cloned.1.call-start = ((), (), s32[]{:S(2)}) async-start(), calls=%async_computation.7 | async-start | bytes 44040192 | tf_op jit(solution)/shard_map/reduce_scatter | solution.py:93
  2147.8 415.1 %all-gather.55.cloned.1.call-start = ((), (), s32[]{:S(2)}) async-start(), calls=%async_computation.19 | async-start | bytes 18350080 | tf_op jit(solution)/shard_map/all_gather | solution.py:67
  2154.3 333.5 %copy-start.7 = (f32[3584]{0:T(1024)S(1)}, f32[3584]{0:T(1024)}, u32[]{:S(2)}) copy-start(f32[3584]{0:T(1024)} %get-tuple-element.7) | copy-start | bytes 43012
  2154.3 583.1 %all-gather.37.cloned.1.call-start = ((), (), s32[]{:S(2)}) async-start(), calls=%async_computation.8 | async-start | bytes 22020096 | tf_op jit(solution)/shard_map/all_gather | solution.py:77
  2487.8 10.6 copy-start.6
  2498.4 299.4 %all-gather.57.cloned.1.call-start = ((), (), s32[]{:S(2)}) async-start(), calls=%async_computation.20 | async-start | bytes 9175040 | tf_op jit(solution)/shard_map/all_gather | solution.py:68
  2501.6 337.9 %all-gather.59.cloned.1.call-start = ((), (), s32[]{:S(2)}) async-start(), calls=%async_computation.21 | async-start | bytes 9175040 | tf_op jit(solution)/shard_map/all_gather | solution.py:69
  2502.2 481.0 %all-gather.61.cloned.1.call-start = ((), (), s32[]{:S(2)}) async-start(), calls=%async_computation.22 | async-start | bytes 18350080 | tf_op jit(solution)/shard_map/all_gather | solution.py:70
  2502.8 273.1 %copy-start.1 = (f32[2,1024,128]{1,2,0:T(8,128)S(1)}, f32[2,1024,128]{1,2,0:T(8,128)}, u32[]{:S(2)}) copy-start(f32[2,1024,128]{1,2,0:T(8,128)} %copy-done) | copy-start | bytes 3145732
  2502.8 273.1 %copy-start.3 = (f32[2,1024,128]{1,2,0:T(8,128)S(1)}, f32[2,1024,128]{1,2,0:T(8,128)}, u32[]{:S(2)}) copy-start(f32[2,1024,128]{1,2,0:T(8,128)} %copy-done.2) | copy-start | bytes 3145732
  2502.8 845.6 %reduce-scatter.9.cloned.1.call-start = ((), (), s32[]{:S(2)}) async-start(), calls=%async_computation.9 | async-start | bytes 44040192 | tf_op jit(solution)/shard_map/reduce_scatter | solution.py:85
  2822.0 38.9 copy-start.5
  3026.7 625.7 %all-gather.63.cloned.1.call-start = ((), (), s32[]{:S(2)}) async-start(), calls=%async_computation.23 | async-start | bytes 64225280 | tf_op jit(solution)/shard_map/all_gather | solution.py:71
  3027.2 336.6 %copy-start.8 = (f32[3584]{0:T(1024)S(1)}, f32[3584]{0:T(1024)}, u32[]{:S(2)}) copy-start(f32[3584]{0:T(1024)} %get-tuple-element.5) | copy-start | bytes 43012
  3027.3 799.6 %all-gather.39.cloned.1.call-start = ((), (), s32[]{:S(2)}) async-start(), calls=%async_computation.10 | async-start | bytes 22020096 | tf_op jit(solution)/shard_map/all_gather | solution.py:88
  3374.3 756.6 %all-gather.65.cloned.1.call-start = ((), (), s32[]{:S(2)}) async-start(), calls=%async_computation.24 | async-start | bytes 64225280 | tf_op jit(solution)/shard_map/all_gather | solution.py:72
  3374.9 1059.8 %all-gather.67.cloned.1.call-start = ((), (), s32[]{:S(2)}) async-start(), calls=%async_computation.25 | async-start | bytes 64225280 | tf_op jit(solution)/shard_map/all_gather | solution.py:73
  3375.6 1507.9 %reduce-scatter.11.cloned.1.call-start = ((), (), s32[]{:S(2)}) async-start(), calls=%async_computation.11 | async-start | bytes 44040192 | tf_op jit(solution)/shard_map/reduce_scatter | solution.py:93
Sparse Core Ops, SparseCore 0:
  14.3 52.4 all-gather.42
  68.3 172.8 all-gather.32
  242.8 49.6 all-gather.44
  293.9 91.9 all-gather.40
  387.2 91.9 all-gather.46
  612.7 321.5 reduce-scatter.4
  935.9 302.5 all-gather.50
  1240.0 172.8 all-gather.34
  1414.5 302.5 all-gather.48
  1718.5 302.2 all-gather.52
  2147.9 321.5 reduce-scatter.6
  2470.9 91.9 all-gather.54
  2564.4 172.8 all-gather.36
  2738.8 49.6 all-gather.56
  2789.8 49.6 all-gather.58
  2840.9 91.9 all-gather.60
  3026.8 321.5 reduce-scatter.8
  3349.8 302.5 all-gather.62
  3653.9 172.8 all-gather.38
  3828.3 302.5 all-gather.64
  4132.4 302.2 all-gather.66
  4561.9 321.5 reduce-scatter.10
where the time goes:
time: 4910 us
  waiting for transfers between devices  3410 us (69%)
  matrix products  1080 us (22%)
  other arithmetic  272 us (6%)
  local copies, waits for them, and re-layouts  124 us (3%)
    reduce_scatter x4, waiting for transfers between devices, device_fn(): lax.psum_scatter(part_sum, 'mp', scatter_dimension=1, tiled=True)  1260 us
    all_gather x4, waiting for transfers between devices, device_fn(): h_blk = lax.all_gather(hidden, 'mp', axis=1, tiled=True)  696 us
    all_gather x2, waiting for transfers between devices, device_fn(): wg_full = lax.all_gather(w_gate[layer_idx], 'tok', axis=0, tiled=True)  463 us
    all_gather x2, waiting for transfers between devices, device_fn(): wu_full = lax.all_gather(w_up[layer_idx], 'tok', axis=0, tiled=True)  434 us
    all_gather x2, waiting for transfers between devices, device_fn(): wd_full = lax.all_gather(w_down[layer_idx], 'tok', axis=1, tiled=True)  373 us
    dot_general x2, matrix products, device_fn(): jnp.einsum('msf,fe->mse', act_val, wd_full, preferred_element_type=jnp.fl...  254 us
    dot_general x2, matrix products, device_fn(): jnp.einsum('mse,ef->msf', h_blk, wg_full, preferred_element_type=jnp.floa...  235 us
    dot_general x2, matrix products, device_fn(): jnp.einsum('mse,ef->msf', h_blk, wu_full, preferred_element_type=jnp.floa...  235 us
  transfers between devices with their start and end apart: 22, of which 18 were waited for; matrix products, arithmetic and copies ran while one was open for 23% of the time, Pallas kernels for 0%

commit v1 on v0

v1 whole, which is shorter than its diff:
```python
import functools

import jax
import jax.numpy as jnp
from jax import lax
from jax.experimental import pallas as pl
from jax.experimental.pallas import tpu as pltpu
from jax.sharding import PartitionSpec as P


NORM_EPS = 1e-5
ROPE_BASE = 10000.0
NEG_BIG = -1e30
F32 = jnp.float32
BF16 = jnp.bfloat16
VMEM_LIMIT = 60 * 1024 * 1024


def seg_positions(seg_rows):
    positions = jnp.arange(seg_rows.shape[-1], dtype=jnp.int32)
    previous = jnp.concatenate([seg_rows[..., :1] - 1, seg_rows[..., :-1]], axis=-1)
    start_at = jnp.where(seg_rows != previous, positions, 0)
    return positions - lax.cummax(start_at, axis=seg_rows.ndim - 1)


def piece_dot(h_ref, piece_refs, whole_ref):
    depth = piece_refs[0].shape[0]
    for j, w_ref in enumerate(piece_refs):
        whole_ref[j * depth:(j + 1) * depth, :] = w_ref[...]
    return jnp.dot(h_ref[...], whole_ref[...], preferred_element_type=F32)


def proj_kernel(rope_tiles, head_dim, h_ref, *refs):
    piece_refs, (cos_ref, sin_ref, out_ref, whole_ref) = refs[:4], refs[4:]
    acc = piece_dot(h_ref, piece_refs, whole_ref)
    half = head_dim // 2

    def roped():
        cos_t, sin_t = cos_ref[...], sin_ref[...]
        for n in range(acc.shape[1] // head_dim):
            lo = n * head_dim
            a, b = acc[:, lo:lo + half], acc[:, lo + half:lo + head_dim]
            out_ref[:, lo:lo + half] = (a * cos_t - b * sin_t).astype(BF16)
            out_ref[:, lo + half:lo + head_dim] = (b * cos_t + a * sin_t).astype(BF16)

    def plain():
        out_ref[...] = acc.astype(BF16)

    if rope_tiles >= 1000:
        roped()
    else:
        tile = pl.program_id(0)
        pl.when(tile < rope_tiles)(roped)
        pl.when(tile >= rope_tiles)(plain)


def project(hidden, pieces, cos_t, sin_t, rope_cols, head_dim, tile=512):
    rows, feat = hidden.shape
    depth, cols = pieces[0].shape
    rope_tiles = 1000 if rope_cols == cols else rope_cols // tile
    return pl.pallas_call(
        functools.partial(proj_kernel, rope_tiles, head_dim),
        grid=(cols // tile,),
        in_specs=[pl.BlockSpec((rows, feat), lambda i: (0, 0))]
        + [pl.BlockSpec((depth, tile), lambda i: (0, i))] * 4
        + [pl.BlockSpec(cos_t.shape, lambda i: (0, 0))] * 2,
        out_specs=pl.BlockSpec((rows, tile), lambda i: (0, i)),
        out_shape=jax.ShapeDtypeStruct((rows, cols), BF16),
        scratch_shapes=[pltpu.VMEM((feat, tile), BF16)],
        compiler_params=pltpu.CompilerParams(vmem_limit_bytes=VMEM_LIMIT),
        cost_estimate=pl.CostEstimate(flops=2 * rows * feat * cols, bytes_accessed=2 * (rows * feat + feat * cols + rows * cols), transcendentals=0),
    )(hidden, *pieces, cos_t, sin_t)


def ffn_kernel(h_ref, *refs):
    out_ref, whole_gate, whole_up = refs[-3:]
    gate = piece_dot(h_ref, refs[0:4], whole_gate)
    up = piece_dot(h_ref, refs[4:8], whole_up)
    out_ref[...] = (gate * jax.nn.sigmoid(gate) * up).astype(BF16)


def ffn_chunk(hidden, pieces, act_buf, total_cols, first_col, tile=256):
    rows, feat = hidden.shape
    depth, both = pieces[0].shape
    cols = both // 2
    steps, base = cols // tile, first_col // tile
    gate_spec = pl.BlockSpec((depth, tile), lambda i: (0, i))
    up_spec = pl.BlockSpec((depth, tile), lambda i: (0, steps + i))
    in_specs = [pl.BlockSpec((rows, feat), lambda i: (0, 0))] + [gate_spec] * 4 + [up_spec] * 4
    operands = [hidden, *pieces, *pieces]
    aliases = {}
    if act_buf is not None:
        in_specs.append(pl.BlockSpec(memory_space=pl.ANY))
        operands.append(act_buf)
        aliases = {9: 0}
    return pl.pallas_call(
        ffn_kernel,
        grid=(steps,),
        in_specs=in_specs,
        out_specs=pl.BlockSpec((rows, tile), lambda i: (0, base + i)),
        out_shape=jax.ShapeDtypeStruct((rows, total_cols), BF16),
        input_output_aliases=aliases,
        scratch_shapes=[pltpu.VMEM((feat, tile), BF16)] * 2,
        compiler_params=pltpu.CompilerParams(vmem_limit_bytes=VMEM_LIMIT),
        cost_estimate=pl.CostEstimate(flops=4 * rows * feat * cols, bytes_accessed=2 * (rows * feat + 2 * feat * cols + rows * cols), transcendentals=rows * cols),
    )(*operands)


def attn_kernel(head_dim, q_ref, ka_ref, va_ref, kb_ref, vb_ref, lo_ref, hi_ref, ia_ref, ib_ref, out_ref):
    lo, hi = lo_ref[0], hi_ref[0]
    ok_a = (ia_ref[...] >= lo) & (ia_ref[...] <= hi)
    ok_b = (ib_ref[...] >= lo) & (ib_ref[...] <= hi)
    dims = (((1,), (1,)), ((), ()))
    scale = head_dim ** -0.5
    for g in range(q_ref.shape[2] // head_dim):
        q = q_ref[0, :, g * head_dim:(g + 1) * head_dim]
        s_a = jnp.where(ok_a, lax.dot_general(q, ka_ref[0], dims, preferred_element_type=F32) * scale, NEG_BIG)
        s_b = jnp.where(ok_b, lax.dot_general(q, kb_ref[0], dims, preferred_element_type=F32) * scale, NEG_BIG)
        top = jnp.maximum(jnp.max(s_a, axis=1, keepdims=True), jnp.max(s_b, axis=1, keepdims=True))
        e_a, e_b = jnp.exp(s_a - top), jnp.exp(s_b - top)
        inv = 1.0 / (jnp.sum(e_a, axis=1, keepdims=True) + jnp.sum(e_b, axis=1, keepdims=True))
        out = jnp.dot((e_a * inv).astype(BF16), va_ref[0], preferred_element_type=F32)
        out = out + jnp.dot((e_b * inv).astype(BF16), vb_ref[0], preferred_element_type=F32)
        out_ref[0, :, g * head_dim:(g + 1) * head_dim] = out.astype(BF16)


def attention(q, kv_a, kv_b, lo, hi, idx_a, idx_b, head_dim):
    micro_n, rows, q_cols = q.shape
    kv_heads = kv_a.shape[2] // head_dim // 2
    group = q_cols // kv_heads
    k_spec = pl.BlockSpec((1, rows, head_dim), lambda m, n: (m, 0, n))
    v_spec = pl.BlockSpec((1, rows, head_dim), lambda m, n: (m, 0, kv_heads + n))
    q_spec = pl.BlockSpec((1, rows, group), lambda m, n: (m, 0, n))
    col_spec = pl.BlockSpec((1, rows, 1), lambda m, n: (m, 0, 0))
    row_spec = pl.BlockSpec((1, rows), lambda m, n: (0, 0))
    return pl.pallas_call(
        functools.partial(attn_kernel, head_dim),
        grid=(micro_n, kv_heads),
        in_specs=[q_spec, k_spec, v_spec, k_spec, v_spec, col_spec, col_spec, row_spec, row_spec],
        out_specs=q_spec,
        out_shape=jax.ShapeDtypeStruct(q.shape, BF16),
        compiler_params=pltpu.CompilerParams(vmem_limit_bytes=VMEM_LIMIT),
        cost_estimate=pl.CostEstimate(flops=16 * micro_n * rows * rows * q_cols, bytes_accessed=8 * micro_n * rows * q_cols, transcendentals=2 * micro_n * rows * rows * q_cols // head_dim),
    )(q, kv_a, kv_a, kv_b, kv_b, lo, hi, idx_a, idx_b)


def after(value, *earlier):
    return lax.optimization_barrier((value, *earlier))[0] if earlier else value


def norm_pieces(pieces, gains):
    feat = sum(p.shape[1] for p in pieces)
    total = sum(jnp.sum(p * p, axis=1, keepdims=True) for p in pieces)
    inv = lax.rsqrt(total / feat + NORM_EPS)
    return jnp.concatenate([(p * inv * g).astype(BF16) for p, g in zip(pieces, gains)], axis=1)


X_ORDER = (
    ('kv', 0, 0), ('q', 0, 0), ('o', 0, 0), ('g', 0, 0), ('g', 0, 1), ('g', 0, 2), ('g', 0, 3),
    ('d', 0, 0), ('d', 0, 1), ('kv', 1, 0), ('q', 1, 0), ('o', 1, 0), ('g', 1, 0), ('g', 1, 1), ('g', 1, 2), ('g', 1, 3),
    ('d', 1, 0), ('d', 1, 1),
)


FFN_CHUNKS = ((2048, 2048, 2048, 1024),) * 2
FAR_FROM = (1, 1)
DOWN_CHUNKS = ((512, 384), (512, 384))


def solution(mesh):
    act_spec = P(None, ('rep', 'tok', 'mp'), None)
    seg_spec = P(None, ('rep', 'tok', 'mp'))
    gain_spec = P(None, None)
    head_in = P(None, 'tok', 'mp', None)
    head_out = P(None, 'mp', None, 'tok')
    ffn_in = P(None, 'tok', 'mp')
    ffn_out = P(None, 'mp', 'tok')
    tok_n = mesh.shape['tok']
    over_x = [(i, i ^ 2) for i in range(tok_n)]
    over_core = [(i, i ^ 1) for i in range(tok_n)]

    def send_x(a):
        return lax.ppermute(a, 'tok', over_x)

    def send_core(a):
        return lax.ppermute(a, 'tok', over_core)

    def send_y(a):
        return lax.ppermute(a, 'mp', [(0, 1), (1, 0)])

    def first_part(own, order):
        k = len(order)
        order.append(k)
        return own, send_core(own), send_x(own), k

    def spread(parts, *earlier):
        own, near, cross, _ = parts
        cross = after(cross, *earlier)
        return own, near, cross, send_core(cross)

    def layer_pair(x_in, seg_ids, g_attn, w_q, w_k, w_v, w_o, g_mlp, w_gate, w_up, w_down):
        micro_n, part_len, feat = x_in.shape
        layers, depth = w_q.shape[0], w_q.shape[1]
        head_dim = w_q.shape[3]
        rows = micro_n * part_len
        ffn_cols = w_gate.shape[2]
        tok = lax.axis_index('tok')
        half_id = lax.axis_index('mp')

        def local_cols(a, axis):
            return [lax.dynamic_slice_in_dim(a, (tok ^ j) * depth, depth, axis) for j in range(4)]

        order = []
        firsts = [[sum(w[:c]) for c in range(len(w))] for w in FFN_CHUNKS]

        def own_piece(kind, l, c):
            if kind == 'kv':
                return jnp.concatenate([w_k[l].reshape(depth, -1), w_v[l].reshape(depth, -1)], axis=1)
            if kind == 'q':
                return w_q[l].reshape(depth, -1)
            if kind == 'o':
                return w_o[l].reshape(-1, depth)
            if kind == 'g':
                at = slice(firsts[l][c], firsts[l][c] + FFN_CHUNKS[l][c])
                return jnp.concatenate([w_gate[l, :, at], w_up[l, :, at]], axis=1)
            at = sum(DOWN_CHUNKS[l][:c])
            return w_down[l, :, at:at + DOWN_CHUNKS[l][c]]

        parts = {key: first_part(own_piece(*key), order) for key in X_ORDER}
        plans = [
            (
                parts['kv', l, 0], parts['q', l, 0], parts['o', l, 0],
                [parts['g', l, c] for c in range(len(FFN_CHUNKS[l]))],
                [parts['d', l, c] for c in range(len(DOWN_CHUNKS[l]))],
            )
            for l in range(layers)
        ]

        x_own = jnp.concatenate(local_cols(x_in.reshape(rows, feat), 1), axis=1)
        seg_far = send_y(seg_ids)
        x_far = send_y(after(x_own, seg_far))
        first_half = jnp.where(half_id == 0, seg_ids, seg_far)
        second_half = jnp.where(half_id == 0, seg_far, seg_ids)
        positions = seg_positions(jnp.concatenate([first_half, second_half], axis=1))
        idx = jnp.arange(part_len, dtype=jnp.int32)
        at_own = half_id * part_len
        at_far = (1 - half_id) * part_len
        inv_freq = ROPE_BASE ** (-2.0 * jnp.arange(head_dim // 2, dtype=F32) / head_dim)

        def tables(at):
            pos = lax.dynamic_slice_in_dim(positions, at, part_len, 1)
            hi = jnp.broadcast_to((idx + at)[None, :], pos.shape)
            angles = (pos.astype(F32)[..., None] * inv_freq).reshape(rows, -1)
            return jnp.cos(angles), jnp.sin(angles), (hi - pos)[..., None], hi[..., None], (idx + at)[None, :]

        cos_own, sin_own, lo_own, hi_own, idx_own = tables(at_own)
        cos_far, sin_far, lo_far, hi_far, idx_far = tables(at_far)

        resid = [x_own[:, j * depth:(j + 1) * depth].astype(F32) for j in range(4)]
        shape3 = (micro_n, part_len, -1)
        k_cols = plans[0][0][0].shape[1] // 2
        q_cols = plans[0][1][0].shape[1]
        gate_q = ()
        out = jnp.zeros((rows, feat), F32)
        y_next = send_y(after(plans[0][2][0], x_far))
        for l in range(layers):
            kv_w, q_w, o_w, gu_w, d_w = plans[l]
            gains = [g.astype(F32)[None, :] for g in local_cols(g_attn[l], 0)]
            h_own = norm_pieces(resid, gains)
            if l == 0:
                h_far = norm_pieces([x_far[:, j * depth:(j + 1) * depth].astype(F32) for j in range(4)], gains)
            else:
                h_far = send_y(h_own)
            kv_w = spread(kv_w, *gate_q)
            q_w = spread(q_w, *gate_q)
            y_own = y_next
            kv_own = project(h_own, kv_w, cos_own, sin_own, k_cols, head_dim)
            q_own = project(h_own, q_w, cos_own, sin_own, q_cols, head_dim)
            o_w = spread(o_w, q_own)
            kv_far = project(h_far, kv_w, cos_far, sin_far, k_cols, head_dim)
            y_cross = send_y(after(o_w[2], (kv_far, h_far)[l]))
            q_far = project(h_far, q_w, cos_far, sin_far, q_cols, head_dim)
            o_y = (y_own, send_core(y_own), y_cross, send_core(y_cross))
            kv_own, q_own, kv_far, q_far = (a.reshape(shape3) for a in (kv_own, q_own, kv_far, q_far))
            o_far = attention(q_far, kv_own, kv_far, lo_far, hi_far, idx_own, idx_far, head_dim)
            o_got = send_y(o_far).reshape(rows, -1)
            o_own = attention(q_own, kv_own, kv_far, lo_own, hi_own, idx_own, idx_far, head_dim).reshape(rows, -1)
            base = [resid[j] + jnp.dot(o_own, o_w[j], preferred_element_type=F32) for j in range(4)]
            base = lax.optimization_barrier(base)
            resid = [base[j] + jnp.dot(o_got, o_y[j], preferred_element_type=F32) for j in range(4)]

            gains = [g.astype(F32)[None, :] for g in local_cols(g_mlp[l], 0)]
            h_own = norm_pieces(resid, gains)
            h_far = send_y(h_own)
            if l + 1 < layers:
                y_next = send_y(after(plans[l + 1][2][0], h_far))
            act_own = act_far = None
            starts = firsts[l]
            last_c = len(gu_w) - 1
            gate = (o_own, h_own)[l]
            pieces = []

            def far_chunk(c, gate, act_far):
                return ffn_chunk(after(h_far, gate), pieces[c], act_far, ffn_cols, starts[c])

            done_far = 0
            for c in range(len(gu_w)):
                pieces.append(spread(gu_w[c], gate))
                if c == last_c:
                    while done_far <= c:
                        gate = act_far = far_chunk(done_far, gate, act_far)
                        done_far += 1
                act_own = ffn_chunk(h_own, pieces[c], act_own, ffn_cols, starts[c])
                gate = act_own
                while FAR_FROM[l] <= c < last_c and done_far <= c:
                    gate = act_far = far_chunk(done_far, gate, act_far)
                    done_far += 1
            sums = []
            gate_d = ()
            for js in ((0, 1), (2, 3)):
                for c, parts_c in enumerate(d_w):
                    w4 = parts_c if js == (0, 1) else spread(parts_c, *gate_d)
                    at = sum(DOWN_CHUNKS[l][:c])
                    fars = []
                    for j in js:
                        far_sum = jnp.dot(act_far, w4[j], preferred_element_type=F32)
                        fars.append(far_sum)
                        got = send_y(far_sum)
                        mine = lax.optimization_barrier(jnp.dot(act_own, w4[j], preferred_element_type=F32))
                        sums.append((j, at, mine, got))
                    gate_d = (mine,) if js == (0, 1) else tuple(fars)
            gate_q = (sums[-1][2],)
            new_resid = [[] for _ in range(4)]
            for j, at, mine, got in sums:
                total = resid[j][:, at:at + mine.shape[1]] + mine + after(got, *gate_q)
                new_resid[j].append(total)
                if l + 1 == layers:
                    out = lax.dynamic_update_slice_in_dim(out, total, (tok ^ j) * depth + at, 1)
            resid = [jnp.concatenate(new_resid[j], axis=1) for j in range(4)]
        return out.reshape(micro_n, part_len, feat)

    return jax.shard_map(
        layer_pair,
        mesh=mesh,
        in_specs=(act_spec, seg_spec, gain_spec, head_in, head_in, head_in, head_out, gain_spec, ffn_in, ffn_in, ffn_out),
        out_specs=act_spec,
        check_vma=False,
    )
```

time: 4910 us -> 3120 us (0.64)
  waiting for transfers between devices: 3410 us -> 1480 us
  Pallas kernels: 0 us -> 816 us
  matrix products: 1080 us -> 522 us
  other arithmetic: 272 us -> 114 us
  starting transfers between devices: 0.86 us -> 63.7 us
    all_gather x18 -> x0, waiting for transfers between devices: 2140 us -> none  [the longest x4 696 us: device_fn(): h_blk = lax.all_gather(hidden, 'mp', axis=1, tiled=True)]
    ppermute x0 -> x85, waiting for transfers between devices: none -> 1480 us  [the longest x27 843 us: send_y(): return lax.ppermute(a, 'mp', [(0, 1), (1, 0)])]
    reduce_scatter x4 -> x0, waiting for transfers between devices: 1260 us -> none  [device_fn(): lax.psum_scatter(part_sum, 'mp', scatter_dimension=1, tiled=True)]
    pallas_call x0 -> x28, Pallas kernels: none -> 816 us  [the longest x16 541 us: ffn_chunk(): pl.pallas_call(ffn_kernel, grid=(steps,), in_specs=in_specs, out_specs=pl...]
    dot_general x18 -> x48, matrix products: 1080 us -> 522 us  [the longest x16 215 us: layer_pair(): far_sum = jnp.dot(act_far, w4[j], preferred_element_type=F32)]
    sub x2 -> x1, other arithmetic: 134 us -> 0.01 us  [seg_positions(): return positions - lax.cummax(start_at, axis=seg_rows.ndim - 1)]
    ppermute x0 -> x85, starting transfers between devices: none -> 63.7 us  [the longest x27 31.1 us: send_y(): return lax.ppermute(a, 'mp', [(0, 1), (1, 0)])]
    concatenate x0 -> x14, other arithmetic: none -> 63.6 us  [the longest x8 43.6 us: own_piece(): return jnp.concatenate([w_gate[l, :, at], w_up[l, :, at]], axis=1)]
  transfers between devices with their start and end apart: 22 -> 85, of which waited for: 18 -> 29; matrix products, arithmetic and copies ran while one was open for 23% -> 23% of each run, Pallas kernels for 0% -> 26%
where the time goes in v1:
time: 3120 us
  waiting for transfers between devices  1480 us (47%)
  Pallas kernels  816 us (26%)
  matrix products  522 us (17%)
  local copies, waits for them, and re-layouts  119 us (4%)
  other arithmetic  114 us (4%)
  starting transfers between devices  63.7 us (2%)
    ppermute x27, waiting for transfers between devices, send_y(): return lax.ppermute(a, 'mp', [(0, 1), (1, 0)])  843 us
    ppermute x18, waiting for transfers between devices, send_x(): return lax.ppermute(a, 'tok', over_x)  616 us
    pallas_call x16, Pallas kernels, ffn_chunk(): pl.pallas_call(ffn_kernel, grid=(steps,), in_specs=in_specs, out_specs=pl...  541 us
    dot_general x16, matrix products, layer_pair(): far_sum = jnp.dot(act_far, w4[j], preferred_element_type=F32)  215 us
    dot_general x16, matrix products, layer_pair(): jnp.dot(act_own, w4[j], preferred_element_type=F32)  184 us
    pallas_call x8, Pallas kernels, project(): pl.pallas_call(functools.partial(proj_kernel, rope_tiles, head_dim), grid...  178 us
    pallas_call x4, Pallas kernels, attention(): pl.pallas_call(functools.partial(attn_kernel, head_dim), grid=(micro_n, k...  97.3 us
    dot_general x8, matrix products, layer_pair(): jnp.dot(o_own, o_w[j], preferred_element_type=F32)  63.1 us
  transfers between devices with their start and end apart: 85, of which 29 were waited for; matrix products, arithmetic and copies ran while one was open for 23% of the time, Pallas kernels for 26%

profile of v1, /device:TPU:0, one launch (start us, length us, event | category | flops | bytes accessed | tf_op | source)
XLA Modules:
  0.0 3117.3 jit_solution(1171233879904695656)
XLA Ops:
  33.9 29.8 slice_bitcast_fusion.4
  83.4 89.8 %collective-permute-done.1.refs_2_ = bf16[896,2048]{1,0:T(8,128)(2,1)} collective-permute-done((bf16[896,2048]{1,0:T(8,128)(2,1)}, bf16[896,2048]{1,0:T(8,128)(2,1)}, u32[]{:S(2)}, u32[]{:S(2)}) %collective-permute-start.1) | collective-permute-done | bytes 3670048 | tf_op jit(solution)/shard_map/ppermute | solution.py:183
  210.0 21.7 shard_map.109
  231.7 31.5 %collective-permute-done.9 = bf16[2048,896]{1,0:T(8,128)(2,1)} collective-permute-done((bf16[2048,896]{1,0:T(8,128)(2,1)}, bf16[2048,896]{1,0:T(8,128)(2,1)}, u32[]{:S(2)}, u32[]{:S(2)}) %collective-permute-start.9) | collective-permute-done | bytes 3670048 | tf_op jit(solution)/shard_map/ppermute | solution.py:183
  265.1 22.9 shard_map.111
  288.3 22.6 shard_map.110
  310.9 21.8 shard_map.113
  333.7 24.1 shard_map.112
  358.7 24.5 shard_map.114
  383.2 36.9 %collective-permute-done.24.refs_2_.refs_6_ = bf16[896,4096]{1,0:T(8,128)(2,1)} collective-permute-done((bf16[896,4096]{1,0:T(8,128)(2,1)}, bf16[896,4096]{1,0:T(8,128)(2,1)}, u32[]{:S(2)}, u32[]{:S(2)}) %collective-permute-start.24) | collective-permute-done | bytes 7340064 | tf_op jit(solution)/shard_map/ppermute | solution.py:183
  455.3 58.6 %collective-permute-done.11 = bf16[2,512,2048]{2,1,0:T(8,128)(2,1)S(1)} collective-permute-done((bf16[2,512,2048]{2,1,0:T(8,128)(2,1)}, bf16[2,512,2048]{2,1,0:T(8,128)(2,1)S(1)}, u32[]{:S(2)}, u32[]{:S(2)}) %collective-permute-start.11) | collective-permute-done | bytes 4194336 | tf_op jit(solution)/shard_map/ppermute | solution.py:189
  549.1 37.9 %shard_map.115.refs_8_ = bf16[1024,7168]{1,0:T(8,128)(2,1)} custom-call(bf16[1024,3584]{1,0:T(8,128)(2,1)} %pad_maximum_fusion.3.h_ref, bf16[896,4096]{1,0:T(8,128)(2,1)} %pad_maximum_fusion.6.refs_0_.refs_4_, bf16[896,4096]{1,0:T(8,128)(2,1)} %collective-permute-done.23.refs_1_.refs_5_, bf16[896,4096]{1,0:T(8,128)(2,1)} %collective-permute-done.24.refs_2_.refs_6_, ...), custom_call_target="tpu_custom_call" | custom-call | flops 30064771072 | bytes 40894464 | tf_op jit(solution)/shard_map/pallas_call | solution.py:96
  587.0 86.7 %collective-permute-done.22.refs_2_.refs_6_ = bf16[896,4096]{1,0:T(8,128)(2,1)} collective-permute-done((bf16[896,4096]{1,0:T(8,128)(2,1)}, bf16[896,4096]{1,0:T(8,128)(2,1)}, u32[]{:S(2)}, u32[]{:S(2)}) %collective-permute-start.22) | collective-permute-done | bytes 7340064 | tf_op jit(solution)/shard_map/ppermute | solution.py:183
  685.7 38.1 %shard_map.116.refs_8_ = bf16[1024,7168]{1,0:T(8,128)(2,1)} custom-call(bf16[1024,3584]{1,0:T(8,128)(2,1)} %pad_maximum_fusion.3.h_ref, bf16[896,4096]{1,0:T(8,128)(2,1)} %pad_maximum_fusion.5.refs_0_.refs_4_, bf16[896,4096]{1,0:T(8,128)(2,1)} %collective-permute-done.21.refs_1_.refs_5_, ...), custom_call_target="tpu_custom_call", output_to_operand_aliasing={{}: (9, {})} | custom-call | flops 30064771072 | bytes 40894464 | tf_op jit(solution)/shard_map/pallas_call | solution.py:96
  723.9 110.6 %collective-permute-done.18.h_ref = bf16[1024,3584]{1,0:T(8,128)(2,1)} collective-permute-done((bf16[1024,3584]{1,0:T(8,128)(2,1)}, bf16[1024,3584]{1,0:T(8,128)(2,1)}, u32[]{:S(2)}, u32[]{:S(2)}) %collective-permute-start.18) | collective-permute-done | bytes 7340064 | tf_op jit(solution)/shard_map/ppermute | solution.py:189
  834.4 37.7 %shard_map.117.refs_8_ = bf16[1024,7168]{1,0:T(8,128)(2,1)} custom-call(bf16[1024,3584]{1,0:T(8,128)(2,1)} %collective-permute-done.18.h_ref, bf16[896,4096]{1,0:T(8,128)(2,1)} %pad_maximum_fusion.6.refs_0_.refs_4_, bf16[896,4096]{1,0:T(8,128)(2,1)} %collective-permute-done.23.refs_1_.refs_5_, bf16[896,4096]{1,0:T(8,128)(2,1)} %collective-permute-done.24.refs_2_.refs_6_, ...), custom_call_target="tpu_custom_call" | custom-call | flops 30064771072 | bytes 40894464 | tf_op jit(solution)/shard_map/pallas_call | solution.py:96
  872.1 37.7 %shard_map.118.refs_8_ = bf16[1024,7168]{1,0:T(8,128)(2,1)} custom-call(bf16[1024,3584]{1,0:T(8,128)(2,1)} %collective-permute-done.18.h_ref, bf16[896,4096]{1,0:T(8,128)(2,1)} %pad_maximum_fusion.5.refs_0_.refs_4_, bf16[896,4096]{1,0:T(8,128)(2,1)} %collective-permute-done.21.refs_1_.refs_5_, ...), custom_call_target="tpu_custom_call", output_to_operand_aliasing={{}: (9, {})} | custom-call | flops 30064771072 | bytes 40894464 | tf_op jit(solution)/shard_map/pallas_call | solution.py:96
  940.4 37.8 %shard_map.119.refs_8_ = bf16[1024,7168]{1,0:T(8,128)(2,1)} custom-call(bf16[1024,3584]{1,0:T(8,128)(2,1)} %pad_maximum_fusion.3.h_ref, bf16[896,4096]{1,0:T(8,128)(2,1)} %pad_maximum_fusion.4.refs_0_.refs_4_, bf16[896,4096]{1,0:T(8,128)(2,1)} %collective-permute-done.19.refs_1_.refs_5_, ...), custom_call_target="tpu_custom_call", output_to_operand_aliasing={{}: (9, {})} | custom-call | flops 30064771072 | bytes 40894464 | tf_op jit(solution)/shard_map/pallas_call | solution.py:96
  978.2 37.9 %shard_map.120.refs_8_ = bf16[1024,7168]{1,0:T(8,128)(2,1)} custom-call(bf16[1024,3584]{1,0:T(8,128)(2,1)} %collective-permute-done.18.h_ref, bf16[896,4096]{1,0:T(8,128)(2,1)} %pad_maximum_fusion.4.refs_0_.refs_4_, bf16[896,4096]{1,0:T(8,128)(2,1)} %collective-permute-done.19.refs_1_.refs_5_, ...), custom_call_target="tpu_custom_call", output_to_operand_aliasing={{}: (9, {})} | custom-call | flops 30064771072 | bytes 40894464 | tf_op jit(solution)/shard_map/pallas_call | solution.py:96
  1030.6 21.7 shard_map.121
  1052.3 13.5 fusion.99
  1065.7 92.0 %collective-permute-done.31 = bf16[7168,512]{1,0:T(8,128)(2,1)} collective-permute-done((bf16[7168,512]{1,0:T(8,128)(2,1)}, bf16[7168,512]{1,0:T(8,128)(2,1)}, u32[]{:S(2)}, u32[]{:S(2)}) %collective-permute-start.31) | collective-permute-done | bytes 7340064 | tf_op jit(solution)/shard_map/ppermute | solution.py:183
  1157.7 21.7 shard_map.122
  1179.4 14.4 fusion.106
  1205.0 14.2 fusion.104
  1242.8 14.1 fusion.89
  1267.8 14.1 fusion.101
  1296.4 13.5 fusion.85
  1333.2 35.0 %collective-permute-done.38 = f32[1024,384]{1,0:T(8,128)} collective-permute-done((f32[1024,384]{1,0:T(8,128)S(1)}, f32[1024,384]{1,0:T(8,128)}, u32[]{:S(2)}, u32[]{:S(2)}) %collective-permute-start.38) | collective-permute-done | bytes 1572896 | tf_op jit(solution)/shard_map/ppermute | solution.py:189
  1394.3 18.8 collective-permute-done.29
  1414.7 32.0 %collective-permute-done.35 = f32[1024,384]{1,0:T(8,128)S(1)} collective-permute-done((f32[1024,384]{1,0:T(8,128)}, f32[1024,384]{1,0:T(8,128)S(1)}, u32[]{:S(2)}, u32[]{:S(2)}) %collective-permute-start.35) | collective-permute-done | bytes 1572896 | tf_op jit(solution)/shard_map/ppermute | solution.py:189
  1448.5 76.6 %collective-permute-done.40 = f32[1024,384]{1,0:T(8,128)} collective-permute-done((f32[1024,384]{1,0:T(8,128)S(1)}, f32[1024,384]{1,0:T(8,128)}, u32[]{:S(2)}, u32[]{:S(2)}) %collective-permute-start.40) | collective-permute-done | bytes 1572896 | tf_op jit(solution)/shard_map/ppermute | solution.py:189
  1527.2 13.6 fusion.110
  1558.4 18.6 collective-permute-done.42
  1595.4 21.9 shard_map.123
  1617.3 50.2 %collective-permute-done.51 = bf16[2048,896]{1,0:T(8,128)(2,1)} collective-permute-done((bf16[2048,896]{1,0:T(8,128)(2,1)}, bf16[2048,896]{1,0:T(8,128)(2,1)}, u32[]{:S(2)}, u32[]{:S(2)}) %collective-permute-start.51) | collective-permute-done | bytes 3670048 | tf_op jit(solution)/shard_map/ppermute | solution.py:183
  1667.8 22.6 shard_map.124
  1690.4 54.4 %collective-permute-done.49.h_ref = bf16[1024,3584]{1,0:T(8,128)(2,1)} collective-permute-done((bf16[1024,3584]{1,0:T(8,128)(2,1)}, bf16[1024,3584]{1,0:T(8,128)(2,1)}, u32[]{:S(2)}, u32[]{:S(2)}) %collective-permute-start.49) | collective-permute-done | bytes 7340064 | tf_op jit(solution)/shard_map/ppermute | solution.py:189
  1744.8 21.8 shard_map.127
  1766.6 22.6 shard_map.125
  1789.2 24.2 shard_map.128
  1815.4 24.5 shard_map.126
  1864.7 125.1 %collective-permute-done.56 = bf16[2048,896]{1,0:T(8,128)(2,1)} collective-permute-done((bf16[2048,896]{1,0:T(8,128)(2,1)}, bf16[2048,896]{1,0:T(8,128)(2,1)}, u32[]{:S(2)}, u32[]{:S(2)}) %collective-permute-start.56) | collective-permute-done | bytes 3670048 | tf_op jit(solution)/shard_map/ppermute | solution.py:189
  2049.0 37.8 %shard_map.129.refs_8_ = bf16[1024,7168]{1,0:T(8,128)(2,1)} custom-call(bf16[1024,3584]{1,0:T(8,128)(2,1)} %pad_maximum_fusion.8.h_ref, bf16[896,4096]{1,0:T(8,128)(2,1)} %pad_maximum_fusion.11.refs_0_.refs_4_, bf16[896,4096]{1,0:T(8,128)(2,1)} %collective-permute-done.65.refs_1_.refs_5_, bf16[896,4096]{1,0:T(8,128)(2,1)} %collective-permute-done.66.refs_2_.refs_6_, ...), custom_call_target="tpu_custom_call" | custom-call | flops 30064771072 | bytes 40894464 | tf_op jit(solution)/shard_map/pallas_call | solution.py:96
  2086.8 116.9 %collective-permute-done.64.refs_2_.refs_6_ = bf16[896,4096]{1,0:T(8,128)(2,1)} collective-permute-done((bf16[896,4096]{1,0:T(8,128)(2,1)}, bf16[896,4096]{1,0:T(8,128)(2,1)}, u32[]{:S(2)}, u32[]{:S(2)}) %collective-permute-start.64) | collective-permute-done | bytes 7340064 | tf_op jit(solution)/shard_map/ppermute | solution.py:183
  2215.7 37.8 %shard_map.130.refs_8_ = bf16[1024,7168]{1,0:T(8,128)(2,1)} custom-call(bf16[1024,3584]{1,0:T(8,128)(2,1)} %pad_maximum_fusion.8.h_ref, bf16[896,4096]{1,0:T(8,128)(2,1)} %pad_maximum_fusion.10.refs_0_.refs_4_, bf16[896,4096]{1,0:T(8,128)(2,1)} %collective-permute-done.63.refs_1_.refs_5_, ...), custom_call_target="tpu_custom_call", output_to_operand_aliasing={{}: (9, {})} | custom-call | flops 30064771072 | bytes 40894464 | tf_op jit(solution)/shard_map/pallas_call | solution.py:96
  2253.4 111.0 %collective-permute-done.60.h_ref = bf16[1024,3584]{1,0:T(8,128)(2,1)} collective-permute-done((bf16[1024,3584]{1,0:T(8,128)(2,1)}, bf16[1024,3584]{1,0:T(8,128)(2,1)}, u32[]{:S(2)}, u32[]{:S(2)}) %collective-permute-start.60) | collective-permute-done | bytes 7340064 | tf_op jit(solution)/shard_map/ppermute | solution.py:189
  2364.4 37.7 %shard_map.131.refs_8_ = bf16[1024,7168]{1,0:T(8,128)(2,1)} custom-call(bf16[1024,3584]{1,0:T(8,128)(2,1)} %collective-permute-done.60.h_ref, bf16[896,4096]{1,0:T(8,128)(2,1)} %pad_maximum_fusion.11.refs_0_.refs_4_, bf16[896,4096]{1,0:T(8,128)(2,1)} %collective-permute-done.65.refs_1_.refs_5_, bf16[896,4096]{1,0:T(8,128)(2,1)} %collective-permute-done.66.refs_2_.refs_6_, ...), custom_call_target="tpu_custom_call" | custom-call | flops 30064771072 | bytes 40894464 | tf_op jit(solution)/shard_map/pallas_call | solution.py:96
  2402.1 37.8 %shard_map.132.refs_8_ = bf16[1024,7168]{1,0:T(8,128)(2,1)} custom-call(bf16[1024,3584]{1,0:T(8,128)(2,1)} %collective-permute-done.60.h_ref, bf16[896,4096]{1,0:T(8,128)(2,1)} %pad_maximum_fusion.10.refs_0_.refs_4_, bf16[896,4096]{1,0:T(8,128)(2,1)} %collective-permute-done.63.refs_1_.refs_5_, ...), custom_call_target="tpu_custom_call", output_to_operand_aliasing={{}: (9, {})} | custom-call | flops 30064771072 | bytes 40894464 | tf_op jit(solution)/shard_map/pallas_call | solution.py:96
  2452.0 38.2 %shard_map.133.refs_8_ = bf16[1024,7168]{1,0:T(8,128)(2,1)} custom-call(bf16[1024,3584]{1,0:T(8,128)(2,1)} %pad_maximum_fusion.8.h_ref, bf16[896,4096]{1,0:T(8,128)(2,1)} %pad_maximum_fusion.9.refs_0_.refs_4_, bf16[896,4096]{1,0:T(8,128)(2,1)} %collective-permute-done.61.refs_1_.refs_5_, ...), custom_call_target="tpu_custom_call", output_to_operand_aliasing={{}: (9, {})} | custom-call | flops 30064771072 | bytes 40894464 | tf_op jit(solution)/shard_map/pallas_call | solution.py:96
  2490.2 37.7 %shard_map.134.refs_8_ = bf16[1024,7168]{1,0:T(8,128)(2,1)} custom-call(bf16[1024,3584]{1,0:T(8,128)(2,1)} %collective-permute-done.60.h_ref, bf16[896,4096]{1,0:T(8,128)(2,1)} %pad_maximum_fusion.9.refs_0_.refs_4_, bf16[896,4096]{1,0:T(8,128)(2,1)} %collective-permute-done.61.refs_1_.refs_5_, ...), custom_call_target="tpu_custom_call", output_to_operand_aliasing={{}: (9, {})} | custom-call | flops 30064771072 | bytes 40894464 | tf_op jit(solution)/shard_map/pallas_call | solution.py:96
  2534.7 21.7 shard_map.135
  2569.9 112.2 %collective-permute-done.73 = bf16[7168,512]{1,0:T(8,128)(2,1)} collective-permute-done((bf16[7168,512]{1,0:T(8,128)(2,1)}, bf16[7168,512]{1,0:T(8,128)(2,1)}, u32[]{:S(2)}, u32[]{:S(2)}) %collective-permute-start.73) | collective-permute-done | bytes 7340064 | tf_op jit(solution)/shard_map/ppermute | solution.py:183
  2682.1 21.7 shard_map.136
  2703.8 14.4 fusion.112
  2719.9 13.5 fusion.88
  2744.5 14.0 fusion.116
  2782.3 14.0 fusion.91
  2806.6 14.6 fusion.113
  2870.7 79.6 %collective-permute-done.83 = f32[1024,384]{1,0:T(8,128)S(1)} collective-permute-done((f32[1024,384]{1,0:T(8,128)S(1)}, f32[1024,384]{1,0:T(8,128)S(1)}, u32[]{:S(2)}, u32[]{:S(2)}) %collective-permute-start.83) | collective-permute-done | bytes 1572896 | tf_op jit(solution)/shard_map/ppermute | solution.py:189
  2963.5 13.7 fusion.122
  2987.7 44.9 %collective-permute-done.78 = f32[1024,512]{1,0:T(8,128)S(1)} collective-permute-done((f32[1024,512]{1,0:T(8,128)}, f32[1024,512]{1,0:T(8,128)S(1)}, u32[]{:S(2)}, u32[]{:S(2)}) %collective-permute-start.78) | collective-permute-done | bytes 2097184 | tf_op jit(solution)/shard_map/ppermute | solution.py:189
  3034.0 43.7 %collective-permute-done.71 = f32[1024,512]{1,0:T(8,128)} collective-permute-done((f32[1024,512]{1,0:T(8,128)}, f32[1024,512]{1,0:T(8,128)}, u32[]{:S(2)}, u32[]{:S(2)}) %collective-permute-start.71) | collective-permute-done | bytes 2097184 | tf_op jit(solution)/shard_map/ppermute | solution.py:189
  3094.2 15.7 collective-permute-done.84
  (490 shorter events, 646.9 us)
Async XLA Ops:
  11.6 169.1 %collective-permute-start.5 = (bf16[896,2048]{1,0:T(8,128)(2,1)}, bf16[896,2048]{1,0:T(8,128)(2,1)}, u32[]{:S(2)}, u32[]{:S(2)}) collective-permute-start(bf16[896,2048]{1,0:T(8,128)(2,1)} %constant_dynamic-update-slice_fusion.refs_0_), channel_id=1, source_target_pairs={{0,2},{1,3},{2,0},{3,1},{4,6},{5,7},{6,4},{7,5}} | collective-permute-start | bytes 11010056 | tf_op jit(solution)/shard_map/ppermute | solution.py:183
  15.0 248.3 %collective-permute-start.4 = (bf16[896,2048]{1,0:T(8,128)(2,1)}, bf16[896,2048]{1,0:T(8,128)(2,1)}, u32[]{:S(2)}, u32[]{:S(2)}) collective-permute-start(bf16[896,2048]{1,0:T(8,128)(2,1)} %constant_dynamic-update-slice_fusion.refs_0_), channel_id=1, source_target_pairs={{0,1},{1,0},{2,3},{3,2},{4,5},{5,4},{6,7},{7,6}} | collective-permute-start | bytes 11010056 | tf_op jit(solution)/shard_map/ppermute | solution.py:186
  20.3 152.9 %collective-permute-start.1 = (bf16[896,2048]{1,0:T(8,128)(2,1)}, bf16[896,2048]{1,0:T(8,128)(2,1)}, u32[]{:S(2)}, u32[]{:S(2)}) collective-permute-start(bf16[896,2048]{1,0:T(8,128)(2,1)} %bitcast.40.refs_0_), channel_id=1, source_target_pairs={{0,2},{1,3},{2,0},{3,1},{4,6},{5,7},{6,4},{7,5}} | collective-permute-start | bytes 11010056 | tf_op jit(solution)/shard_map/ppermute | solution.py:183
  20.4 187.7 %collective-permute-start = (bf16[896,2048]{1,0:T(8,128)(2,1)}, bf16[896,2048]{1,0:T(8,128)(2,1)}, u32[]{:S(2)}, u32[]{:S(2)}) collective-permute-start(bf16[896,2048]{1,0:T(8,128)(2,1)} %bitcast.40.refs_0_), channel_id=1, source_target_pairs={{0,1},{1,0},{2,3},{3,2},{4,5},{5,4},{6,7},{7,6}} | collective-permute-start | bytes 11010056 | tf_op jit(solution)/shard_map/ppermute | solution.py:186
  31.7 160.2 %collective-permute-start.7 = (bf16[1024,3584]{1,0:T(8,128)(2,1)}, bf16[1024,3584]{1,0:T(8,128)(2,1)}, u32[]{:S(2)}, u32[]{:S(2)}) collective-permute-start(bf16[1024,3584]{1,0:T(8,128)(2,1)} %pad_maximum_fusion.1), channel_id=1, source_target_pairs={{0,4},{4,0},{1,5},{5,1},{2,6},{6,2},{3,7},{7,3}} | collective-permute-start | bytes 22020104 | tf_op jit(solution)/shard_map/ppermute | solution.py:189
  208.0 229.1 %collective-permute-start.8 = (bf16[2048,896]{1,0:T(8,128)(2,1)}, bf16[2048,896]{1,0:T(8,128)(2,1)}, u32[]{:S(2)}, u32[]{:S(2)}) collective-permute-start(bf16[2048,896]{1,0:T(8,128)(2,1)} %bitcast.6), channel_id=1, source_target_pairs={{0,1},{1,0},{2,3},{3,2},{4,5},{5,4},{6,7},{7,6}} | collective-permute-start | bytes 11010056 | tf_op jit(solution)/shard_map/ppermute | solution.py:186
  208.5 211.6 %collective-permute-start.24 = (bf16[896,4096]{1,0:T(8,128)(2,1)}, bf16[896,4096]{1,0:T(8,128)(2,1)}, u32[]{:S(2)}, u32[]{:S(2)}) collective-permute-start(bf16[896,4096]{1,0:T(8,128)(2,1)} %pad_maximum_fusion.6.refs_0_.refs_4_), channel_id=1, source_target_pairs={{0,2},{1,3},{2,0},{3,1},{4,6},{5,7},{6,4},{7,5}} | collective-permute-start | bytes 22020104 | tf_op jit(solution)/shard_map/ppermute | solution.py:183
  263.3 173.9 %collective-permute-start.10 = (bf16[2048,896]{1,0:T(8,128)(2,1)}, bf16[2048,896]{1,0:T(8,128)(2,1)}, u32[]{:S(2)}, u32[]{:S(2)}) collective-permute-start(bf16[2048,896]{1,0:T(8,128)(2,1)} %collective-permute-done.9), channel_id=1, source_target_pairs={{0,1},{1,0},{2,3},{3,2},{4,5},{5,4},{6,7},{7,6}} | collective-permute-start | bytes 11010056 | tf_op jit(solution)/shard_map/ppermute | solution.py:186
  263.3 174.4 %collective-permute-start.12 = (bf16[2048,896]{1,0:T(8,128)(2,1)}, bf16[2048,896]{1,0:T(8,128)(2,1)}, u32[]{:S(2)}, u32[]{:S(2)}) collective-permute-start(bf16[2048,896]{1,0:T(8,128)(2,1)} %bitcast.6), channel_id=1, source_target_pairs={{0,4},{4,0},{1,5},{5,1},{2,6},{6,2},{3,7},{7,3}} | collective-permute-start | bytes 11010056 | tf_op jit(solution)/shard_map/ppermute | solution.py:189
  288.0 158.2 %collective-permute-start.14 = (bf16[2048,896]{1,0:T(8,128)(2,1)}, bf16[2048,896]{1,0:T(8,128)(2,1)}, u32[]{:S(2)}, u32[]{:S(2)}) collective-permute-start(bf16[2048,896]{1,0:T(8,128)(2,1)} %collective-permute-done.9), channel_id=1, source_target_pairs={{0,4},{4,0},{1,5},{5,1},{2,6},{6,2},{3,7},{7,3}} | collective-permute-start | bytes 11010056 | tf_op jit(solution)/shard_map/ppermute | solution.py:189
  420.1 93.7 %collective-permute-start.11 = (bf16[2,512,2048]{2,1,0:T(8,128)(2,1)}, bf16[2,512,2048]{2,1,0:T(8,128)(2,1)S(1)}, u32[]{:S(2)}, u32[]{:S(2)}) collective-permute-start(bf16[2,512,2048]{2,1,0:T(8,128)(2,1)} %shard_map.114), channel_id=1, source_target_pairs={{0,4},{4,0},{1,5},{5,1},{2,6},{6,2},{3,7},{7,3}} | collective-permute-start | bytes 12582920 | tf_op jit(solution)/shard_map/ppermute | solution.py:189
  437.2 111.9 %collective-permute-start.23 = (bf16[896,4096]{1,0:T(8,128)(2,1)S(1)}, bf16[896,4096]{1,0:T(8,128)(2,1)}, u32[]{:S(2)}, u32[]{:S(2)}) collective-permute-start(bf16[896,4096]{1,0:T(8,128)(2,1)S(1)} %bitcast.207), channel_id=1, source_target_pairs={{0,1},{1,0},{2,3},{3,2},{4,5},{5,4},{6,7},{7,6}} | collective-permute-start | bytes 22020104 | tf_op jit(solution)/shard_map/ppermute | solution.py:186
  437.2 111.8 %collective-permute-start.25 = (bf16[896,4096]{1,0:T(8,128)(2,1)}, bf16[896,4096]{1,0:T(8,128)(2,1)}, u32[]{:S(2)}, u32[]{:S(2)}) collective-permute-start(bf16[896,4096]{1,0:T(8,128)(2,1)} %collective-permute-done.24.refs_2_.refs_6_), channel_id=1, source_target_pairs={{0,1},{1,0},{2,3},{3,2},{4,5},{5,4},{6,7},{7,6}} | collective-permute-start | bytes 22020104 | tf_op jit(solution)/shard_map/ppermute | solution.py:186
  437.7 92.5 %collective-permute-start.13 = (bf16[2048,896]{1,0:T(8,128)(2,1)}, bf16[2048,896]{1,0:T(8,128)(2,1)S(1)}, u32[]{:S(2)}, u32[]{:S(2)}) collective-permute-start(bf16[2048,896]{1,0:T(8,128)(2,1)} %collective-permute-done.12), channel_id=1, source_target_pairs={{0,1},{1,0},{2,3},{3,2},{4,5},{5,4},{6,7},{7,6}} | collective-permute-start | bytes 11010056 | tf_op jit(solution)/shard_map/ppermute | solution.py:186
  446.2 89.0 %collective-permute-start.15 = (bf16[2048,896]{1,0:T(8,128)(2,1)}, bf16[2048,896]{1,0:T(8,128)(2,1)S(1)}, u32[]{:S(2)}, u32[]{:S(2)}) collective-permute-start(bf16[2048,896]{1,0:T(8,128)(2,1)} %collective-permute-done.14), channel_id=1, source_target_pairs={{0,1},{1,0},{2,3},{3,2},{4,5},{5,4},{6,7},{7,6}} | collective-permute-start | bytes 11010056 | tf_op jit(solution)/shard_map/ppermute | solution.py:186
  513.8 159.9 %collective-permute-start.22 = (bf16[896,4096]{1,0:T(8,128)(2,1)}, bf16[896,4096]{1,0:T(8,128)(2,1)}, u32[]{:S(2)}, u32[]{:S(2)}) collective-permute-start(bf16[896,4096]{1,0:T(8,128)(2,1)} %pad_maximum_fusion.5.refs_0_.refs_4_), channel_id=1, source_target_pairs={{0,2},{1,3},{2,0},{3,1},{4,6},{5,7},{6,4},{7,5}} | collective-permute-start | bytes 22020104 | tf_op jit(solution)/shard_map/ppermute | solution.py:183
  530.3 152.7 %collective-permute-start.21 = (bf16[896,4096]{1,0:T(8,128)(2,1)}, bf16[896,4096]{1,0:T(8,128)(2,1)}, u32[]{:S(2)}, u32[]{:S(2)}) collective-permute-start(bf16[896,4096]{1,0:T(8,128)(2,1)} %pad_maximum_fusion.5.refs_0_.refs_4_), channel_id=1, source_target_pairs={{0,1},{1,0},{2,3},{3,2},{4,5},{5,4},{6,7},{7,6}} | collective-permute-start | bytes 22020104 | tf_op jit(solution)/shard_map/ppermute | solution.py:186
  673.7 160.7 %collective-permute-start.18 = (bf16[1024,3584]{1,0:T(8,128)(2,1)}, bf16[1024,3584]{1,0:T(8,128)(2,1)}, u32[]{:S(2)}, u32[]{:S(2)}) collective-permute-start(bf16[1024,3584]{1,0:T(8,128)(2,1)} %pad_maximum_fusion.3.h_ref), channel_id=1, source_target_pairs={{0,4},{4,0},{1,5},{5,1},{2,6},{6,2},{3,7},{7,3}} | collective-permute-start | bytes 22020104 | tf_op jit(solution)/shard_map/ppermute | solution.py:189
  681.5 228.3 %collective-permute-start.20 = (bf16[896,4096]{1,0:T(8,128)(2,1)}, bf16[896,4096]{1,0:T(8,128)(2,1)}, u32[]{:S(2)}, u32[]{:S(2)}) collective-permute-start(bf16[896,4096]{1,0:T(8,128)(2,1)} %pad_maximum_fusion.4.refs_0_.refs_4_), channel_id=1, source_target_pairs={{0,2},{1,3},{2,0},{3,1},{4,6},{5,7},{6,4},{7,5}} | collective-permute-start | bytes 22020104 | tf_op jit(solution)/shard_map/ppermute | solution.py:183
  683.0 257.1 %collective-permute-start.19 = (bf16[896,4096]{1,0:T(8,128)(2,1)}, bf16[896,4096]{1,0:T(8,128)(2,1)}, u32[]{:S(2)}, u32[]{:S(2)}) collective-permute-start(bf16[896,4096]{1,0:T(8,128)(2,1)} %pad_maximum_fusion.4.refs_0_.refs_4_), channel_id=1, source_target_pairs={{0,1},{1,0},{2,3},{3,2},{4,5},{5,4},{6,7},{7,6}} | collective-permute-start | bytes 22020104 | tf_op jit(solution)/shard_map/ppermute | solution.py:186
  917.9 98.3 %collective-permute-start.17 = (bf16[896,2048]{1,0:T(8,128)(2,1)}, bf16[896,2048]{1,0:T(8,128)(2,1)}, u32[]{:S(2)}, u32[]{:S(2)}) collective-permute-start(bf16[896,2048]{1,0:T(8,128)(2,1)} %pad_maximum_fusion.12.refs_0_.refs_4_), channel_id=1, source_target_pairs={{0,2},{1,3},{2,0},{3,1},{4,6},{5,7},{6,4},{7,5}} | collective-permute-start | bytes 11010056 | tf_op jit(solution)/shard_map/ppermute | solution.py:183
  919.6 109.0 %collective-permute-start.16 = (bf16[896,2048]{1,0:T(8,128)(2,1)}, bf16[896,2048]{1,0:T(8,128)(2,1)}, u32[]{:S(2)}, u32[]{:S(2)}) collective-permute-start(bf16[896,2048]{1,0:T(8,128)(2,1)} %pad_maximum_fusion.12.refs_0_.refs_4_), channel_id=1, source_target_pairs={{0,1},{1,0},{2,3},{3,2},{4,5},{5,4},{6,7},{7,6}} | collective-permute-start | bytes 11010056 | tf_op jit(solution)/shard_map/ppermute | solution.py:186
  929.3 123.0 %collective-permute-start.32 = (bf16[7168,384]{1,0:T(8,128)(2,1)}, bf16[7168,384]{1,0:T(8,128)(2,1)}, u32[]{:S(2)}, u32[]{:S(2)}) collective-permute-start(bf16[7168,384]{1,0:T(8,128)(2,1)} %get-tuple-element.142), channel_id=1, source_target_pairs={{0,1},{1,0},{2,3},{3,2},{4,5},{5,4},{6,7},{7,6}} | collective-permute-start | bytes 16515080 | tf_op jit(solution)/shard_map/ppermute | solution.py:186
  940.1 217.6 %collective-permute-start.31 = (bf16[7168,512]{1,0:T(8,128)(2,1)}, bf16[7168,512]{1,0:T(8,128)(2,1)}, u32[]{:S(2)}, u32[]{:S(2)}) collective-permute-start(bf16[7168,512]{1,0:T(8,128)(2,1)} %get-tuple-element.140), channel_id=1, source_target_pairs={{0,2},{1,3},{2,0},{3,1},{4,6},{5,7},{6,4},{7,5}} | collective-permute-start | bytes 22020104 | tf_op jit(solution)/shard_map/ppermute | solution.py:183
  1016.2 265.7 %collective-permute-start.30 = (bf16[7168,384]{1,0:T(8,128)(2,1)}, bf16[7168,384]{1,0:T(8,128)(2,1)}, u32[]{:S(2)}, u32[]{:S(2)}) collective-permute-start(bf16[7168,384]{1,0:T(8,128)(2,1)} %get-tuple-element.142), channel_id=1, source_target_pairs={{0,2},{1,3},{2,0},{3,1},{4,6},{5,7},{6,4},{7,5}} | collective-permute-start | bytes 16515080 | tf_op jit(solution)/shard_map/ppermute | solution.py:183
  1028.5 176.4 %collective-permute-start.36 = (bf16[7168,512]{1,0:T(8,128)(2,1)}, bf16[7168,512]{1,0:T(8,128)(2,1)}, u32[]{:S(2)}, u32[]{:S(2)}) collective-permute-start(bf16[7168,512]{1,0:T(8,128)(2,1)} %get-tuple-element.140), channel_id=1, source_target_pairs={{0,1},{1,0},{2,3},{3,2},{4,5},{5,4},{6,7},{7,6}} | collective-permute-start | bytes 22020104 | tf_op jit(solution)/shard_map/ppermute | solution.py:186
  1157.7 110.1 %collective-permute-start.33 = (bf16[7168,512]{1,0:T(8,128)(2,1)}, bf16[7168,512]{1,0:T(8,128)(2,1)}, u32[]{:S(2)}, u32[]{:S(2)}) collective-permute-start(bf16[7168,512]{1,0:T(8,128)(2,1)} %collective-permute-done.31), channel_id=1, source_target_pairs={{0,1},{1,0},{2,3},{3,2},{4,5},{5,4},{6,7},{7,6}} | collective-permute-start | bytes 22020104 | tf_op jit(solution)/shard_map/ppermute | solution.py:186
  1240.7 129.2 %collective-permute-start.37 = (f32[1024,512]{1,0:T(8,128)}, f32[1024,512]{1,0:T(8,128)S(1)}, u32[]{:S(2)}, u32[]{:S(2)}) collective-permute-start(f32[1024,512]{1,0:T(8,128)} %fusion.104), channel_id=1, source_target_pairs={{0,4},{4,0},{1,5},{5,1},{2,6},{6,2},{3,7},{7,3}} | collective-permute-start | bytes 6291464 | tf_op jit(solution)/shard_map/ppermute | solution.py:189
  1242.4 204.3 %collective-permute-start.39 = (f32[1024,512]{1,0:T(8,128)}, f32[1024,512]{1,0:T(8,128)S(1)}, u32[]{:S(2)}, u32[]{:S(2)}) collective-permute-start(f32[1024,512]{1,0:T(8,128)} %fusion.100), channel_id=1, source_target_pairs={{0,4},{4,0},{1,5},{5,1},{2,6},{6,2},{3,7},{7,3}} | collective-permute-start | bytes 6291464 | tf_op jit(solution)/shard_map/ppermute | solution.py:189
  1281.9 88.3 %collective-permute-start.34 = (bf16[7168,384]{1,0:T(8,128)(2,1)}, bf16[7168,384]{1,0:T(8,128)(2,1)}, u32[]{:S(2)}, u32[]{:S(2)}) collective-permute-start(bf16[7168,384]{1,0:T(8,128)(2,1)} %collective-permute-done.30), channel_id=1, source_target_pairs={{0,1},{1,0},{2,3},{3,2},{4,5},{5,4},{6,7},{7,6}} | collective-permute-start | bytes 16515080 | tf_op jit(solution)/shard_map/ppermute | solution.py:186
  1296.1 117.0 %collective-permute-start.29 = (f32[1024,512]{1,0:T(8,128)}, f32[1024,512]{1,0:T(8,128)S(1)}, u32[]{:S(2)}, u32[]{:S(2)}) collective-permute-start(f32[1024,512]{1,0:T(8,128)} %fusion.89), channel_id=1, source_target_pairs={{0,4},{4,0},{1,5},{5,1},{2,6},{6,2},{3,7},{7,3}} | collective-permute-start | bytes 6291464 | tf_op jit(solution)/shard_map/ppermute | solution.py:189
  1369.9 157.3 %collective-permute-start.41 = (f32[1024,512]{1,0:T(8,128)}, f32[1024,512]{1,0:T(8,128)}, u32[]{:S(2)}, u32[]{:S(2)}) collective-permute-start(f32[1024,512]{1,0:T(8,128)} %fusion.101), channel_id=1, source_target_pairs={{0,4},{4,0},{1,5},{5,1},{2,6},{6,2},{3,7},{7,3}} | collective-permute-start | bytes 6291464 | tf_op jit(solution)/shard_map/ppermute | solution.py:189
  1370.2 154.8 %collective-permute-start.40 = (f32[1024,384]{1,0:T(8,128)S(1)}, f32[1024,384]{1,0:T(8,128)}, u32[]{:S(2)}, u32[]{:S(2)}) collective-permute-start(f32[1024,384]{1,0:T(8,128)S(1)} %fusion.108), channel_id=1, source_target_pairs={{0,4},{4,0},{1,5},{5,1},{2,6},{6,2},{3,7},{7,3}} | collective-permute-start | bytes 4718600 | tf_op jit(solution)/shard_map/ppermute | solution.py:189
  1413.0 172.3 %collective-permute-start.44 = (bf16[896,2048]{1,0:T(8,128)(2,1)}, bf16[896,2048]{1,0:T(8,128)(2,1)}, u32[]{:S(2)}, u32[]{:S(2)}) collective-permute-start(bf16[896,2048]{1,0:T(8,128)(2,1)} %bitcast.57.refs_0_), channel_id=1, source_target_pairs={{0,2},{1,3},{2,0},{3,1},{4,6},{5,7},{6,4},{7,5}} | collective-permute-start | bytes 11010056 | tf_op jit(solution)/shard_map/ppermute | solution.py:183
  1446.7 140.4 %collective-permute-start.43 = (bf16[896,2048]{1,0:T(8,128)(2,1)}, bf16[896,2048]{1,0:T(8,128)(2,1)}, u32[]{:S(2)}, u32[]{:S(2)}) collective-permute-start(bf16[896,2048]{1,0:T(8,128)(2,1)} %bitcast.57.refs_0_), channel_id=1, source_target_pairs={{0,1},{1,0},{2,3},{3,2},{4,5},{5,4},{6,7},{7,6}} | collective-permute-start | bytes 11010056 | tf_op jit(solution)/shard_map/ppermute | solution.py:186
  1446.8 140.1 %collective-permute-start.47 = (bf16[896,2048]{1,0:T(8,128)(2,1)}, bf16[896,2048]{1,0:T(8,128)(2,1)}, u32[]{:S(2)}, u32[]{:S(2)}) collective-permute-start(bf16[896,2048]{1,0:T(8,128)(2,1)} %constant_dynamic-update-slice_fusion.2.refs_0_), channel_id=1, source_target_pairs={{0,2},{1,3},{2,0},{3,1},{4,6},{5,7},{6,4},{7,5}} | collective-permute-start | bytes 11010056 | tf_op jit(solution)/shard_map/ppermute | solution.py:183
  1583.7 161.2 %collective-permute-start.49 = (bf16[1024,3584]{1,0:T(8,128)(2,1)}, bf16[1024,3584]{1,0:T(8,128)(2,1)}, u32[]{:S(2)}, u32[]{:S(2)}) collective-permute-start(bf16[1024,3584]{1,0:T(8,128)(2,1)} %pad_maximum_fusion.7.h_ref), channel_id=1, source_target_pairs={{0,4},{4,0},{1,5},{5,1},{2,6},{6,2},{3,7},{7,3}} | collective-permute-start | bytes 22020104 | tf_op jit(solution)/shard_map/ppermute | solution.py:189
  1595.1 269.0 %collective-permute-start.50 = (bf16[2048,896]{1,0:T(8,128)(2,1)}, bf16[2048,896]{1,0:T(8,128)(2,1)}, u32[]{:S(2)}, u32[]{:S(2)}) collective-permute-start(bf16[2048,896]{1,0:T(8,128)(2,1)} %bitcast.24), channel_id=1, source_target_pairs={{0,1},{1,0},{2,3},{3,2},{4,5},{5,4},{6,7},{7,6}} | collective-permute-start | bytes 11010056 | tf_op jit(solution)/shard_map/ppermute | solution.py:186
  1667.4 188.4 %collective-permute-start.54 = (bf16[2048,896]{1,0:T(8,128)(2,1)}, bf16[2048,896]{1,0:T(8,128)(2,1)}, u32[]{:S(2)}, u32[]{:S(2)}) collective-permute-start(bf16[2048,896]{1,0:T(8,128)(2,1)} %bitcast.24), channel_id=1, source_target_pairs={{0,4},{4,0},{1,5},{5,1},{2,6},{6,2},{3,7},{7,3}} | collective-permute-start | bytes 11010056 | tf_op jit(solution)/shard_map/ppermute | solution.py:189
  1667.8 189.8 %collective-permute-start.52 = (bf16[2048,896]{1,0:T(8,128)(2,1)}, bf16[2048,896]{1,0:T(8,128)(2,1)}, u32[]{:S(2)}, u32[]{:S(2)}) collective-permute-start(bf16[2048,896]{1,0:T(8,128)(2,1)} %collective-permute-done.51), channel_id=1, source_target_pairs={{0,1},{1,0},{2,3},{3,2},{4,5},{5,4},{6,7},{7,6}} | collective-permute-start | bytes 11010056 | tf_op jit(solution)/shard_map/ppermute | solution.py:186
  1813.4 185.0 %collective-permute-start.53 = (bf16[2,512,2048]{2,1,0:T(8,128)(2,1)}, bf16[2,512,2048]{2,1,0:T(8,128)(2,1)}, u32[]{:S(2)}, u32[]{:S(2)}) collective-permute-start(bf16[2,512,2048]{2,1,0:T(8,128)(2,1)} %shard_map.128), channel_id=1, source_target_pairs={{0,4},{4,0},{1,5},{5,1},{2,6},{6,2},{3,7},{7,3}} | collective-permute-start | bytes 12582920 | tf_op jit(solution)/shard_map/ppermute | solution.py:189
  1815.1 174.7 %collective-permute-start.56 = (bf16[2048,896]{1,0:T(8,128)(2,1)}, bf16[2048,896]{1,0:T(8,128)(2,1)}, u32[]{:S(2)}, u32[]{:S(2)}) collective-permute-start(bf16[2048,896]{1,0:T(8,128)(2,1)} %collective-permute-done.51), channel_id=1, source_target_pairs={{0,4},{4,0},{1,5},{5,1},{2,6},{6,2},{3,7},{7,3}} | collective-permute-start | bytes 11010056 | tf_op jit(solution)/shard_map/ppermute | solution.py:189
  1855.8 181.1 %collective-permute-start.66 = (bf16[896,4096]{1,0:T(8,128)(2,1)}, bf16[896,4096]{1,0:T(8,128)(2,1)}, u32[]{:S(2)}, u32[]{:S(2)}) collective-permute-start(bf16[896,4096]{1,0:T(8,128)(2,1)} %pad_maximum_fusion.11.refs_0_.refs_4_), channel_id=1, source_target_pairs={{0,2},{1,3},{2,0},{3,1},{4,6},{5,7},{6,4},{7,5}} | collective-permute-start | bytes 22020104 | tf_op jit(solution)/shard_map/ppermute | solution.py:183
  1857.5 157.4 %collective-permute-start.55 = (bf16[2048,896]{1,0:T(8,128)(2,1)}, bf16[2048,896]{1,0:T(8,128)(2,1)S(1)}, u32[]{:S(2)}, u32[]{:S(2)}) collective-permute-start(bf16[2048,896]{1,0:T(8,128)(2,1)} %collective-permute-done.54), channel_id=1, source_target_pairs={{0,1},{1,0},{2,3},{3,2},{4,5},{5,4},{6,7},{7,6}} | collective-permute-start | bytes 11010056 | tf_op jit(solution)/shard_map/ppermute | solution.py:186
  1864.2 180.9 %collective-permute-start.65 = (bf16[896,4096]{1,0:T(8,128)(2,1)}, bf16[896,4096]{1,0:T(8,128)(2,1)}, u32[]{:S(2)}, u32[]{:S(2)}) collective-permute-start(bf16[896,4096]{1,0:T(8,128)(2,1)} %pad_maximum_fusion.11.refs_0_.refs_4_), channel_id=1, source_target_pairs={{0,1},{1,0},{2,3},{3,2},{4,5},{5,4},{6,7},{7,6}} | collective-permute-start | bytes 22020104 | tf_op jit(solution)/shard_map/ppermute | solution.py:186
  2043.4 160.3 %collective-permute-start.64 = (bf16[896,4096]{1,0:T(8,128)(2,1)}, bf16[896,4096]{1,0:T(8,128)(2,1)}, u32[]{:S(2)}, u32[]{:S(2)}) collective-permute-start(bf16[896,4096]{1,0:T(8,128)(2,1)} %pad_maximum_fusion.10.refs_0_.refs_4_), channel_id=1, source_target_pairs={{0,2},{1,3},{2,0},{3,1},{4,6},{5,7},{6,4},{7,5}} | collective-permute-start | bytes 22020104 | tf_op jit(solution)/shard_map/ppermute | solution.py:183
  2045.1 167.7 %collective-permute-start.63 = (bf16[896,4096]{1,0:T(8,128)(2,1)}, bf16[896,4096]{1,0:T(8,128)(2,1)}, u32[]{:S(2)}, u32[]{:S(2)}) collective-permute-start(bf16[896,4096]{1,0:T(8,128)(2,1)} %pad_maximum_fusion.10.refs_0_.refs_4_), channel_id=1, source_target_pairs={{0,1},{1,0},{2,3},{3,2},{4,5},{5,4},{6,7},{7,6}} | collective-permute-start | bytes 22020104 | tf_op jit(solution)/shard_map/ppermute | solution.py:186
  2203.7 160.7 %collective-permute-start.60 = (bf16[1024,3584]{1,0:T(8,128)(2,1)}, bf16[1024,3584]{1,0:T(8,128)(2,1)}, u32[]{:S(2)}, u32[]{:S(2)}) collective-permute-start(bf16[1024,3584]{1,0:T(8,128)(2,1)} %pad_maximum_fusion.8.h_ref), channel_id=1, source_target_pairs={{0,4},{4,0},{1,5},{5,1},{2,6},{6,2},{3,7},{7,3}} | collective-permute-start | bytes 22020104 | tf_op jit(solution)/shard_map/ppermute | solution.py:189
  2211.3 228.7 %collective-permute-start.62 = (bf16[896,4096]{1,0:T(8,128)(2,1)}, bf16[896,4096]{1,0:T(8,128)(2,1)}, u32[]{:S(2)}, u32[]{:S(2)}) collective-permute-start(bf16[896,4096]{1,0:T(8,128)(2,1)} %pad_maximum_fusion.9.refs_0_.refs_4_), channel_id=1, source_target_pairs={{0,2},{1,3},{2,0},{3,1},{4,6},{5,7},{6,4},{7,5}} | collective-permute-start | bytes 22020104 | tf_op jit(solution)/shard_map/ppermute | solution.py:183
  2212.8 231.7 %collective-permute-start.61 = (bf16[896,4096]{1,0:T(8,128)(2,1)}, bf16[896,4096]{1,0:T(8,128)(2,1)}, u32[]{:S(2)}, u32[]{:S(2)}) collective-permute-start(bf16[896,4096]{1,0:T(8,128)(2,1)} %pad_maximum_fusion.9.refs_0_.refs_4_), channel_id=1, source_target_pairs={{0,1},{1,0},{2,3},{3,2},{4,5},{5,4},{6,7},{7,6}} | collective-permute-start | bytes 22020104 | tf_op jit(solution)/shard_map/ppermute | solution.py:186
  2442.2 85.7 %collective-permute-start.59 = (bf16[896,2048]{1,0:T(8,128)(2,1)}, bf16[896,2048]{1,0:T(8,128)(2,1)}, u32[]{:S(2)}, u32[]{:S(2)}) collective-permute-start(bf16[896,2048]{1,0:T(8,128)(2,1)} %pad_maximum_fusion.17.refs_0_.refs_4_), channel_id=1, source_target_pairs={{0,2},{1,3},{2,0},{3,1},{4,6},{5,7},{6,4},{7,5}} | collective-permute-start | bytes 11010056 | tf_op jit(solution)/shard_map/ppermute | solution.py:183
  2443.9 85.8 %collective-permute-start.58 = (bf16[896,2048]{1,0:T(8,128)(2,1)}, bf16[896,2048]{1,0:T(8,128)(2,1)}, u32[]{:S(2)}, u32[]{:S(2)}) collective-permute-start(bf16[896,2048]{1,0:T(8,128)(2,1)} %pad_maximum_fusion.17.refs_0_.refs_4_), channel_id=1, source_target_pairs={{0,1},{1,0},{2,3},{3,2},{4,5},{5,4},{6,7},{7,6}} | collective-permute-start | bytes 11010056 | tf_op jit(solution)/shard_map/ppermute | solution.py:186
  2444.1 112.3 %collective-permute-start.74 = (bf16[7168,384]{1,0:T(8,128)(2,1)}, bf16[7168,384]{1,0:T(8,128)(2,1)}, u32[]{:S(2)}, u32[]{:S(2)}) collective-permute-start(bf16[7168,384]{1,0:T(8,128)(2,1)} %get-tuple-element.141), channel_id=1, source_target_pairs={{0,1},{1,0},{2,3},{3,2},{4,5},{5,4},{6,7},{7,6}} | collective-permute-start | bytes 16515080 | tf_op jit(solution)/shard_map/ppermute | solution.py:186
  2444.5 237.6 %collective-permute-start.73 = (bf16[7168,512]{1,0:T(8,128)(2,1)}, bf16[7168,512]{1,0:T(8,128)(2,1)}, u32[]{:S(2)}, u32[]{:S(2)}) collective-permute-start(bf16[7168,512]{1,0:T(8,128)(2,1)} %get-tuple-element.139), channel_id=1, source_target_pairs={{0,2},{1,3},{2,0},{3,1},{4,6},{5,7},{6,4},{7,5}} | collective-permute-start | bytes 22020104 | tf_op jit(solution)/shard_map/ppermute | solution.py:183
  2528.1 293.1 %collective-permute-start.72 = (bf16[7168,384]{1,0:T(8,128)(2,1)}, bf16[7168,384]{1,0:T(8,128)(2,1)}, u32[]{:S(2)}, u32[]{:S(2)}) collective-permute-start(bf16[7168,384]{1,0:T(8,128)(2,1)} %get-tuple-element.141), channel_id=1, source_target_pairs={{0,2},{1,3},{2,0},{3,1},{4,6},{5,7},{6,4},{7,5}} | collective-permute-start | bytes 16515080 | tf_op jit(solution)/shard_map/ppermute | solution.py:183
  2529.8 214.7 %collective-permute-start.77 = (bf16[7168,512]{1,0:T(8,128)(2,1)}, bf16[7168,512]{1,0:T(8,128)(2,1)}, u32[]{:S(2)}, u32[]{:S(2)}) collective-permute-start(bf16[7168,512]{1,0:T(8,128)(2,1)} %get-tuple-element.139), channel_id=1, source_target_pairs={{0,1},{1,0},{2,3},{3,2},{4,5},{5,4},{6,7},{7,6}} | collective-permute-start | bytes 22020104 | tf_op jit(solution)/shard_map/ppermute | solution.py:186
  2682.1 124.5 %collective-permute-start.75 = (bf16[7168,512]{1,0:T(8,128)(2,1)}, bf16[7168,512]{1,0:T(8,128)(2,1)}, u32[]{:S(2)}, u32[]{:S(2)}) collective-permute-start(bf16[7168,512]{1,0:T(8,128)(2,1)} %collective-permute-done.73), channel_id=1, source_target_pairs={{0,1},{1,0},{2,3},{3,2},{4,5},{5,4},{6,7},{7,6}} | collective-permute-start | bytes 22020104 | tf_op jit(solution)/shard_map/ppermute | solution.py:186
  2718.1 259.0 %collective-permute-start.81 = (f32[1024,512]{1,0:T(8,128)}, f32[1024,512]{1,0:T(8,128)}, u32[]{:S(2)}, u32[]{:S(2)}) collective-permute-start(f32[1024,512]{1,0:T(8,128)} %fusion.112), channel_id=1, source_target_pairs={{0,4},{4,0},{1,5},{5,1},{2,6},{6,2},{3,7},{7,3}} | collective-permute-start | bytes 6291464 | tf_op jit(solution)/shard_map/ppermute | solution.py:189
  2821.2 131.1 %collective-permute-start.76 = (bf16[7168,384]{1,0:T(8,128)(2,1)}, bf16[7168,384]{1,0:T(8,128)(2,1)}, u32[]{:S(2)}, u32[]{:S(2)}) collective-permute-start(bf16[7168,384]{1,0:T(8,128)(2,1)} %collective-permute-done.72), channel_id=1, source_target_pairs={{0,1},{1,0},{2,3},{3,2},{4,5},{5,4},{6,7},{7,6}} | collective-permute-start | bytes 16515080 | tf_op jit(solution)/shard_map/ppermute | solution.py:186
  2834.8 144.1 %collective-permute-start.80 = (f32[1024,384]{1,0:T(8,128)}, f32[1024,384]{1,0:T(8,128)S(1)}, u32[]{:S(2)}, u32[]{:S(2)}) collective-permute-start(f32[1024,384]{1,0:T(8,128)} %fusion.117), channel_id=1, source_target_pairs={{0,4},{4,0},{1,5},{5,1},{2,6},{6,2},{3,7},{7,3}} | collective-permute-start | bytes 4718600 | tf_op jit(solution)/shard_map/ppermute | solution.py:189
  2835.2 115.5 %collective-permute-start.82 = (f32[1024,512]{1,0:T(8,128)}, f32[1024,512]{1,0:T(8,128)S(1)}, u32[]{:S(2)}, u32[]{:S(2)}) collective-permute-start(f32[1024,512]{1,0:T(8,128)} %fusion.113), channel_id=1, source_target_pairs={{0,4},{4,0},{1,5},{5,1},{2,6},{6,2},{3,7},{7,3}} | collective-permute-start | bytes 6291464 | tf_op jit(solution)/shard_map/ppermute | solution.py:189
  2859.9 90.3 %collective-permute-start.83 = (f32[1024,384]{1,0:T(8,128)S(1)}, f32[1024,384]{1,0:T(8,128)S(1)}, u32[]{:S(2)}, u32[]{:S(2)}) collective-permute-start(f32[1024,384]{1,0:T(8,128)S(1)} %fusion.121), channel_id=1, source_target_pairs={{0,4},{4,0},{1,5},{5,1},{2,6},{6,2},{3,7},{7,3}} | collective-permute-start | bytes 4718600 | tf_op jit(solution)/shard_map/ppermute | solution.py:189
  2952.3 125.4 %collective-permute-start.71 = (f32[1024,512]{1,0:T(8,128)}, f32[1024,512]{1,0:T(8,128)}, u32[]{:S(2)}, u32[]{:S(2)}) collective-permute-start(f32[1024,512]{1,0:T(8,128)} %fusion.91), channel_id=1, source_target_pairs={{0,4},{4,0},{1,5},{5,1},{2,6},{6,2},{3,7},{7,3}} | collective-permute-start | bytes 6291464 | tf_op jit(solution)/shard_map/ppermute | solution.py:189
  2977.2 132.7 %collective-permute-start.84 = (f32[1024,384]{1,0:T(8,128)}, f32[1024,384]{1,0:T(8,128)}, u32[]{:S(2)}, u32[]{:S(2)}) collective-permute-start(f32[1024,384]{1,0:T(8,128)} %fusion.122), channel_id=1, source_target_pairs={{0,4},{4,0},{1,5},{5,1},{2,6},{6,2},{3,7},{7,3}} | collective-permute-start | bytes 4718600 | tf_op jit(solution)/shard_map/ppermute | solution.py:189
  (126 other events, 2703.8 us)

commit v2 on v1

--- a/solution.py
+++ b/solution.py
@@ -158,13 +158,17 @@
 X_ORDER = (
     ('kv', 0, 0), ('q', 0, 0), ('o', 0, 0), ('g', 0, 0), ('g', 0, 1), ('g', 0, 2), ('g', 0, 3),
     ('d', 0, 0), ('d', 0, 1), ('kv', 1, 0), ('q', 1, 0), ('o', 1, 0), ('g', 1, 0), ('g', 1, 1), ('g', 1, 2), ('g', 1, 3),
-    ('d', 1, 0), ('d', 1, 1),
+    ('d', 1, 0), ('d', 1, 1), ('d', 1, 2),
 )
 
 
 FFN_CHUNKS = ((2048, 2048, 2048, 1024),) * 2
-FAR_FROM = (1, 1)
-DOWN_CHUNKS = ((512, 384), (512, 384))
+DOWN_CHUNKS = ((512, 384), (384, 256, 256))
+FFN_STEPS = (
+    ('w0', 'w1', 'f0', 'f1', 'f2', 'w2', 'f3', 'w3'),
+    ('w0', 'w1', 'f0', 'f1', 'f2', 'f3', 'w2', 'w3'),
+)
+DOWN_STEPS = (('o', 'f0', 'w0', 'f1', 'w1'), ('f0', 'o', 'f1', 'w0', 'w1', 'f2', 'w2'))
 
 
 def solution(mesh):
@@ -236,9 +240,9 @@
             for l in range(layers)
         ]
 
-        x_own = jnp.concatenate(local_cols(x_in.reshape(rows, feat), 1), axis=1)
         seg_far = send_y(seg_ids)
-        x_far = send_y(after(x_own, seg_far))
+        x_got = send_y(x_in)
+        x_own, x_far = ([p.astype(F32) for p in local_cols(a.reshape(rows, feat), 1)] for a in (x_in, x_got))
         first_half = jnp.where(half_id == 0, seg_ids, seg_far)
         second_half = jnp.where(half_id == 0, seg_far, seg_ids)
         positions = seg_positions(jnp.concatenate([first_half, second_half], axis=1))
@@ -256,19 +260,19 @@
         cos_own, sin_own, lo_own, hi_own, idx_own = tables(at_own)
         cos_far, sin_far, lo_far, hi_far, idx_far = tables(at_far)
 
-        resid = [x_own[:, j * depth:(j + 1) * depth].astype(F32) for j in range(4)]
+        resid = x_own
         shape3 = (micro_n, part_len, -1)
         k_cols = plans[0][0][0].shape[1] // 2
         q_cols = plans[0][1][0].shape[1]
         gate_q = ()
         out = jnp.zeros((rows, feat), F32)
-        y_next = send_y(after(plans[0][2][0], x_far))
+        y_next = send_y(after(plans[0][2][0], x_got))
         for l in range(layers):
             kv_w, q_w, o_w, gu_w, d_w = plans[l]
             gains = [g.astype(F32)[None, :] for g in local_cols(g_attn[l], 0)]
             h_own = norm_pieces(resid, gains)
             if l == 0:
-                h_far = norm_pieces([x_far[:, j * depth:(j + 1) * depth].astype(F32) for j in range(4)], gains)
+                h_far = norm_pieces(x_far, gains)
             else:
                 h_far = send_y(h_own)
             kv_w = spread(kv_w, *gate_q)
@@ -296,46 +300,64 @@
                 y_next = send_y(after(plans[l + 1][2][0], h_far))
             act_own = act_far = None
             starts = firsts[l]
-            last_c = len(gu_w) - 1
             gate = (o_own, h_own)[l]
             pieces = []
 
             def far_chunk(c, gate, act_far):
                 return ffn_chunk(after(h_far, gate), pieces[c], act_far, ffn_cols, starts[c])
 
-            done_far = 0
-            for c in range(len(gu_w)):
-                pieces.append(spread(gu_w[c], gate))
-                if c == last_c:
-                    while done_far <= c:
-                        gate = act_far = far_chunk(done_far, gate, act_far)
-                        done_far += 1
-                act_own = ffn_chunk(h_own, pieces[c], act_own, ffn_cols, starts[c])
-                gate = act_own
-                while FAR_FROM[l] <= c < last_c and done_far <= c:
-                    gate = act_far = far_chunk(done_far, gate, act_far)
-                    done_far += 1
-            sums = []
-            gate_d = ()
-            for js in ((0, 1), (2, 3)):
-                for c, parts_c in enumerate(d_w):
-                    w4 = parts_c if js == (0, 1) else spread(parts_c, *gate_d)
-                    at = sum(DOWN_CHUNKS[l][:c])
-                    fars = []
-                    for j in js:
-                        far_sum = jnp.dot(act_far, w4[j], preferred_element_type=F32)
-                        fars.append(far_sum)
-                        got = send_y(far_sum)
-                        mine = lax.optimization_barrier(jnp.dot(act_own, w4[j], preferred_element_type=F32))
-                        sums.append((j, at, mine, got))
-                    gate_d = (mine,) if js == (0, 1) else tuple(fars)
-            gate_q = (sums[-1][2],)
+            for step in FFN_STEPS[l]:
+                c = int(step[1])
+                if c == len(pieces):
+                    pieces.append(spread(gu_w[c], gate))
+                if step[0] == 'f':
+                    act_far = far_chunk(c, gate, act_far)
+                    gate = act_far
+                else:
+                    act_own = ffn_chunk(after(h_own, gate), pieces[c], act_own, ffn_cols, starts[c])
+                    gate = act_own
+            far_sums = {}
+            own_sums = {}
+            gates = (gate,)
+            own_gate = ()
+            cols_at = [sum(DOWN_CHUNKS[l][:c]) for c in range(len(d_w))]
+
+            def far_dots(js, c, w4):
+                got_here = []
+                for j in js:
+                    far_sum = jnp.dot(act_far, w4[j], preferred_element_type=F32)
+                    far_sums[j, c] = send_y(far_sum)
+                    got_here.append(far_sum)
+                return tuple(got_here)
+
+            def own_dots(js, c, w4):
+                for j in js:
+                    dot = jnp.dot(after(act_own, *own_gate), w4[j], preferred_element_type=F32)
+                    own_sums[j, c] = lax.optimization_barrier(dot)
+                return tuple(own_sums[j, c] for j in js)
+
+            for c, parts_c in enumerate(d_w):
+                far_dots((0, 1), c, parts_c)
+            spreads = {}
+            for step in DOWN_STEPS[l]:
+                if step == 'o':
+                    gates = sum((own_dots((0, 1), c, parts_c) for c, parts_c in enumerate(d_w)), ())
+                    continue
+                c = int(step[1])
+                if step[0] == 'f':
+                    spreads[c] = spread(d_w[c], *gates)
+                    own_gate = gates = far_dots((2, 3), c, spreads[c])
+                else:
+                    gates = own_dots((2, 3), c, spreads[c])
             new_resid = [[] for _ in range(4)]
-            for j, at, mine, got in sums:
-                total = resid[j][:, at:at + mine.shape[1]] + mine + after(got, *gate_q)
+            for j, c in far_sums:
+                width = DOWN_CHUNKS[l][c]
+                at = cols_at[c]
+                total = resid[j][:, at:at + width] + own_sums[j, c] + after(far_sums[j, c], *gates)
                 new_resid[j].append(total)
                 if l + 1 == layers:
                     out = lax.dynamic_update_slice_in_dim(out, total, (tok ^ j) * depth + at, 1)
+            gate_q = gates
             resid = [jnp.concatenate(new_resid[j], axis=1) for j in range(4)]
         return out.reshape(micro_n, part_len, feat)
 

time: 3120 us -> 3040 us (0.974)
  waiting for transfers between devices: 1480 us -> 1390 us
    ppermute x18 -> x19, waiting for transfers between devices: 616 us -> 534 us  [send_x(): return lax.ppermute(a, 'tok', over_x)]
    dot_general x32 -> x40, matrix products: 399 us -> 424 us  [the longest x20 231 us: far_dots(): far_sum = jnp.dot(act_far, w4[j], preferred_element_type=F32)]
    ppermute x27 -> x31, waiting for transfers between devices: 843 us -> 836 us  [send_y(): return lax.ppermute(a, 'mp', [(0, 1), (1, 0)])]
  transfers between devices with their start and end apart: 85 -> 92, of which waited for: 29 -> 31; matrix products, arithmetic and copies ran while one was open for 23% -> 25% of each run, Pallas kernels for 26% -> 27%
where the time goes in v2:
time: 3040 us
  waiting for transfers between devices  1390 us (46%)
  Pallas kernels  816 us (27%)
  matrix products  548 us (18%)
  other arithmetic  119 us (4%)
  local copies, waits for them, and re-layouts  106 us (3%)
  starting transfers between devices  55.5 us (2%)
    ppermute x31, waiting for transfers between devices, send_y(): return lax.ppermute(a, 'mp', [(0, 1), (1, 0)])  836 us
    pallas_call x16, Pallas kernels, ffn_chunk(): pl.pallas_call(ffn_kernel, grid=(steps,), in_specs=in_specs, out_specs=pl...  541 us
    ppermute x19, waiting for transfers between devices, send_x(): return lax.ppermute(a, 'tok', over_x)  534 us
    dot_general x20, matrix products, far_dots(): far_sum = jnp.dot(act_far, w4[j], preferred_element_type=F32)  231 us
    dot_general x20, matrix products, own_dots(): dot = jnp.dot(after(act_own, *own_gate), w4[j], preferred_element_type=F32)  193 us
    pallas_call x8, Pallas kernels, project(): pl.pallas_call(functools.partial(proj_kernel, rope_tiles, head_dim), grid...  179 us
    pallas_call x4, Pallas kernels, attention(): pl.pallas_call(functools.partial(attn_kernel, head_dim), grid=(micro_n, k...  96.9 us
    dot_general x8, matrix products, layer_pair(): jnp.dot(o_got, o_y[j], preferred_element_type=F32)  63.9 us
  transfers between devices with their start and end apart: 92, of which 31 were waited for; matrix products, arithmetic and copies ran while one was open for 25% of the time, Pallas kernels for 27%

profile of v2, /device:TPU:0, one launch (start us, length us, event | category | flops | bytes accessed | tf_op | source)
XLA Modules:
  0.0 3039.1 jit_solution(4255532153423620389)
XLA Ops:
  27.1 28.3 slice_bitcast_fusion.5
  75.8 96.9 %collective-permute-done.3 = s32[2,512]{1,0:T(2,128)S(1)} collective-permute-done((s32[2,512]{1,0:T(2,128)S(1)}, s32[2,512]{1,0:T(2,128)S(1)}, u32[]{:S(2)}, u32[]{:S(2)}) %collective-permute-start.3) | collective-permute-done | bytes 4128 | tf_op jit(solution)/shard_map/ppermute | solution.py:193
  202.9 21.7 shard_map.109
  224.7 39.8 %collective-permute-done.9 = bf16[2048,896]{1,0:T(8,128)(2,1)} collective-permute-done((bf16[2048,896]{1,0:T(8,128)(2,1)}, bf16[2048,896]{1,0:T(8,128)(2,1)}, u32[]{:S(2)}, u32[]{:S(2)}) %collective-permute-start.9) | collective-permute-done | bytes 3670048 | tf_op jit(solution)/shard_map/ppermute | solution.py:187
  266.0 23.2 shard_map.110
  289.2 22.9 shard_map.111
  312.1 21.8 shard_map.113
  334.8 24.1 shard_map.114
  359.4 61.4 %collective-permute-done.18.refs_2_.refs_6_ = bf16[896,4096]{1,0:T(8,128)(2,1)} collective-permute-done((bf16[896,4096]{1,0:T(8,128)(2,1)}, bf16[896,4096]{1,0:T(8,128)(2,1)}, u32[]{:S(2)}, u32[]{:S(2)}) %collective-permute-start.18) | collective-permute-done | bytes 7340064 | tf_op jit(solution)/shard_map/ppermute | solution.py:187
  423.3 24.3 shard_map.112
  469.9 60.7 %collective-permute-done.14 = bf16[2048,896]{1,0:T(8,128)(2,1)} collective-permute-done((bf16[2048,896]{1,0:T(8,128)(2,1)}, bf16[2048,896]{1,0:T(8,128)(2,1)}, u32[]{:S(2)}, u32[]{:S(2)}) %collective-permute-start.14) | collective-permute-done | bytes 3670048 | tf_op jit(solution)/shard_map/ppermute | solution.py:193
  577.0 37.9 %shard_map.115.refs_8_ = bf16[1024,7168]{1,0:T(8,128)(2,1)} custom-call(bf16[1024,3584]{1,0:T(8,128)(2,1)} %pad_maximum_fusion.2.h_ref, bf16[896,4096]{1,0:T(8,128)(2,1)} %pad_maximum_fusion.3.refs_0_.refs_4_, bf16[896,4096]{1,0:T(8,128)(2,1)} %collective-permute-done.17.refs_1_.refs_5_, bf16[896,4096]{1,0:T(8,128)(2,1)} %collective-permute-done.18.refs_2_.refs_6_, ...), custom_call_target="tpu_custom_call" | custom-call | flops 30064771072 | bytes 40894464 | tf_op jit(solution)/shard_map/pallas_call | solution.py:96
  614.9 83.8 %collective-permute-done.21.refs_2_.refs_6_ = bf16[896,4096]{1,0:T(8,128)(2,1)} collective-permute-done((bf16[896,4096]{1,0:T(8,128)(2,1)}, bf16[896,4096]{1,0:T(8,128)(2,1)}, u32[]{:S(2)}, u32[]{:S(2)}) %collective-permute-start.21) | collective-permute-done | bytes 7340064 | tf_op jit(solution)/shard_map/ppermute | solution.py:187
  710.7 37.7 %shard_map.116.refs_8_ = bf16[1024,7168]{1,0:T(8,128)(2,1)} custom-call(bf16[1024,3584]{1,0:T(8,128)(2,1)} %pad_maximum_fusion.2.h_ref, bf16[896,4096]{1,0:T(8,128)(2,1)} %pad_maximum_fusion.4.refs_0_.refs_4_, bf16[896,4096]{1,0:T(8,128)(2,1)} %collective-permute-done.20.refs_1_.refs_5_, ...), custom_call_target="tpu_custom_call", output_to_operand_aliasing={{}: (9, {})} | custom-call | flops 30064771072 | bytes 40894464 | tf_op jit(solution)/shard_map/pallas_call | solution.py:96
  748.5 111.0 %collective-permute-done.16.h_ref = bf16[1024,3584]{1,0:T(8,128)(2,1)} collective-permute-done((bf16[1024,3584]{1,0:T(8,128)(2,1)}, bf16[1024,3584]{1,0:T(8,128)(2,1)}, u32[]{:S(2)}, u32[]{:S(2)}) %collective-permute-start.16) | collective-permute-done | bytes 7340064 | tf_op jit(solution)/shard_map/ppermute | solution.py:193
  859.4 37.7 %shard_map.117.refs_8_ = bf16[1024,7168]{1,0:T(8,128)(2,1)} custom-call(bf16[1024,3584]{1,0:T(8,128)(2,1)} %collective-permute-done.16.h_ref, bf16[896,4096]{1,0:T(8,128)(2,1)} %pad_maximum_fusion.3.refs_0_.refs_4_, bf16[896,4096]{1,0:T(8,128)(2,1)} %collective-permute-done.17.refs_1_.refs_5_, bf16[896,4096]{1,0:T(8,128)(2,1)} %collective-permute-done.18.refs_2_.refs_6_, ...), custom_call_target="tpu_custom_call" | custom-call | flops 30064771072 | bytes 40894464 | tf_op jit(solution)/shard_map/pallas_call | solution.py:96
  897.1 37.7 %shard_map.118.refs_8_ = bf16[1024,7168]{1,0:T(8,128)(2,1)} custom-call(bf16[1024,3584]{1,0:T(8,128)(2,1)} %collective-permute-done.16.h_ref, bf16[896,4096]{1,0:T(8,128)(2,1)} %pad_maximum_fusion.4.refs_0_.refs_4_, bf16[896,4096]{1,0:T(8,128)(2,1)} %collective-permute-done.20.refs_1_.refs_5_, ...), custom_call_target="tpu_custom_call", output_to_operand_aliasing={{}: (9, {})} | custom-call | flops 30064771072 | bytes 40894464 | tf_op jit(solution)/shard_map/pallas_call | solution.py:96
  950.7 37.9 %shard_map.119.refs_8_ = bf16[1024,7168]{1,0:T(8,128)(2,1)} custom-call(bf16[1024,3584]{1,0:T(8,128)(2,1)} %collective-permute-done.16.h_ref, bf16[896,4096]{1,0:T(8,128)(2,1)} %pad_maximum_fusion.5.refs_0_.refs_4_, bf16[896,4096]{1,0:T(8,128)(2,1)} %collective-permute-done.23.refs_1_.refs_5_, ...), custom_call_target="tpu_custom_call", output_to_operand_aliasing={{}: (9, {})} | custom-call | flops 30064771072 | bytes 40894464 | tf_op jit(solution)/shard_map/pallas_call | solution.py:96
  988.6 37.8 %shard_map.120.refs_8_ = bf16[1024,7168]{1,0:T(8,128)(2,1)} custom-call(bf16[1024,3584]{1,0:T(8,128)(2,1)} %pad_maximum_fusion.2.h_ref, bf16[896,4096]{1,0:T(8,128)(2,1)} %pad_maximum_fusion.5.refs_0_.refs_4_, bf16[896,4096]{1,0:T(8,128)(2,1)} %collective-permute-done.23.refs_1_.refs_5_, ...), custom_call_target="tpu_custom_call", output_to_operand_aliasing={{}: (9, {})} | custom-call | flops 30064771072 | bytes 40894464 | tf_op jit(solution)/shard_map/pallas_call | solution.py:96
  1037.9 21.7 shard_map.121
  1059.5 21.7 shard_map.122
  1081.3 14.1 fusion.110
  1128.6 68.2 %collective-permute-done.31 = bf16[7168,512]{1,0:T(8,128)(2,1)} collective-permute-done((bf16[7168,512]{1,0:T(8,128)(2,1)}, bf16[7168,512]{1,0:T(8,128)(2,1)}, u32[]{:S(2)}, u32[]{:S(2)}) %collective-permute-start.31) | collective-permute-done | bytes 7340064 | tf_op jit(solution)/shard_map/ppermute | solution.py:187
  1206.9 14.5 fusion.111
  1221.4 14.0 fusion.119
  1237.5 14.2 fusion.112
  1273.8 44.2 %collective-permute-done.30 = bf16[7168,384]{1,0:T(8,128)(2,1)} collective-permute-done((bf16[7168,384]{1,0:T(8,128)(2,1)S(1)}, bf16[7168,384]{1,0:T(8,128)(2,1)}, u32[]{:S(2)}, u32[]{:S(2)}) %collective-permute-start.30) | collective-permute-done | bytes 5505056 | tf_op jit(solution)/shard_map/ppermute | solution.py:187
  1330.5 14.1 fusion.101
  1346.4 13.5 fusion.97
  1359.8 13.4 fusion.115
  1373.6 13.7 fusion.116
  1414.3 32.0 %collective-permute-done.36 = f32[1024,384]{1,0:T(8,128)} collective-permute-done((f32[1024,384]{1,0:T(8,128)}, f32[1024,384]{1,0:T(8,128)}, u32[]{:S(2)}, u32[]{:S(2)}) %collective-permute-start.36) | collective-permute-done | bytes 1572896 | tf_op jit(solution)/shard_map/ppermute | solution.py:193
  1447.8 32.2 %collective-permute-done.40 = f32[1024,384]{1,0:T(8,128)} collective-permute-done((f32[1024,384]{1,0:T(8,128)}, f32[1024,384]{1,0:T(8,128)}, u32[]{:S(2)}, u32[]{:S(2)}) %collective-permute-start.40) | collective-permute-done | bytes 1572896 | tf_op jit(solution)/shard_map/ppermute | solution.py:193
  1486.3 38.6 %collective-permute-done.41 = f32[1024,512]{1,0:T(8,128)S(1)} collective-permute-done((f32[1024,512]{1,0:T(8,128)}, f32[1024,512]{1,0:T(8,128)S(1)}, u32[]{:S(2)}, u32[]{:S(2)}) %collective-permute-start.41) | collective-permute-done | bytes 2097184 | tf_op jit(solution)/shard_map/ppermute | solution.py:193
  1531.1 26.9 collective-permute-done.42
  1582.2 21.7 shard_map.123
  1603.9 47.2 %collective-permute-done.51 = bf16[2048,896]{1,0:T(8,128)(2,1)} collective-permute-done((bf16[2048,896]{1,0:T(8,128)(2,1)}, bf16[2048,896]{1,0:T(8,128)(2,1)}, u32[]{:S(2)}, u32[]{:S(2)}) %collective-permute-start.51) | collective-permute-done | bytes 3670048 | tf_op jit(solution)/shard_map/ppermute | solution.py:187
  1651.3 22.6 shard_map.124
  1673.9 51.9 %collective-permute-done.49.h_ref = bf16[1024,3584]{1,0:T(8,128)(2,1)} collective-permute-done((bf16[1024,3584]{1,0:T(8,128)(2,1)}, bf16[1024,3584]{1,0:T(8,128)(2,1)}, u32[]{:S(2)}, u32[]{:S(2)}) %collective-permute-start.49) | collective-permute-done | bytes 7340064 | tf_op jit(solution)/shard_map/ppermute | solution.py:193
  1725.9 22.1 shard_map.127
  1747.9 22.7 shard_map.125
  1770.7 24.2 shard_map.128
  1796.9 24.3 shard_map.126
  1845.8 126.1 %collective-permute-done.56 = bf16[2048,896]{1,0:T(8,128)(2,1)} collective-permute-done((bf16[2048,896]{1,0:T(8,128)(2,1)}, bf16[2048,896]{1,0:T(8,128)(2,1)}, u32[]{:S(2)}, u32[]{:S(2)}) %collective-permute-start.56) | collective-permute-done | bytes 3670048 | tf_op jit(solution)/shard_map/ppermute | solution.py:193
  2031.3 37.7 %shard_map.129.refs_8_ = bf16[1024,7168]{1,0:T(8,128)(2,1)} custom-call(bf16[1024,3584]{1,0:T(8,128)(2,1)} %pad_maximum_fusion.7.h_ref, bf16[896,4096]{1,0:T(8,128)(2,1)} %pad_maximum_fusion.8.refs_0_.refs_4_, bf16[896,4096]{1,0:T(8,128)(2,1)} %collective-permute-done.59.refs_1_.refs_5_, bf16[896,4096]{1,0:T(8,128)(2,1)} %collective-permute-done.60.refs_2_.refs_6_, ...), custom_call_target="tpu_custom_call" | custom-call | flops 30064771072 | bytes 40894464 | tf_op jit(solution)/shard_map/pallas_call | solution.py:96
  2069.0 117.0 %collective-permute-done.63.refs_2_.refs_6_ = bf16[896,4096]{1,0:T(8,128)(2,1)} collective-permute-done((bf16[896,4096]{1,0:T(8,128)(2,1)}, bf16[896,4096]{1,0:T(8,128)(2,1)}, u32[]{:S(2)}, u32[]{:S(2)}) %collective-permute-start.63) | collective-permute-done | bytes 7340064 | tf_op jit(solution)/shard_map/ppermute | solution.py:187
  2198.0 37.7 %shard_map.130.refs_8_ = bf16[1024,7168]{1,0:T(8,128)(2,1)} custom-call(bf16[1024,3584]{1,0:T(8,128)(2,1)} %pad_maximum_fusion.7.h_ref, bf16[896,4096]{1,0:T(8,128)(2,1)} %pad_maximum_fusion.9.refs_0_.refs_4_, bf16[896,4096]{1,0:T(8,128)(2,1)} %collective-permute-done.62.refs_1_.refs_5_, ...), custom_call_target="tpu_custom_call", output_to_operand_aliasing={{}: (9, {})} | custom-call | flops 30064771072 | bytes 40894464 | tf_op jit(solution)/shard_map/pallas_call | solution.py:96
  2235.7 111.0 %collective-permute-done.58.h_ref = bf16[1024,3584]{1,0:T(8,128)(2,1)} collective-permute-done((bf16[1024,3584]{1,0:T(8,128)(2,1)}, bf16[1024,3584]{1,0:T(8,128)(2,1)}, u32[]{:S(2)}, u32[]{:S(2)}) %collective-permute-start.58) | collective-permute-done | bytes 7340064 | tf_op jit(solution)/shard_map/ppermute | solution.py:193
  2346.7 37.7 %shard_map.131.refs_8_ = bf16[1024,7168]{1,0:T(8,128)(2,1)} custom-call(bf16[1024,3584]{1,0:T(8,128)(2,1)} %collective-permute-done.58.h_ref, bf16[896,4096]{1,0:T(8,128)(2,1)} %pad_maximum_fusion.8.refs_0_.refs_4_, bf16[896,4096]{1,0:T(8,128)(2,1)} %collective-permute-done.59.refs_1_.refs_5_, bf16[896,4096]{1,0:T(8,128)(2,1)} %collective-permute-done.60.refs_2_.refs_6_, ...), custom_call_target="tpu_custom_call" | custom-call | flops 30064771072 | bytes 40894464 | tf_op jit(solution)/shard_map/pallas_call | solution.py:96
  2384.4 37.8 %shard_map.132.refs_8_ = bf16[1024,7168]{1,0:T(8,128)(2,1)} custom-call(bf16[1024,3584]{1,0:T(8,128)(2,1)} %collective-permute-done.58.h_ref, bf16[896,4096]{1,0:T(8,128)(2,1)} %pad_maximum_fusion.9.refs_0_.refs_4_, bf16[896,4096]{1,0:T(8,128)(2,1)} %collective-permute-done.62.refs_1_.refs_5_, ...), custom_call_target="tpu_custom_call", output_to_operand_aliasing={{}: (9, {})} | custom-call | flops 30064771072 | bytes 40894464 | tf_op jit(solution)/shard_map/pallas_call | solution.py:96
  2434.3 37.9 %shard_map.133.refs_8_ = bf16[1024,7168]{1,0:T(8,128)(2,1)} custom-call(bf16[1024,3584]{1,0:T(8,128)(2,1)} %collective-permute-done.58.h_ref, bf16[896,4096]{1,0:T(8,128)(2,1)} %pad_maximum_fusion.10.refs_0_.refs_4_, bf16[896,4096]{1,0:T(8,128)(2,1)} %collective-permute-done.65.refs_1_.refs_5_, ...), custom_call_target="tpu_custom_call", output_to_operand_aliasing={{}: (9, {})} | custom-call | flops 30064771072 | bytes 40894464 | tf_op jit(solution)/shard_map/pallas_call | solution.py:96
  2472.2 34.4 %collective-permute-done.69.refs_2_.refs_6_ = bf16[896,2048]{1,0:T(8,128)(2,1)} collective-permute-done((bf16[896,2048]{1,0:T(8,128)(2,1)}, bf16[896,2048]{1,0:T(8,128)(2,1)}, u32[]{:S(2)}, u32[]{:S(2)}) %collective-permute-start.69) | collective-permute-done | bytes 3670048 | tf_op jit(solution)/shard_map/ppermute | solution.py:187
  2515.7 21.7 shard_map.134
  2537.4 37.8 %shard_map.135.refs_8_ = bf16[1024,7168]{1,0:T(8,128)(2,1)} custom-call(bf16[1024,3584]{1,0:T(8,128)(2,1)} %pad_maximum_fusion.7.h_ref, bf16[896,4096]{1,0:T(8,128)(2,1)} %pad_maximum_fusion.10.refs_0_.refs_4_, bf16[896,4096]{1,0:T(8,128)(2,1)} %collective-permute-done.65.refs_1_.refs_5_, ...), custom_call_target="tpu_custom_call", output_to_operand_aliasing={{}: (9, {})} | custom-call | flops 30064771072 | bytes 40894464 | tf_op jit(solution)/shard_map/pallas_call | solution.py:96
  2575.2 22.1 shard_map.136
  2597.3 31.2 %collective-permute-done.71 = bf16[7168,384]{1,0:T(8,128)(2,1)} collective-permute-done((bf16[7168,384]{1,0:T(8,128)(2,1)}, bf16[7168,384]{1,0:T(8,128)(2,1)}, u32[]{:S(2)}, u32[]{:S(2)}) %collective-permute-start.71) | collective-permute-done | bytes 5505056 | tf_op jit(solution)/shard_map/ppermute | solution.py:187
  2705.5 13.3 fusion.123
  2853.2 21.9 collective-permute-done.87
  2881.5 15.9 collective-permute-done.84
  2897.9 22.1 collective-permute-done.83
  2920.4 21.9 collective-permute-done.82
  2961.6 25.7 collective-permute-done.90
  2987.3 22.6 collective-permute-done.89
  3013.1 18.5 collective-permute-done.91
  (538 shorter events, 704.4 us)
Async XLA Ops:
  8.6 165.2 %collective-permute-start.1 = (bf16[896,2048]{1,0:T(8,128)(2,1)}, bf16[896,2048]{1,0:T(8,128)(2,1)}, u32[]{:S(2)}, u32[]{:S(2)}) collective-permute-start(bf16[896,2048]{1,0:T(8,128)(2,1)} %bitcast.42.refs_0_), channel_id=1, source_target_pairs={{0,2},{1,3},{2,0},{3,1},{4,6},{5,7},{6,4},{7,5}} | collective-permute-start | bytes 11010056 | tf_op jit(solution)/shard_map/ppermute | solution.py:187
  11.9 183.2 %collective-permute-start = (bf16[896,2048]{1,0:T(8,128)(2,1)}, bf16[896,2048]{1,0:T(8,128)(2,1)}, u32[]{:S(2)}, u32[]{:S(2)}) collective-permute-start(bf16[896,2048]{1,0:T(8,128)(2,1)} %bitcast.42.refs_0_), channel_id=1, source_target_pairs={{0,1},{1,0},{2,3},{3,2},{4,5},{5,4},{6,7},{7,6}} | collective-permute-start | bytes 11010056 | tf_op jit(solution)/shard_map/ppermute | solution.py:190
  11.9 170.3 %collective-permute-start.7 = (bf16[2,512,3584]{2,1,0:T(8,128)(2,1)}, bf16[2,512,3584]{2,1,0:T(8,128)(2,1)}, u32[]{:S(2)}, u32[]{:S(2)}) collective-permute-start(bf16[2,512,3584]{2,1,0:T(8,128)(2,1)} %param.11), channel_id=1, source_target_pairs={{0,4},{4,0},{1,5},{5,1},{2,6},{6,2},{3,7},{7,3}} | collective-permute-start | bytes 22020104 | tf_op jit(solution)/shard_map/ppermute | solution.py:193
  13.5 159.2 %collective-permute-start.3 = (s32[2,512]{1,0:T(2,128)S(1)}, s32[2,512]{1,0:T(2,128)S(1)}, u32[]{:S(2)}, u32[]{:S(2)}) collective-permute-start(s32[2,512]{1,0:T(2,128)S(1)} %copy-done.79), channel_id=1, source_target_pairs={{0,4},{4,0},{1,5},{5,1},{2,6},{6,2},{3,7},{7,3}} | collective-permute-start | bytes 12296 | tf_op jit(solution)/shard_map/ppermute | solution.py:193
  23.5 158.4 %collective-permute-start.5 = (bf16[896,2048]{1,0:T(8,128)(2,1)}, bf16[896,2048]{1,0:T(8,128)(2,1)}, u32[]{:S(2)}, u32[]{:S(2)}) collective-permute-start(bf16[896,2048]{1,0:T(8,128)(2,1)} %constant_dynamic-update-slice_fusion.refs_0_), channel_id=1, source_target_pairs={{0,2},{1,3},{2,0},{3,1},{4,6},{5,7},{6,4},{7,5}} | collective-permute-start | bytes 11010056 | tf_op jit(solution)/shard_map/ppermute | solution.py:187
  172.7 91.8 %collective-permute-start.4 = (bf16[896,2048]{1,0:T(8,128)(2,1)}, bf16[896,2048]{1,0:T(8,128)(2,1)}, u32[]{:S(2)}, u32[]{:S(2)}) collective-permute-start(bf16[896,2048]{1,0:T(8,128)(2,1)} %constant_dynamic-update-slice_fusion.refs_0_), channel_id=1, source_target_pairs={{0,1},{1,0},{2,3},{3,2},{4,5},{5,4},{6,7},{7,6}} | collective-permute-start | bytes 11010056 | tf_op jit(solution)/shard_map/ppermute | solution.py:190
  181.9 82.5 %collective-permute-start.9 = (bf16[2048,896]{1,0:T(8,128)(2,1)}, bf16[2048,896]{1,0:T(8,128)(2,1)}, u32[]{:S(2)}, u32[]{:S(2)}) collective-permute-start(bf16[2048,896]{1,0:T(8,128)(2,1)} %bitcast.234), channel_id=1, source_target_pairs={{0,2},{1,3},{2,0},{3,1},{4,6},{5,7},{6,4},{7,5}} | collective-permute-start | bytes 11010056 | tf_op jit(solution)/shard_map/ppermute | solution.py:187
  182.2 83.7 %collective-permute-start.6 = (bf16[896,2048]{1,0:T(8,128)(2,1)}, bf16[896,2048]{1,0:T(8,128)(2,1)}, u32[]{:S(2)}, u32[]{:S(2)}) collective-permute-start(bf16[896,2048]{1,0:T(8,128)(2,1)} %collective-permute-done.5.refs_2_), channel_id=1, source_target_pairs={{0,1},{1,0},{2,3},{3,2},{4,5},{5,4},{6,7},{7,6}} | collective-permute-start | bytes 11010056 | tf_op jit(solution)/shard_map/ppermute | solution.py:190
  195.1 225.7 %collective-permute-start.18 = (bf16[896,4096]{1,0:T(8,128)(2,1)}, bf16[896,4096]{1,0:T(8,128)(2,1)}, u32[]{:S(2)}, u32[]{:S(2)}) collective-permute-start(bf16[896,4096]{1,0:T(8,128)(2,1)} %pad_maximum_fusion.3.refs_0_.refs_4_), channel_id=1, source_target_pairs={{0,2},{1,3},{2,0},{3,1},{4,6},{5,7},{6,4},{7,5}} | collective-permute-start | bytes 22020104 | tf_op jit(solution)/shard_map/ppermute | solution.py:187
  202.7 259.4 %collective-permute-start.8 = (bf16[2048,896]{1,0:T(8,128)(2,1)S(1)}, bf16[2048,896]{1,0:T(8,128)(2,1)}, u32[]{:S(2)}, u32[]{:S(2)}) collective-permute-start(bf16[2048,896]{1,0:T(8,128)(2,1)S(1)} %bitcast.235), channel_id=1, source_target_pairs={{0,1},{1,0},{2,3},{3,2},{4,5},{5,4},{6,7},{7,6}} | collective-permute-start | bytes 11010056 | tf_op jit(solution)/shard_map/ppermute | solution.py:190
  264.5 197.7 %collective-permute-start.10 = (bf16[2048,896]{1,0:T(8,128)(2,1)}, bf16[2048,896]{1,0:T(8,128)(2,1)}, u32[]{:S(2)}, u32[]{:S(2)}) collective-permute-start(bf16[2048,896]{1,0:T(8,128)(2,1)} %collective-permute-done.9), channel_id=1, source_target_pairs={{0,1},{1,0},{2,3},{3,2},{4,5},{5,4},{6,7},{7,6}} | collective-permute-start | bytes 11010056 | tf_op jit(solution)/shard_map/ppermute | solution.py:190
  264.5 198.2 %collective-permute-start.12 = (bf16[2048,896]{1,0:T(8,128)(2,1)S(1)}, bf16[2048,896]{1,0:T(8,128)(2,1)}, u32[]{:S(2)}, u32[]{:S(2)}) collective-permute-start(bf16[2048,896]{1,0:T(8,128)(2,1)S(1)} %bitcast.236), channel_id=1, source_target_pairs={{0,4},{4,0},{1,5},{5,1},{2,6},{6,2},{3,7},{7,3}} | collective-permute-start | bytes 11010056 | tf_op jit(solution)/shard_map/ppermute | solution.py:193
  358.9 179.0 %collective-permute-start.11 = (bf16[2,512,2048]{2,1,0:T(8,128)(2,1)}, bf16[2,512,2048]{2,1,0:T(8,128)(2,1)}, u32[]{:S(2)}, u32[]{:S(2)}) collective-permute-start(bf16[2,512,2048]{2,1,0:T(8,128)(2,1)} %shard_map.114), channel_id=1, source_target_pairs={{0,4},{4,0},{1,5},{5,1},{2,6},{6,2},{3,7},{7,3}} | collective-permute-start | bytes 12582920 | tf_op jit(solution)/shard_map/ppermute | solution.py:193
  420.8 109.8 %collective-permute-start.14 = (bf16[2048,896]{1,0:T(8,128)(2,1)}, bf16[2048,896]{1,0:T(8,128)(2,1)}, u32[]{:S(2)}, u32[]{:S(2)}) collective-permute-start(bf16[2048,896]{1,0:T(8,128)(2,1)} %collective-permute-done.9), channel_id=1, source_target_pairs={{0,4},{4,0},{1,5},{5,1},{2,6},{6,2},{3,7},{7,3}} | collective-permute-start | bytes 11010056 | tf_op jit(solution)/shard_map/ppermute | solution.py:193
  462.1 114.9 %collective-permute-start.17 = (bf16[896,4096]{1,0:T(8,128)(2,1)}, bf16[896,4096]{1,0:T(8,128)(2,1)}, u32[]{:S(2)}, u32[]{:S(2)}) collective-permute-start(bf16[896,4096]{1,0:T(8,128)(2,1)} %pad_maximum_fusion.3.refs_0_.refs_4_), channel_id=1, source_target_pairs={{0,1},{1,0},{2,3},{3,2},{4,5},{5,4},{6,7},{7,6}} | collective-permute-start | bytes 22020104 | tf_op jit(solution)/shard_map/ppermute | solution.py:190
  462.2 114.8 %collective-permute-start.19 = (bf16[896,4096]{1,0:T(8,128)(2,1)}, bf16[896,4096]{1,0:T(8,128)(2,1)}, u32[]{:S(2)}, u32[]{:S(2)}) collective-permute-start(bf16[896,4096]{1,0:T(8,128)(2,1)} %collective-permute-done.18.refs_2_.refs_6_), channel_id=1, source_target_pairs={{0,1},{1,0},{2,3},{3,2},{4,5},{5,4},{6,7},{7,6}} | collective-permute-start | bytes 22020104 | tf_op jit(solution)/shard_map/ppermute | solution.py:190
  462.7 92.4 %collective-permute-start.13 = (bf16[2048,896]{1,0:T(8,128)(2,1)}, bf16[2048,896]{1,0:T(8,128)(2,1)S(1)}, u32[]{:S(2)}, u32[]{:S(2)}) collective-permute-start(bf16[2048,896]{1,0:T(8,128)(2,1)} %collective-permute-done.12), channel_id=1, source_target_pairs={{0,1},{1,0},{2,3},{3,2},{4,5},{5,4},{6,7},{7,6}} | collective-permute-start | bytes 11010056 | tf_op jit(solution)/shard_map/ppermute | solution.py:190
  538.0 160.7 %collective-permute-start.21 = (bf16[896,4096]{1,0:T(8,128)(2,1)}, bf16[896,4096]{1,0:T(8,128)(2,1)}, u32[]{:S(2)}, u32[]{:S(2)}) collective-permute-start(bf16[896,4096]{1,0:T(8,128)(2,1)} %pad_maximum_fusion.4.refs_0_.refs_4_), channel_id=1, source_target_pairs={{0,2},{1,3},{2,0},{3,1},{4,6},{5,7},{6,4},{7,5}} | collective-permute-start | bytes 22020104 | tf_op jit(solution)/shard_map/ppermute | solution.py:187
  555.1 150.5 %collective-permute-start.20 = (bf16[896,4096]{1,0:T(8,128)(2,1)}, bf16[896,4096]{1,0:T(8,128)(2,1)}, u32[]{:S(2)}, u32[]{:S(2)}) collective-permute-start(bf16[896,4096]{1,0:T(8,128)(2,1)} %pad_maximum_fusion.4.refs_0_.refs_4_), channel_id=1, source_target_pairs={{0,1},{1,0},{2,3},{3,2},{4,5},{5,4},{6,7},{7,6}} | collective-permute-start | bytes 22020104 | tf_op jit(solution)/shard_map/ppermute | solution.py:190
  698.7 160.7 %collective-permute-start.16 = (bf16[1024,3584]{1,0:T(8,128)(2,1)}, bf16[1024,3584]{1,0:T(8,128)(2,1)}, u32[]{:S(2)}, u32[]{:S(2)}) collective-permute-start(bf16[1024,3584]{1,0:T(8,128)(2,1)} %pad_maximum_fusion.2.h_ref), channel_id=1, source_target_pairs={{0,4},{4,0},{1,5},{5,1},{2,6},{6,2},{3,7},{7,3}} | collective-permute-start | bytes 22020104 | tf_op jit(solution)/shard_map/ppermute | solution.py:193
  705.2 229.6 %collective-permute-start.24 = (bf16[896,4096]{1,0:T(8,128)(2,1)}, bf16[896,4096]{1,0:T(8,128)(2,1)}, u32[]{:S(2)}, u32[]{:S(2)}) collective-permute-start(bf16[896,4096]{1,0:T(8,128)(2,1)} %pad_maximum_fusion.5.refs_0_.refs_4_), channel_id=1, source_target_pairs={{0,2},{1,3},{2,0},{3,1},{4,6},{5,7},{6,4},{7,5}} | collective-permute-start | bytes 22020104 | tf_op jit(solution)/shard_map/ppermute | solution.py:187
  705.5 245.2 %collective-permute-start.23 = (bf16[896,4096]{1,0:T(8,128)(2,1)}, bf16[896,4096]{1,0:T(8,128)(2,1)}, u32[]{:S(2)}, u32[]{:S(2)}) collective-permute-start(bf16[896,4096]{1,0:T(8,128)(2,1)} %pad_maximum_fusion.5.refs_0_.refs_4_), channel_id=1, source_target_pairs={{0,1},{1,0},{2,3},{3,2},{4,5},{5,4},{6,7},{7,6}} | collective-permute-start | bytes 22020104 | tf_op jit(solution)/shard_map/ppermute | solution.py:190
  943.1 83.3 %collective-permute-start.27 = (bf16[896,2048]{1,0:T(8,128)(2,1)}, bf16[896,2048]{1,0:T(8,128)(2,1)}, u32[]{:S(2)}, u32[]{:S(2)}) collective-permute-start(bf16[896,2048]{1,0:T(8,128)(2,1)} %pad_maximum_fusion.11.refs_0_.refs_4_), channel_id=1, source_target_pairs={{0,2},{1,3},{2,0},{3,1},{4,6},{5,7},{6,4},{7,5}} | collective-permute-start | bytes 11010056 | tf_op jit(solution)/shard_map/ppermute | solution.py:187
  943.6 94.2 %collective-permute-start.26 = (bf16[896,2048]{1,0:T(8,128)(2,1)}, bf16[896,2048]{1,0:T(8,128)(2,1)}, u32[]{:S(2)}, u32[]{:S(2)}) collective-permute-start(bf16[896,2048]{1,0:T(8,128)(2,1)} %pad_maximum_fusion.11.refs_0_.refs_4_), channel_id=1, source_target_pairs={{0,1},{1,0},{2,3},{3,2},{4,5},{5,4},{6,7},{7,6}} | collective-permute-start | bytes 11010056 | tf_op jit(solution)/shard_map/ppermute | solution.py:190
  950.4 145.0 %collective-permute-start.32 = (bf16[7168,512]{1,0:T(8,128)(2,1)}, bf16[7168,512]{1,0:T(8,128)(2,1)}, u32[]{:S(2)}, u32[]{:S(2)}) collective-permute-start(bf16[7168,512]{1,0:T(8,128)(2,1)} %slice_bitcast_fusion), channel_id=1, source_target_pairs={{0,1},{1,0},{2,3},{3,2},{4,5},{5,4},{6,7},{7,6}} | collective-permute-start | bytes 22020104 | tf_op jit(solution)/shard_map/ppermute | solution.py:190
  1036.4 160.4 %collective-permute-start.31 = (bf16[7168,512]{1,0:T(8,128)(2,1)}, bf16[7168,512]{1,0:T(8,128)(2,1)}, u32[]{:S(2)}, u32[]{:S(2)}) collective-permute-start(bf16[7168,512]{1,0:T(8,128)(2,1)} %slice_bitcast_fusion), channel_id=1, source_target_pairs={{0,2},{1,3},{2,0},{3,1},{4,6},{5,7},{6,4},{7,5}} | collective-permute-start | bytes 22020104 | tf_op jit(solution)/shard_map/ppermute | solution.py:187
  1196.8 121.2 %collective-permute-start.30 = (bf16[7168,384]{1,0:T(8,128)(2,1)S(1)}, bf16[7168,384]{1,0:T(8,128)(2,1)}, u32[]{:S(2)}, u32[]{:S(2)}) collective-permute-start(bf16[7168,384]{1,0:T(8,128)(2,1)S(1)} %bitcast.233), channel_id=1, source_target_pairs={{0,2},{1,3},{2,0},{3,1},{4,6},{5,7},{6,4},{7,5}} | collective-permute-start | bytes 16515080 | tf_op jit(solution)/shard_map/ppermute | solution.py:187
  1235.4 164.4 %collective-permute-start.37 = (f32[1024,512]{1,0:T(8,128)}, f32[1024,512]{1,0:T(8,128)}, u32[]{:S(2)}, u32[]{:S(2)}) collective-permute-start(f32[1024,512]{1,0:T(8,128)} %fusion.119), channel_id=1, source_target_pairs={{0,4},{4,0},{1,5},{5,1},{2,6},{6,2},{3,7},{7,3}} | collective-permute-start | bytes 6291464 | tf_op jit(solution)/shard_map/ppermute | solution.py:193
  1235.9 210.3 %collective-permute-start.39 = (f32[1024,512]{1,0:T(8,128)}, f32[1024,512]{1,0:T(8,128)S(1)}, u32[]{:S(2)}, u32[]{:S(2)}) collective-permute-start(f32[1024,512]{1,0:T(8,128)} %fusion.111), channel_id=1, source_target_pairs={{0,4},{4,0},{1,5},{5,1},{2,6},{6,2},{3,7},{7,3}} | collective-permute-start | bytes 6291464 | tf_op jit(solution)/shard_map/ppermute | solution.py:193
  1387.3 92.7 %collective-permute-start.40 = (f32[1024,384]{1,0:T(8,128)}, f32[1024,384]{1,0:T(8,128)}, u32[]{:S(2)}, u32[]{:S(2)}) collective-permute-start(f32[1024,384]{1,0:T(8,128)} %fusion.115), channel_id=1, source_target_pairs={{0,4},{4,0},{1,5},{5,1},{2,6},{6,2},{3,7},{7,3}} | collective-permute-start | bytes 4718600 | tf_op jit(solution)/shard_map/ppermute | solution.py:193
  1399.8 125.0 %collective-permute-start.41 = (f32[1024,512]{1,0:T(8,128)}, f32[1024,512]{1,0:T(8,128)S(1)}, u32[]{:S(2)}, u32[]{:S(2)}) collective-permute-start(f32[1024,512]{1,0:T(8,128)} %fusion.112), channel_id=1, source_target_pairs={{0,4},{4,0},{1,5},{5,1},{2,6},{6,2},{3,7},{7,3}} | collective-permute-start | bytes 6291464 | tf_op jit(solution)/shard_map/ppermute | solution.py:193
  1412.8 152.2 %collective-permute-start.44 = (bf16[896,2048]{1,0:T(8,128)(2,1)}, bf16[896,2048]{1,0:T(8,128)(2,1)}, u32[]{:S(2)}, u32[]{:S(2)}) collective-permute-start(bf16[896,2048]{1,0:T(8,128)(2,1)} %bitcast.59.refs_0_), channel_id=1, source_target_pairs={{0,2},{1,3},{2,0},{3,1},{4,6},{5,7},{6,4},{7,5}} | collective-permute-start | bytes 11010056 | tf_op jit(solution)/shard_map/ppermute | solution.py:187
  1446.3 127.7 %collective-permute-start.43 = (bf16[896,2048]{1,0:T(8,128)(2,1)}, bf16[896,2048]{1,0:T(8,128)(2,1)}, u32[]{:S(2)}, u32[]{:S(2)}) collective-permute-start(bf16[896,2048]{1,0:T(8,128)(2,1)} %bitcast.59.refs_0_), channel_id=1, source_target_pairs={{0,1},{1,0},{2,3},{3,2},{4,5},{5,4},{6,7},{7,6}} | collective-permute-start | bytes 11010056 | tf_op jit(solution)/shard_map/ppermute | solution.py:190
  1446.3 127.7 %collective-permute-start.47 = (bf16[896,2048]{1,0:T(8,128)(2,1)}, bf16[896,2048]{1,0:T(8,128)(2,1)}, u32[]{:S(2)}, u32[]{:S(2)}) collective-permute-start(bf16[896,2048]{1,0:T(8,128)(2,1)} %constant_dynamic-update-slice_fusion.2.refs_0_), channel_id=1, source_target_pairs={{0,2},{1,3},{2,0},{3,1},{4,6},{5,7},{6,4},{7,5}} | collective-permute-start | bytes 11010056 | tf_op jit(solution)/shard_map/ppermute | solution.py:187
  1480.0 78.1 %collective-permute-start.42 = (f32[1024,384]{1,0:T(8,128)}, f32[1024,384]{1,0:T(8,128)S(1)}, u32[]{:S(2)}, u32[]{:S(2)}) collective-permute-start(f32[1024,384]{1,0:T(8,128)} %fusion.116), channel_id=1, source_target_pairs={{0,4},{4,0},{1,5},{5,1},{2,6},{6,2},{3,7},{7,3}} | collective-permute-start | bytes 4718600 | tf_op jit(solution)/shard_map/ppermute | solution.py:193
  1564.7 161.2 %collective-permute-start.49 = (bf16[1024,3584]{1,0:T(8,128)(2,1)}, bf16[1024,3584]{1,0:T(8,128)(2,1)}, u32[]{:S(2)}, u32[]{:S(2)}) collective-permute-start(bf16[1024,3584]{1,0:T(8,128)(2,1)} %pad_maximum_fusion.6.h_ref), channel_id=1, source_target_pairs={{0,4},{4,0},{1,5},{5,1},{2,6},{6,2},{3,7},{7,3}} | collective-permute-start | bytes 22020104 | tf_op jit(solution)/shard_map/ppermute | solution.py:193
  1565.0 86.1 %collective-permute-start.51 = (bf16[2048,896]{1,0:T(8,128)(2,1)}, bf16[2048,896]{1,0:T(8,128)(2,1)}, u32[]{:S(2)}, u32[]{:S(2)}) collective-permute-start(bf16[2048,896]{1,0:T(8,128)(2,1)} %bitcast.25), channel_id=1, source_target_pairs={{0,2},{1,3},{2,0},{3,1},{4,6},{5,7},{6,4},{7,5}} | collective-permute-start | bytes 11010056 | tf_op jit(solution)/shard_map/ppermute | solution.py:187
  1582.2 263.0 %collective-permute-start.50 = (bf16[2048,896]{1,0:T(8,128)(2,1)}, bf16[2048,896]{1,0:T(8,128)(2,1)}, u32[]{:S(2)}, u32[]{:S(2)}) collective-permute-start(bf16[2048,896]{1,0:T(8,128)(2,1)} %bitcast.25), channel_id=1, source_target_pairs={{0,1},{1,0},{2,3},{3,2},{4,5},{5,4},{6,7},{7,6}} | collective-permute-start | bytes 11010056 | tf_op jit(solution)/shard_map/ppermute | solution.py:190
  1651.1 186.0 %collective-permute-start.54 = (bf16[2048,896]{1,0:T(8,128)(2,1)}, bf16[2048,896]{1,0:T(8,128)(2,1)}, u32[]{:S(2)}, u32[]{:S(2)}) collective-permute-start(bf16[2048,896]{1,0:T(8,128)(2,1)} %bitcast.25), channel_id=1, source_target_pairs={{0,4},{4,0},{1,5},{5,1},{2,6},{6,2},{3,7},{7,3}} | collective-permute-start | bytes 11010056 | tf_op jit(solution)/shard_map/ppermute | solution.py:193
  1651.3 187.3 %collective-permute-start.52 = (bf16[2048,896]{1,0:T(8,128)(2,1)}, bf16[2048,896]{1,0:T(8,128)(2,1)}, u32[]{:S(2)}, u32[]{:S(2)}) collective-permute-start(bf16[2048,896]{1,0:T(8,128)(2,1)} %collective-permute-done.51), channel_id=1, source_target_pairs={{0,1},{1,0},{2,3},{3,2},{4,5},{5,4},{6,7},{7,6}} | collective-permute-start | bytes 11010056 | tf_op jit(solution)/shard_map/ppermute | solution.py:190
  1794.9 185.8 %collective-permute-start.53 = (bf16[2,512,2048]{2,1,0:T(8,128)(2,1)}, bf16[2,512,2048]{2,1,0:T(8,128)(2,1)}, u32[]{:S(2)}, u32[]{:S(2)}) collective-permute-start(bf16[2,512,2048]{2,1,0:T(8,128)(2,1)} %shard_map.128), channel_id=1, source_target_pairs={{0,4},{4,0},{1,5},{5,1},{2,6},{6,2},{3,7},{7,3}} | collective-permute-start | bytes 12582920 | tf_op jit(solution)/shard_map/ppermute | solution.py:193
  1795.1 176.7 %collective-permute-start.56 = (bf16[2048,896]{1,0:T(8,128)(2,1)}, bf16[2048,896]{1,0:T(8,128)(2,1)}, u32[]{:S(2)}, u32[]{:S(2)}) collective-permute-start(bf16[2048,896]{1,0:T(8,128)(2,1)} %collective-permute-done.51), channel_id=1, source_target_pairs={{0,4},{4,0},{1,5},{5,1},{2,6},{6,2},{3,7},{7,3}} | collective-permute-start | bytes 11010056 | tf_op jit(solution)/shard_map/ppermute | solution.py:193
  1837.1 182.1 %collective-permute-start.60 = (bf16[896,4096]{1,0:T(8,128)(2,1)}, bf16[896,4096]{1,0:T(8,128)(2,1)}, u32[]{:S(2)}, u32[]{:S(2)}) collective-permute-start(bf16[896,4096]{1,0:T(8,128)(2,1)} %pad_maximum_fusion.8.refs_0_.refs_4_), channel_id=1, source_target_pairs={{0,2},{1,3},{2,0},{3,1},{4,6},{5,7},{6,4},{7,5}} | collective-permute-start | bytes 22020104 | tf_op jit(solution)/shard_map/ppermute | solution.py:187
  1838.6 158.6 %collective-permute-start.55 = (bf16[2048,896]{1,0:T(8,128)(2,1)}, bf16[2048,896]{1,0:T(8,128)(2,1)S(1)}, u32[]{:S(2)}, u32[]{:S(2)}) collective-permute-start(bf16[2048,896]{1,0:T(8,128)(2,1)} %collective-permute-done.54), channel_id=1, source_target_pairs={{0,1},{1,0},{2,3},{3,2},{4,5},{5,4},{6,7},{7,6}} | collective-permute-start | bytes 11010056 | tf_op jit(solution)/shard_map/ppermute | solution.py:190
  1845.2 181.9 %collective-permute-start.59 = (bf16[896,4096]{1,0:T(8,128)(2,1)}, bf16[896,4096]{1,0:T(8,128)(2,1)}, u32[]{:S(2)}, u32[]{:S(2)}) collective-permute-start(bf16[896,4096]{1,0:T(8,128)(2,1)} %pad_maximum_fusion.8.refs_0_.refs_4_), channel_id=1, source_target_pairs={{0,1},{1,0},{2,3},{3,2},{4,5},{5,4},{6,7},{7,6}} | collective-permute-start | bytes 22020104 | tf_op jit(solution)/shard_map/ppermute | solution.py:190
  2025.6 160.4 %collective-permute-start.63 = (bf16[896,4096]{1,0:T(8,128)(2,1)}, bf16[896,4096]{1,0:T(8,128)(2,1)}, u32[]{:S(2)}, u32[]{:S(2)}) collective-permute-start(bf16[896,4096]{1,0:T(8,128)(2,1)} %pad_maximum_fusion.9.refs_0_.refs_4_), channel_id=1, source_target_pairs={{0,2},{1,3},{2,0},{3,1},{4,6},{5,7},{6,4},{7,5}} | collective-permute-start | bytes 22020104 | tf_op jit(solution)/shard_map/ppermute | solution.py:187
  2027.1 166.9 %collective-permute-start.62 = (bf16[896,4096]{1,0:T(8,128)(2,1)}, bf16[896,4096]{1,0:T(8,128)(2,1)}, u32[]{:S(2)}, u32[]{:S(2)}) collective-permute-start(bf16[896,4096]{1,0:T(8,128)(2,1)} %pad_maximum_fusion.9.refs_0_.refs_4_), channel_id=1, source_target_pairs={{0,1},{1,0},{2,3},{3,2},{4,5},{5,4},{6,7},{7,6}} | collective-permute-start | bytes 22020104 | tf_op jit(solution)/shard_map/ppermute | solution.py:190
  2186.0 160.7 %collective-permute-start.58 = (bf16[1024,3584]{1,0:T(8,128)(2,1)}, bf16[1024,3584]{1,0:T(8,128)(2,1)}, u32[]{:S(2)}, u32[]{:S(2)}) collective-permute-start(bf16[1024,3584]{1,0:T(8,128)(2,1)} %pad_maximum_fusion.7.h_ref), channel_id=1, source_target_pairs={{0,4},{4,0},{1,5},{5,1},{2,6},{6,2},{3,7},{7,3}} | collective-permute-start | bytes 22020104 | tf_op jit(solution)/shard_map/ppermute | solution.py:193
  2192.3 230.0 %collective-permute-start.66 = (bf16[896,4096]{1,0:T(8,128)(2,1)}, bf16[896,4096]{1,0:T(8,128)(2,1)}, u32[]{:S(2)}, u32[]{:S(2)}) collective-permute-start(bf16[896,4096]{1,0:T(8,128)(2,1)} %pad_maximum_fusion.10.refs_0_.refs_4_), channel_id=1, source_target_pairs={{0,2},{1,3},{2,0},{3,1},{4,6},{5,7},{6,4},{7,5}} | collective-permute-start | bytes 22020104 | tf_op jit(solution)/shard_map/ppermute | solution.py:187
  2194.0 232.3 %collective-permute-start.65 = (bf16[896,4096]{1,0:T(8,128)(2,1)}, bf16[896,4096]{1,0:T(8,128)(2,1)}, u32[]{:S(2)}, u32[]{:S(2)}) collective-permute-start(bf16[896,4096]{1,0:T(8,128)(2,1)} %pad_maximum_fusion.10.refs_0_.refs_4_), channel_id=1, source_target_pairs={{0,1},{1,0},{2,3},{3,2},{4,5},{5,4},{6,7},{7,6}} | collective-permute-start | bytes 22020104 | tf_op jit(solution)/shard_map/ppermute | solution.py:190
  2424.6 82.0 %collective-permute-start.69 = (bf16[896,2048]{1,0:T(8,128)(2,1)}, bf16[896,2048]{1,0:T(8,128)(2,1)}, u32[]{:S(2)}, u32[]{:S(2)}) collective-permute-start(bf16[896,2048]{1,0:T(8,128)(2,1)} %pad_maximum_fusion.16.refs_0_.refs_4_), channel_id=1, source_target_pairs={{0,2},{1,3},{2,0},{3,1},{4,6},{5,7},{6,4},{7,5}} | collective-permute-start | bytes 11010056 | tf_op jit(solution)/shard_map/ppermute | solution.py:187
  2426.1 89.1 %collective-permute-start.68 = (bf16[896,2048]{1,0:T(8,128)(2,1)}, bf16[896,2048]{1,0:T(8,128)(2,1)}, u32[]{:S(2)}, u32[]{:S(2)}) collective-permute-start(bf16[896,2048]{1,0:T(8,128)(2,1)} %pad_maximum_fusion.16.refs_0_.refs_4_), channel_id=1, source_target_pairs={{0,1},{1,0},{2,3},{3,2},{4,5},{5,4},{6,7},{7,6}} | collective-permute-start | bytes 11010056 | tf_op jit(solution)/shard_map/ppermute | solution.py:190
  2506.6 121.8 %collective-permute-start.71 = (bf16[7168,384]{1,0:T(8,128)(2,1)}, bf16[7168,384]{1,0:T(8,128)(2,1)}, u32[]{:S(2)}, u32[]{:S(2)}) collective-permute-start(bf16[7168,384]{1,0:T(8,128)(2,1)} %get-tuple-element.169), channel_id=1, source_target_pairs={{0,2},{1,3},{2,0},{3,1},{4,6},{5,7},{6,4},{7,5}} | collective-permute-start | bytes 16515080 | tf_op jit(solution)/shard_map/ppermute | solution.py:187
  2508.1 160.3 %collective-permute-start.76 = (bf16[7168,384]{1,0:T(8,128)(2,1)}, bf16[7168,384]{1,0:T(8,128)(2,1)}, u32[]{:S(2)}, u32[]{:S(2)}) collective-permute-start(bf16[7168,384]{1,0:T(8,128)(2,1)} %get-tuple-element.169), channel_id=1, source_target_pairs={{0,1},{1,0},{2,3},{3,2},{4,5},{5,4},{6,7},{7,6}} | collective-permute-start | bytes 16515080 | tf_op jit(solution)/shard_map/ppermute | solution.py:190
  2514.9 177.9 %collective-permute-start.77 = (bf16[7168,256]{1,0:T(8,128)(2,1)}, bf16[7168,256]{1,0:T(8,128)(2,1)}, u32[]{:S(2)}, u32[]{:S(2)}) collective-permute-start(bf16[7168,256]{1,0:T(8,128)(2,1)} %get-tuple-element.171), channel_id=1, source_target_pairs={{0,1},{1,0},{2,3},{3,2},{4,5},{5,4},{6,7},{7,6}} | collective-permute-start | bytes 11010056 | tf_op jit(solution)/shard_map/ppermute | solution.py:190
  2515.2 232.2 %collective-permute-start.75 = (bf16[7168,256]{1,0:T(8,128)(2,1)}, bf16[7168,256]{1,0:T(8,128)(2,1)}, u32[]{:S(2)}, u32[]{:S(2)}) collective-permute-start(bf16[7168,256]{1,0:T(8,128)(2,1)} %get-tuple-element.171), channel_id=1, source_target_pairs={{0,2},{1,3},{2,0},{3,1},{4,6},{5,7},{6,4},{7,5}} | collective-permute-start | bytes 11010056 | tf_op jit(solution)/shard_map/ppermute | solution.py:187
  2515.7 146.2 %collective-permute-start.78 = (bf16[7168,256]{1,0:T(8,128)(2,1)}, bf16[7168,256]{1,0:T(8,128)(2,1)S(1)}, u32[]{:S(2)}, u32[]{:S(2)}) collective-permute-start(bf16[7168,256]{1,0:T(8,128)(2,1)} %get-tuple-element.172), channel_id=1, source_target_pairs={{0,1},{1,0},{2,3},{3,2},{4,5},{5,4},{6,7},{7,6}} | collective-permute-start | bytes 11010056 | tf_op jit(solution)/shard_map/ppermute | solution.py:190
  2662.0 146.0 %collective-permute-start.74 = (bf16[7168,256]{1,0:T(8,128)(2,1)}, bf16[7168,256]{1,0:T(8,128)(2,1)}, u32[]{:S(2)}, u32[]{:S(2)}) collective-permute-start(bf16[7168,256]{1,0:T(8,128)(2,1)} %get-tuple-element.172), channel_id=1, source_target_pairs={{0,2},{1,3},{2,0},{3,1},{4,6},{5,7},{6,4},{7,5}} | collective-permute-start | bytes 11010056 | tf_op jit(solution)/shard_map/ppermute | solution.py:187
  2668.4 184.3 %collective-permute-start.86 = (f32[1024,384]{1,0:T(8,128)}, f32[1024,384]{1,0:T(8,128)}, u32[]{:S(2)}, u32[]{:S(2)}) collective-permute-start(f32[1024,384]{1,0:T(8,128)} %fusion.121), channel_id=1, source_target_pairs={{0,4},{4,0},{1,5},{5,1},{2,6},{6,2},{3,7},{7,3}} | collective-permute-start | bytes 4718600 | tf_op jit(solution)/shard_map/ppermute | solution.py:193
  2680.1 171.0 %collective-permute-start.85 = (f32[1024,256]{1,0:T(8,128)}, f32[1024,256]{1,0:T(8,128)}, u32[]{:S(2)}, u32[]{:S(2)}) collective-permute-start(f32[1024,256]{1,0:T(8,128)} %fusion.136), channel_id=1, source_target_pairs={{0,4},{4,0},{1,5},{5,1},{2,6},{6,2},{3,7},{7,3}} | collective-permute-start | bytes 3145736 | tf_op jit(solution)/shard_map/ppermute | solution.py:193
  2692.8 250.1 %collective-permute-start.81 = (f32[1024,384]{1,0:T(8,128)}, f32[1024,384]{1,0:T(8,128)}, u32[]{:S(2)}, u32[]{:S(2)}) collective-permute-start(f32[1024,384]{1,0:T(8,128)} %fusion.134), channel_id=1, source_target_pairs={{0,4},{4,0},{1,5},{5,1},{2,6},{6,2},{3,7},{7,3}} | collective-permute-start | bytes 4718600 | tf_op jit(solution)/shard_map/ppermute | solution.py:193
  2781.9 162.5 %collective-permute-start.73 = (f32[1024,384]{1,0:T(8,128)}, f32[1024,384]{1,0:T(8,128)}, u32[]{:S(2)}, u32[]{:S(2)}) collective-permute-start(f32[1024,384]{1,0:T(8,128)} %fusion.99), channel_id=1, source_target_pairs={{0,4},{4,0},{1,5},{5,1},{2,6},{6,2},{3,7},{7,3}} | collective-permute-start | bytes 4718600 | tf_op jit(solution)/shard_map/ppermute | solution.py:193
  2897.4 112.5 %collective-permute-start.88 = (f32[1024,256]{1,0:T(8,128)}, f32[1024,256]{1,0:T(8,128)}, u32[]{:S(2)}, u32[]{:S(2)}) collective-permute-start(f32[1024,256]{1,0:T(8,128)} %fusion.126), channel_id=1, source_target_pairs={{0,4},{4,0},{1,5},{5,1},{2,6},{6,2},{3,7},{7,3}} | collective-permute-start | bytes 3145736 | tf_op jit(solution)/shard_map/ppermute | solution.py:193
  2942.8 88.9 %collective-permute-start.91 = (f32[1024,256]{1,0:T(8,128)}, f32[1024,256]{1,0:T(8,128)}, u32[]{:S(2)}, u32[]{:S(2)}) collective-permute-start(f32[1024,256]{1,0:T(8,128)} %fusion.131), channel_id=1, source_target_pairs={{0,4},{4,0},{1,5},{5,1},{2,6},{6,2},{3,7},{7,3}} | collective-permute-start | bytes 3145736 | tf_op jit(solution)/shard_map/ppermute | solution.py:193
  (143 other events, 3778.1 us)

commit v3 on v2

--- a/solution.py
+++ b/solution.py
@@ -157,16 +157,16 @@
 
 X_ORDER = (
     ('kv', 0, 0), ('q', 0, 0), ('o', 0, 0), ('g', 0, 0), ('g', 0, 1), ('g', 0, 2), ('g', 0, 3),
-    ('d', 0, 0), ('d', 0, 1), ('kv', 1, 0), ('q', 1, 0), ('o', 1, 0), ('g', 1, 0), ('g', 1, 1), ('g', 1, 2), ('g', 1, 3),
+    ('d', 0, 0), ('d', 0, 1), ('kv', 1, 0), ('q', 1, 0), ('o', 1, 0), ('g', 1, 0), ('g', 1, 1), ('g', 1, 2), ('g', 1, 3), ('g', 1, 4),
     ('d', 1, 0), ('d', 1, 1), ('d', 1, 2),
 )
 
 
-FFN_CHUNKS = ((2048, 2048, 2048, 1024),) * 2
+FFN_CHUNKS = ((2048, 2048, 2048, 1024), (2048, 2048, 1536, 1024, 512))
 DOWN_CHUNKS = ((512, 384), (384, 256, 256))
 FFN_STEPS = (
     ('w0', 'w1', 'f0', 'f1', 'f2', 'w2', 'f3', 'w3'),
-    ('w0', 'w1', 'f0', 'f1', 'f2', 'f3', 'w2', 'w3'),
+    ('w0', 'w1', 'f0', 'f1', 'f2', 'f3', 'f4', 'w2', 'w3', 'w4'),
 )
 DOWN_STEPS = (('o', 'f0', 'w0', 'f1', 'w1'), ('f0', 'o', 'f1', 'w0', 'w1', 'f2', 'w2'))
 

time: 3040 us -> 3090 us (1.016)
    ppermute x19 -> x20, waiting for transfers between devices: 534 us -> 559 us  [send_x(): return lax.ppermute(a, 'tok', over_x)]
    pallas_call x16 -> x18, Pallas kernels: 541 us -> 552 us  [ffn_chunk(): pl.pallas_call(ffn_kernel, grid=(steps,), in_specs=in_specs, out_specs=pl...]
  transfers between devices with their start and end apart: 92 -> 95, of which waited for: 31 -> 33; matrix products, arithmetic and copies ran while one was open for 25% -> 24% of each run, Pallas kernels for 27% -> 27%
where the time goes in v3:
time: 3090 us
  waiting for transfers between devices  1410 us (46%)
  Pallas kernels  827 us (27%)
  matrix products  547 us (18%)
  other arithmetic  116 us (4%)
  local copies, waits for them, and re-layouts  112 us (4%)
  starting transfers between devices  70.1 us (2%)
    ppermute x31, waiting for transfers between devices, send_y(): return lax.ppermute(a, 'mp', [(0, 1), (1, 0)])  836 us
    ppermute x20, waiting for transfers between devices, send_x(): return lax.ppermute(a, 'tok', over_x)  559 us
    pallas_call x18, Pallas kernels, ffn_chunk(): pl.pallas_call(ffn_kernel, grid=(steps,), in_specs=in_specs, out_specs=pl...  552 us
    dot_general x20, matrix products, far_dots(): far_sum = jnp.dot(act_far, w4[j], preferred_element_type=F32)  239 us
    dot_general x20, matrix products, own_dots(): dot = jnp.dot(after(act_own, *own_gate), w4[j], preferred_element_type=F32)  184 us
    pallas_call x8, Pallas kernels, project(): pl.pallas_call(functools.partial(proj_kernel, rope_tiles, head_dim), grid...  178 us
    pallas_call x4, Pallas kernels, attention(): pl.pallas_call(functools.partial(attn_kernel, head_dim), grid=(micro_n, k...  97 us
    dot_general x8, matrix products, layer_pair(): jnp.dot(o_got, o_y[j], preferred_element_type=F32)  63.9 us
  transfers between devices with their start and end apart: 95, of which 33 were waited for; matrix products, arithmetic and copies ran while one was open for 24% of the time, Pallas kernels for 27%

profile of v3, /device:TPU:0, one launch (start us, length us, event | category | flops | bytes accessed | tf_op | source)
XLA Modules:
  0.0 3086.8 jit_solution(16691434300456301836)
XLA Ops:
  28.3 24.1 slice_bitcast_fusion.5
  75.0 97.6 %collective-permute-done.3 = s32[2,512]{1,0:T(2,128)S(1)} collective-permute-done((s32[2,512]{1,0:T(2,128)S(1)}, s32[2,512]{1,0:T(2,128)S(1)}, u32[]{:S(2)}, u32[]{:S(2)}) %collective-permute-start.3) | collective-permute-done | bytes 4128 | tf_op jit(solution)/shard_map/ppermute | solution.py:193
  203.2 21.7 shard_map.109
  224.9 39.5 %collective-permute-done.9 = bf16[2048,896]{1,0:T(8,128)(2,1)} collective-permute-done((bf16[2048,896]{1,0:T(8,128)(2,1)}, bf16[2048,896]{1,0:T(8,128)(2,1)}, u32[]{:S(2)}, u32[]{:S(2)}) %collective-permute-start.9) | collective-permute-done | bytes 3670048 | tf_op jit(solution)/shard_map/ppermute | solution.py:187
  264.4 22.0 shard_map.113
  288.0 22.7 shard_map.111
  310.6 22.6 shard_map.110
  334.2 24.1 shard_map.114
  358.9 61.9 %collective-permute-done.18.refs_2_.refs_6_ = bf16[896,4096]{1,0:T(8,128)(2,1)} collective-permute-done((bf16[896,4096]{1,0:T(8,128)(2,1)}, bf16[896,4096]{1,0:T(8,128)(2,1)}, u32[]{:S(2)}, u32[]{:S(2)}) %collective-permute-start.18) | collective-permute-done | bytes 7340064 | tf_op jit(solution)/shard_map/ppermute | solution.py:187
  423.3 24.5 shard_map.112
  470.1 66.7 %collective-permute-done.14 = bf16[2048,896]{1,0:T(8,128)(2,1)} collective-permute-done((bf16[2048,896]{1,0:T(8,128)(2,1)}, bf16[2048,896]{1,0:T(8,128)(2,1)}, u32[]{:S(2)}, u32[]{:S(2)}) %collective-permute-start.14) | collective-permute-done | bytes 3670048 | tf_op jit(solution)/shard_map/ppermute | solution.py:193
  582.8 37.9 %shard_map.115.refs_8_ = bf16[1024,7168]{1,0:T(8,128)(2,1)} custom-call(bf16[1024,3584]{1,0:T(8,128)(2,1)} %pad_maximum_fusion.2.h_ref, bf16[896,4096]{1,0:T(8,128)(2,1)} %pad_maximum_fusion.3.refs_0_.refs_4_, bf16[896,4096]{1,0:T(8,128)(2,1)} %collective-permute-done.17.refs_1_.refs_5_, bf16[896,4096]{1,0:T(8,128)(2,1)} %collective-permute-done.18.refs_2_.refs_6_, ...), custom_call_target="tpu_custom_call" | custom-call | flops 30064771072 | bytes 40894464 | tf_op jit(solution)/shard_map/pallas_call | solution.py:96
  620.7 84.2 %collective-permute-done.21.refs_2_.refs_6_ = bf16[896,4096]{1,0:T(8,128)(2,1)} collective-permute-done((bf16[896,4096]{1,0:T(8,128)(2,1)}, bf16[896,4096]{1,0:T(8,128)(2,1)}, u32[]{:S(2)}, u32[]{:S(2)}) %collective-permute-start.21) | collective-permute-done | bytes 7340064 | tf_op jit(solution)/shard_map/ppermute | solution.py:187
  716.9 37.8 %shard_map.116.refs_8_ = bf16[1024,7168]{1,0:T(8,128)(2,1)} custom-call(bf16[1024,3584]{1,0:T(8,128)(2,1)} %pad_maximum_fusion.2.h_ref, bf16[896,4096]{1,0:T(8,128)(2,1)} %pad_maximum_fusion.4.refs_0_.refs_4_, bf16[896,4096]{1,0:T(8,128)(2,1)} %collective-permute-done.20.refs_1_.refs_5_, ...), custom_call_target="tpu_custom_call", output_to_operand_aliasing={{}: (9, {})} | custom-call | flops 30064771072 | bytes 40894464 | tf_op jit(solution)/shard_map/pallas_call | solution.py:96
  754.7 110.9 %collective-permute-done.16.h_ref = bf16[1024,3584]{1,0:T(8,128)(2,1)} collective-permute-done((bf16[1024,3584]{1,0:T(8,128)(2,1)}, bf16[1024,3584]{1,0:T(8,128)(2,1)}, u32[]{:S(2)}, u32[]{:S(2)}) %collective-permute-start.16) | collective-permute-done | bytes 7340064 | tf_op jit(solution)/shard_map/ppermute | solution.py:193
  865.6 37.7 %shard_map.117.refs_8_ = bf16[1024,7168]{1,0:T(8,128)(2,1)} custom-call(bf16[1024,3584]{1,0:T(8,128)(2,1)} %collective-permute-done.16.h_ref, bf16[896,4096]{1,0:T(8,128)(2,1)} %pad_maximum_fusion.3.refs_0_.refs_4_, bf16[896,4096]{1,0:T(8,128)(2,1)} %collective-permute-done.17.refs_1_.refs_5_, bf16[896,4096]{1,0:T(8,128)(2,1)} %collective-permute-done.18.refs_2_.refs_6_, ...), custom_call_target="tpu_custom_call" | custom-call | flops 30064771072 | bytes 40894464 | tf_op jit(solution)/shard_map/pallas_call | solution.py:96
  903.3 37.7 %shard_map.118.refs_8_ = bf16[1024,7168]{1,0:T(8,128)(2,1)} custom-call(bf16[1024,3584]{1,0:T(8,128)(2,1)} %collective-permute-done.16.h_ref, bf16[896,4096]{1,0:T(8,128)(2,1)} %pad_maximum_fusion.4.refs_0_.refs_4_, bf16[896,4096]{1,0:T(8,128)(2,1)} %collective-permute-done.20.refs_1_.refs_5_, ...), custom_call_target="tpu_custom_call", output_to_operand_aliasing={{}: (9, {})} | custom-call | flops 30064771072 | bytes 40894464 | tf_op jit(solution)/shard_map/pallas_call | solution.py:96
  956.6 38.2 %shard_map.119.refs_8_ = bf16[1024,7168]{1,0:T(8,128)(2,1)} custom-call(bf16[1024,3584]{1,0:T(8,128)(2,1)} %collective-permute-done.16.h_ref, bf16[896,4096]{1,0:T(8,128)(2,1)} %pad_maximum_fusion.5.refs_0_.refs_4_, bf16[896,4096]{1,0:T(8,128)(2,1)} %collective-permute-done.23.refs_1_.refs_5_, ...), custom_call_target="tpu_custom_call", output_to_operand_aliasing={{}: (9, {})} | custom-call | flops 30064771072 | bytes 40894464 | tf_op jit(solution)/shard_map/pallas_call | solution.py:96
  994.7 37.8 %shard_map.120.refs_8_ = bf16[1024,7168]{1,0:T(8,128)(2,1)} custom-call(bf16[1024,3584]{1,0:T(8,128)(2,1)} %pad_maximum_fusion.2.h_ref, bf16[896,4096]{1,0:T(8,128)(2,1)} %pad_maximum_fusion.5.refs_0_.refs_4_, bf16[896,4096]{1,0:T(8,128)(2,1)} %collective-permute-done.23.refs_1_.refs_5_, ...), custom_call_target="tpu_custom_call", output_to_operand_aliasing={{}: (9, {})} | custom-call | flops 30064771072 | bytes 40894464 | tf_op jit(solution)/shard_map/pallas_call | solution.py:96
  1044.2 21.7 shard_map.121
  1065.9 21.7 shard_map.122
  1087.6 13.9 fusion.110
  1134.8 68.1 %collective-permute-done.31 = bf16[7168,512]{1,0:T(8,128)(2,1)} collective-permute-done((bf16[7168,512]{1,0:T(8,128)(2,1)}, bf16[7168,512]{1,0:T(8,128)(2,1)}, u32[]{:S(2)}, u32[]{:S(2)}) %collective-permute-start.31) | collective-permute-done | bytes 7340064 | tf_op jit(solution)/shard_map/ppermute | solution.py:187
  1213.1 14.3 fusion.111
  1227.4 14.1 fusion.119
  1243.5 14.1 fusion.112
  1280.0 44.1 %collective-permute-done.30 = bf16[7168,384]{1,0:T(8,128)(2,1)} collective-permute-done((bf16[7168,384]{1,0:T(8,128)(2,1)S(1)}, bf16[7168,384]{1,0:T(8,128)(2,1)}, u32[]{:S(2)}, u32[]{:S(2)}) %collective-permute-start.30) | collective-permute-done | bytes 5505056 | tf_op jit(solution)/shard_map/ppermute | solution.py:187
  1338.1 14.0 fusion.101
  1381.1 13.7 fusion.116
  1420.8 31.6 %collective-permute-done.36 = f32[1024,384]{1,0:T(8,128)} collective-permute-done((f32[1024,384]{1,0:T(8,128)}, f32[1024,384]{1,0:T(8,128)}, u32[]{:S(2)}, u32[]{:S(2)}) %collective-permute-start.36) | collective-permute-done | bytes 1572896 | tf_op jit(solution)/shard_map/ppermute | solution.py:193
  1454.1 32.0 %collective-permute-done.40 = f32[1024,384]{1,0:T(8,128)} collective-permute-done((f32[1024,384]{1,0:T(8,128)}, f32[1024,384]{1,0:T(8,128)}, u32[]{:S(2)}, u32[]{:S(2)}) %collective-permute-start.40) | collective-permute-done | bytes 1572896 | tf_op jit(solution)/shard_map/ppermute | solution.py:193
  1493.8 37.1 %collective-permute-done.41 = f32[1024,512]{1,0:T(8,128)S(1)} collective-permute-done((f32[1024,512]{1,0:T(8,128)}, f32[1024,512]{1,0:T(8,128)S(1)}, u32[]{:S(2)}, u32[]{:S(2)}) %collective-permute-start.41) | collective-permute-done | bytes 2097184 | tf_op jit(solution)/shard_map/ppermute | solution.py:193
  1537.3 26.9 collective-permute-done.42
  1588.8 21.7 shard_map.123
  1610.5 46.5 %collective-permute-done.51 = bf16[2048,896]{1,0:T(8,128)(2,1)} collective-permute-done((bf16[2048,896]{1,0:T(8,128)(2,1)}, bf16[2048,896]{1,0:T(8,128)(2,1)}, u32[]{:S(2)}, u32[]{:S(2)}) %collective-permute-start.51) | collective-permute-done | bytes 3670048 | tf_op jit(solution)/shard_map/ppermute | solution.py:187
  1658.8 22.7 shard_map.124
  1681.5 50.5 %collective-permute-done.49.h_ref = bf16[1024,3584]{1,0:T(8,128)(2,1)} collective-permute-done((bf16[1024,3584]{1,0:T(8,128)(2,1)}, bf16[1024,3584]{1,0:T(8,128)(2,1)}, u32[]{:S(2)}, u32[]{:S(2)}) %collective-permute-start.49) | collective-permute-done | bytes 7340064 | tf_op jit(solution)/shard_map/ppermute | solution.py:193
  1732.0 22.1 shard_map.127
  1754.1 22.7 shard_map.125
  1776.8 24.2 shard_map.128
  1803.0 24.3 shard_map.126
  1852.1 125.9 %collective-permute-done.56 = bf16[2048,896]{1,0:T(8,128)(2,1)} collective-permute-done((bf16[2048,896]{1,0:T(8,128)(2,1)}, bf16[2048,896]{1,0:T(8,128)(2,1)}, u32[]{:S(2)}, u32[]{:S(2)}) %collective-permute-start.56) | collective-permute-done | bytes 3670048 | tf_op jit(solution)/shard_map/ppermute | solution.py:193
  2037.4 37.7 %shard_map.129.refs_8_ = bf16[1024,7168]{1,0:T(8,128)(2,1)} custom-call(bf16[1024,3584]{1,0:T(8,128)(2,1)} %pad_maximum_fusion.7.h_ref, bf16[896,4096]{1,0:T(8,128)(2,1)} %pad_maximum_fusion.8.refs_0_.refs_4_, bf16[896,4096]{1,0:T(8,128)(2,1)} %collective-permute-done.59.refs_1_.refs_5_, bf16[896,4096]{1,0:T(8,128)(2,1)} %collective-permute-done.60.refs_2_.refs_6_, ...), custom_call_target="tpu_custom_call" | custom-call | flops 30064771072 | bytes 40894464 | tf_op jit(solution)/shard_map/pallas_call | solution.py:96
  2075.2 116.7 %collective-permute-done.63.refs_2_.refs_6_ = bf16[896,4096]{1,0:T(8,128)(2,1)} collective-permute-done((bf16[896,4096]{1,0:T(8,128)(2,1)}, bf16[896,4096]{1,0:T(8,128)(2,1)}, u32[]{:S(2)}, u32[]{:S(2)}) %collective-permute-start.63) | collective-permute-done | bytes 7340064 | tf_op jit(solution)/shard_map/ppermute | solution.py:187
  2203.9 37.8 %shard_map.130.refs_8_ = bf16[1024,7168]{1,0:T(8,128)(2,1)} custom-call(bf16[1024,3584]{1,0:T(8,128)(2,1)} %pad_maximum_fusion.7.h_ref, bf16[896,4096]{1,0:T(8,128)(2,1)} %pad_maximum_fusion.9.refs_0_.refs_4_, bf16[896,4096]{1,0:T(8,128)(2,1)} %collective-permute-done.62.refs_1_.refs_5_, ...), custom_call_target="tpu_custom_call", output_to_operand_aliasing={{}: (9, {})} | custom-call | flops 30064771072 | bytes 40894464 | tf_op jit(solution)/shard_map/pallas_call | solution.py:96
  2241.6 110.9 %collective-permute-done.58.h_ref = bf16[1024,3584]{1,0:T(8,128)(2,1)} collective-permute-done((bf16[1024,3584]{1,0:T(8,128)(2,1)}, bf16[1024,3584]{1,0:T(8,128)(2,1)}, u32[]{:S(2)}, u32[]{:S(2)}) %collective-permute-start.58) | collective-permute-done | bytes 7340064 | tf_op jit(solution)/shard_map/ppermute | solution.py:193
  2352.6 37.7 %shard_map.131.refs_8_ = bf16[1024,7168]{1,0:T(8,128)(2,1)} custom-call(bf16[1024,3584]{1,0:T(8,128)(2,1)} %collective-permute-done.58.h_ref, bf16[896,4096]{1,0:T(8,128)(2,1)} %pad_maximum_fusion.8.refs_0_.refs_4_, bf16[896,4096]{1,0:T(8,128)(2,1)} %collective-permute-done.59.refs_1_.refs_5_, bf16[896,4096]{1,0:T(8,128)(2,1)} %collective-permute-done.60.refs_2_.refs_6_, ...), custom_call_target="tpu_custom_call" | custom-call | flops 30064771072 | bytes 40894464 | tf_op jit(solution)/shard_map/pallas_call | solution.py:96
  2390.3 37.7 %shard_map.132.refs_8_ = bf16[1024,7168]{1,0:T(8,128)(2,1)} custom-call(bf16[1024,3584]{1,0:T(8,128)(2,1)} %collective-permute-done.58.h_ref, bf16[896,4096]{1,0:T(8,128)(2,1)} %pad_maximum_fusion.9.refs_0_.refs_4_, bf16[896,4096]{1,0:T(8,128)(2,1)} %collective-permute-done.62.refs_1_.refs_5_, ...), custom_call_target="tpu_custom_call", output_to_operand_aliasing={{}: (9, {})} | custom-call | flops 30064771072 | bytes 40894464 | tf_op jit(solution)/shard_map/pallas_call | solution.py:96
  2437.4 29.9 shard_map.133.refs_8_
  2467.3 45.1 %collective-permute-done.69.refs_2_.refs_6_ = bf16[896,2048]{1,0:T(8,128)(2,1)} collective-permute-done((bf16[896,2048]{1,0:T(8,128)(2,1)S(1)}, bf16[896,2048]{1,0:T(8,128)(2,1)}, u32[]{:S(2)}, u32[]{:S(2)}) %collective-permute-start.69) | collective-permute-done | bytes 3670048 | tf_op jit(solution)/shard_map/ppermute | solution.py:187
  2519.2 21.7 shard_map.134.refs_8_
  2540.9 17.9 collective-permute-done.72.refs_2_.refs_6_
  2582.5 29.8 shard_map.136.refs_8_
  2612.3 21.7 shard_map.137.refs_8_
  2634.1 13.9 shard_map.138
  2648.0 28.7 collective-permute-done.74
  2732.4 13.9 fusion.122
  2901.4 21.5 collective-permute-done.90
  2931.5 13.9 collective-permute-done.87
  2946.9 20.9 collective-permute-done.86
  2969.4 20.9 collective-permute-done.85
  3006.4 28.9 collective-permute-done.93
  3035.3 22.5 collective-permute-done.92
  3062.3 17.3 collective-permute-done.94
  (507 shorter events, 760.3 us)
Async XLA Ops:
  8.6 165.2 %collective-permute-start.1 = (bf16[896,2048]{1,0:T(8,128)(2,1)}, bf16[896,2048]{1,0:T(8,128)(2,1)}, u32[]{:S(2)}, u32[]{:S(2)}) collective-permute-start(bf16[896,2048]{1,0:T(8,128)(2,1)} %bitcast.44.refs_0_), channel_id=1, source_target_pairs={{0,2},{1,3},{2,0},{3,1},{4,6},{5,7},{6,4},{7,5}} | collective-permute-start | bytes 11010056 | tf_op jit(solution)/shard_map/ppermute | solution.py:187
  11.9 183.2 %collective-permute-start = (bf16[896,2048]{1,0:T(8,128)(2,1)}, bf16[896,2048]{1,0:T(8,128)(2,1)}, u32[]{:S(2)}, u32[]{:S(2)}) collective-permute-start(bf16[896,2048]{1,0:T(8,128)(2,1)} %bitcast.44.refs_0_), channel_id=1, source_target_pairs={{0,1},{1,0},{2,3},{3,2},{4,5},{5,4},{6,7},{7,6}} | collective-permute-start | bytes 11010056 | tf_op jit(solution)/shard_map/ppermute | solution.py:190
  11.9 170.0 %collective-permute-start.7 = (bf16[2,512,3584]{2,1,0:T(8,128)(2,1)}, bf16[2,512,3584]{2,1,0:T(8,128)(2,1)}, u32[]{:S(2)}, u32[]{:S(2)}) collective-permute-start(bf16[2,512,3584]{2,1,0:T(8,128)(2,1)} %param.11), channel_id=1, source_target_pairs={{0,4},{4,0},{1,5},{5,1},{2,6},{6,2},{3,7},{7,3}} | collective-permute-start | bytes 22020104 | tf_op jit(solution)/shard_map/ppermute | solution.py:193
  13.4 159.2 %collective-permute-start.3 = (s32[2,512]{1,0:T(2,128)S(1)}, s32[2,512]{1,0:T(2,128)S(1)}, u32[]{:S(2)}, u32[]{:S(2)}) collective-permute-start(s32[2,512]{1,0:T(2,128)S(1)} %copy-done.80), channel_id=1, source_target_pairs={{0,4},{4,0},{1,5},{5,1},{2,6},{6,2},{3,7},{7,3}} | collective-permute-start | bytes 12296 | tf_op jit(solution)/shard_map/ppermute | solution.py:193
  23.5 173.3 %collective-permute-start.5 = (bf16[896,2048]{1,0:T(8,128)(2,1)}, bf16[896,2048]{1,0:T(8,128)(2,1)}, u32[]{:S(2)}, u32[]{:S(2)}) collective-permute-start(bf16[896,2048]{1,0:T(8,128)(2,1)} %constant_dynamic-update-slice_fusion.refs_0_), channel_id=1, source_target_pairs={{0,2},{1,3},{2,0},{3,1},{4,6},{5,7},{6,4},{7,5}} | collective-permute-start | bytes 11010056 | tf_op jit(solution)/shard_map/ppermute | solution.py:187
  172.7 113.8 %collective-permute-start.4 = (bf16[896,2048]{1,0:T(8,128)(2,1)}, bf16[896,2048]{1,0:T(8,128)(2,1)}, u32[]{:S(2)}, u32[]{:S(2)}) collective-permute-start(bf16[896,2048]{1,0:T(8,128)(2,1)} %constant_dynamic-update-slice_fusion.refs_0_), channel_id=1, source_target_pairs={{0,1},{1,0},{2,3},{3,2},{4,5},{5,4},{6,7},{7,6}} | collective-permute-start | bytes 11010056 | tf_op jit(solution)/shard_map/ppermute | solution.py:190
  181.9 82.5 %collective-permute-start.9 = (bf16[2048,896]{1,0:T(8,128)(2,1)}, bf16[2048,896]{1,0:T(8,128)(2,1)}, u32[]{:S(2)}, u32[]{:S(2)}) collective-permute-start(bf16[2048,896]{1,0:T(8,128)(2,1)} %bitcast.230), channel_id=1, source_target_pairs={{0,2},{1,3},{2,0},{3,1},{4,6},{5,7},{6,4},{7,5}} | collective-permute-start | bytes 11010056 | tf_op jit(solution)/shard_map/ppermute | solution.py:187
  195.1 225.7 %collective-permute-start.18 = (bf16[896,4096]{1,0:T(8,128)(2,1)}, bf16[896,4096]{1,0:T(8,128)(2,1)}, u32[]{:S(2)}, u32[]{:S(2)}) collective-permute-start(bf16[896,4096]{1,0:T(8,128)(2,1)} %pad_maximum_fusion.3.refs_0_.refs_4_), channel_id=1, source_target_pairs={{0,2},{1,3},{2,0},{3,1},{4,6},{5,7},{6,4},{7,5}} | collective-permute-start | bytes 22020104 | tf_op jit(solution)/shard_map/ppermute | solution.py:187
  196.8 91.1 %collective-permute-start.6 = (bf16[896,2048]{1,0:T(8,128)(2,1)}, bf16[896,2048]{1,0:T(8,128)(2,1)}, u32[]{:S(2)}, u32[]{:S(2)}) collective-permute-start(bf16[896,2048]{1,0:T(8,128)(2,1)} %collective-permute-done.5.refs_2_), channel_id=1, source_target_pairs={{0,1},{1,0},{2,3},{3,2},{4,5},{5,4},{6,7},{7,6}} | collective-permute-start | bytes 11010056 | tf_op jit(solution)/shard_map/ppermute | solution.py:190
  202.7 259.7 %collective-permute-start.8 = (bf16[2048,896]{1,0:T(8,128)(2,1)S(1)}, bf16[2048,896]{1,0:T(8,128)(2,1)}, u32[]{:S(2)}, u32[]{:S(2)}) collective-permute-start(bf16[2048,896]{1,0:T(8,128)(2,1)S(1)} %bitcast.231), channel_id=1, source_target_pairs={{0,1},{1,0},{2,3},{3,2},{4,5},{5,4},{6,7},{7,6}} | collective-permute-start | bytes 11010056 | tf_op jit(solution)/shard_map/ppermute | solution.py:190
  264.4 198.0 %collective-permute-start.10 = (bf16[2048,896]{1,0:T(8,128)(2,1)}, bf16[2048,896]{1,0:T(8,128)(2,1)}, u32[]{:S(2)}, u32[]{:S(2)}) collective-permute-start(bf16[2048,896]{1,0:T(8,128)(2,1)} %collective-permute-done.9), channel_id=1, source_target_pairs={{0,1},{1,0},{2,3},{3,2},{4,5},{5,4},{6,7},{7,6}} | collective-permute-start | bytes 11010056 | tf_op jit(solution)/shard_map/ppermute | solution.py:190
  286.4 176.5 %collective-permute-start.12 = (bf16[2048,896]{1,0:T(8,128)(2,1)S(1)}, bf16[2048,896]{1,0:T(8,128)(2,1)}, u32[]{:S(2)}, u32[]{:S(2)}) collective-permute-start(bf16[2048,896]{1,0:T(8,128)(2,1)S(1)} %bitcast.232), channel_id=1, source_target_pairs={{0,4},{4,0},{1,5},{5,1},{2,6},{6,2},{3,7},{7,3}} | collective-permute-start | bytes 11010056 | tf_op jit(solution)/shard_map/ppermute | solution.py:193
  358.4 185.8 %collective-permute-start.11 = (bf16[2,512,2048]{2,1,0:T(8,128)(2,1)}, bf16[2,512,2048]{2,1,0:T(8,128)(2,1)}, u32[]{:S(2)}, u32[]{:S(2)}) collective-permute-start(bf16[2,512,2048]{2,1,0:T(8,128)(2,1)} %shard_map.114), channel_id=1, source_target_pairs={{0,4},{4,0},{1,5},{5,1},{2,6},{6,2},{3,7},{7,3}} | collective-permute-start | bytes 12582920 | tf_op jit(solution)/shard_map/ppermute | solution.py:193
  420.8 116.0 %collective-permute-start.14 = (bf16[2048,896]{1,0:T(8,128)(2,1)}, bf16[2048,896]{1,0:T(8,128)(2,1)}, u32[]{:S(2)}, u32[]{:S(2)}) collective-permute-start(bf16[2048,896]{1,0:T(8,128)(2,1)} %collective-permute-done.9), channel_id=1, source_target_pairs={{0,4},{4,0},{1,5},{5,1},{2,6},{6,2},{3,7},{7,3}} | collective-permute-start | bytes 11010056 | tf_op jit(solution)/shard_map/ppermute | solution.py:193
  462.4 120.4 %collective-permute-start.17 = (bf16[896,4096]{1,0:T(8,128)(2,1)}, bf16[896,4096]{1,0:T(8,128)(2,1)}, u32[]{:S(2)}, u32[]{:S(2)}) collective-permute-start(bf16[896,4096]{1,0:T(8,128)(2,1)} %pad_maximum_fusion.3.refs_0_.refs_4_), channel_id=1, source_target_pairs={{0,1},{1,0},{2,3},{3,2},{4,5},{5,4},{6,7},{7,6}} | collective-permute-start | bytes 22020104 | tf_op jit(solution)/shard_map/ppermute | solution.py:190
  462.4 120.4 %collective-permute-start.19 = (bf16[896,4096]{1,0:T(8,128)(2,1)}, bf16[896,4096]{1,0:T(8,128)(2,1)}, u32[]{:S(2)}, u32[]{:S(2)}) collective-permute-start(bf16[896,4096]{1,0:T(8,128)(2,1)} %collective-permute-done.18.refs_2_.refs_6_), channel_id=1, source_target_pairs={{0,1},{1,0},{2,3},{3,2},{4,5},{5,4},{6,7},{7,6}} | collective-permute-start | bytes 22020104 | tf_op jit(solution)/shard_map/ppermute | solution.py:190
  462.9 98.1 %collective-permute-start.13 = (bf16[2048,896]{1,0:T(8,128)(2,1)}, bf16[2048,896]{1,0:T(8,128)(2,1)S(1)}, u32[]{:S(2)}, u32[]{:S(2)}) collective-permute-start(bf16[2048,896]{1,0:T(8,128)(2,1)} %collective-permute-done.12), channel_id=1, source_target_pairs={{0,1},{1,0},{2,3},{3,2},{4,5},{5,4},{6,7},{7,6}} | collective-permute-start | bytes 11010056 | tf_op jit(solution)/shard_map/ppermute | solution.py:190
  544.2 160.7 %collective-permute-start.21 = (bf16[896,4096]{1,0:T(8,128)(2,1)}, bf16[896,4096]{1,0:T(8,128)(2,1)}, u32[]{:S(2)}, u32[]{:S(2)}) collective-permute-start(bf16[896,4096]{1,0:T(8,128)(2,1)} %pad_maximum_fusion.4.refs_0_.refs_4_), channel_id=1, source_target_pairs={{0,2},{1,3},{2,0},{3,1},{4,6},{5,7},{6,4},{7,5}} | collective-permute-start | bytes 22020104 | tf_op jit(solution)/shard_map/ppermute | solution.py:187
  561.0 151.9 %collective-permute-start.20 = (bf16[896,4096]{1,0:T(8,128)(2,1)}, bf16[896,4096]{1,0:T(8,128)(2,1)}, u32[]{:S(2)}, u32[]{:S(2)}) collective-permute-start(bf16[896,4096]{1,0:T(8,128)(2,1)} %pad_maximum_fusion.4.refs_0_.refs_4_), channel_id=1, source_target_pairs={{0,1},{1,0},{2,3},{3,2},{4,5},{5,4},{6,7},{7,6}} | collective-permute-start | bytes 22020104 | tf_op jit(solution)/shard_map/ppermute | solution.py:190
  704.9 160.7 %collective-permute-start.16 = (bf16[1024,3584]{1,0:T(8,128)(2,1)}, bf16[1024,3584]{1,0:T(8,128)(2,1)}, u32[]{:S(2)}, u32[]{:S(2)}) collective-permute-start(bf16[1024,3584]{1,0:T(8,128)(2,1)} %pad_maximum_fusion.2.h_ref), channel_id=1, source_target_pairs={{0,4},{4,0},{1,5},{5,1},{2,6},{6,2},{3,7},{7,3}} | collective-permute-start | bytes 22020104 | tf_op jit(solution)/shard_map/ppermute | solution.py:193
  712.4 228.7 %collective-permute-start.24 = (bf16[896,4096]{1,0:T(8,128)(2,1)}, bf16[896,4096]{1,0:T(8,128)(2,1)}, u32[]{:S(2)}, u32[]{:S(2)}) collective-permute-start(bf16[896,4096]{1,0:T(8,128)(2,1)} %pad_maximum_fusion.5.refs_0_.refs_4_), channel_id=1, source_target_pairs={{0,2},{1,3},{2,0},{3,1},{4,6},{5,7},{6,4},{7,5}} | collective-permute-start | bytes 22020104 | tf_op jit(solution)/shard_map/ppermute | solution.py:187
  712.9 243.6 %collective-permute-start.23 = (bf16[896,4096]{1,0:T(8,128)(2,1)}, bf16[896,4096]{1,0:T(8,128)(2,1)}, u32[]{:S(2)}, u32[]{:S(2)}) collective-permute-start(bf16[896,4096]{1,0:T(8,128)(2,1)} %pad_maximum_fusion.5.refs_0_.refs_4_), channel_id=1, source_target_pairs={{0,1},{1,0},{2,3},{3,2},{4,5},{5,4},{6,7},{7,6}} | collective-permute-start | bytes 22020104 | tf_op jit(solution)/shard_map/ppermute | solution.py:190
  949.1 83.4 %collective-permute-start.27 = (bf16[896,2048]{1,0:T(8,128)(2,1)}, bf16[896,2048]{1,0:T(8,128)(2,1)}, u32[]{:S(2)}, u32[]{:S(2)}) collective-permute-start(bf16[896,2048]{1,0:T(8,128)(2,1)} %pad_maximum_fusion.11.refs_0_.refs_4_), channel_id=1, source_target_pairs={{0,2},{1,3},{2,0},{3,1},{4,6},{5,7},{6,4},{7,5}} | collective-permute-start | bytes 11010056 | tf_op jit(solution)/shard_map/ppermute | solution.py:187
  949.4 94.8 %collective-permute-start.26 = (bf16[896,2048]{1,0:T(8,128)(2,1)}, bf16[896,2048]{1,0:T(8,128)(2,1)}, u32[]{:S(2)}, u32[]{:S(2)}) collective-permute-start(bf16[896,2048]{1,0:T(8,128)(2,1)} %pad_maximum_fusion.11.refs_0_.refs_4_), channel_id=1, source_target_pairs={{0,1},{1,0},{2,3},{3,2},{4,5},{5,4},{6,7},{7,6}} | collective-permute-start | bytes 11010056 | tf_op jit(solution)/shard_map/ppermute | solution.py:190
  956.3 145.3 %collective-permute-start.32 = (bf16[7168,512]{1,0:T(8,128)(2,1)}, bf16[7168,512]{1,0:T(8,128)(2,1)}, u32[]{:S(2)}, u32[]{:S(2)}) collective-permute-start(bf16[7168,512]{1,0:T(8,128)(2,1)} %slice_bitcast_fusion), channel_id=1, source_target_pairs={{0,1},{1,0},{2,3},{3,2},{4,5},{5,4},{6,7},{7,6}} | collective-permute-start | bytes 22020104 | tf_op jit(solution)/shard_map/ppermute | solution.py:190
  1042.5 160.4 %collective-permute-start.31 = (bf16[7168,512]{1,0:T(8,128)(2,1)}, bf16[7168,512]{1,0:T(8,128)(2,1)}, u32[]{:S(2)}, u32[]{:S(2)}) collective-permute-start(bf16[7168,512]{1,0:T(8,128)(2,1)} %slice_bitcast_fusion), channel_id=1, source_target_pairs={{0,2},{1,3},{2,0},{3,1},{4,6},{5,7},{6,4},{7,5}} | collective-permute-start | bytes 22020104 | tf_op jit(solution)/shard_map/ppermute | solution.py:187
  1202.9 121.2 %collective-permute-start.30 = (bf16[7168,384]{1,0:T(8,128)(2,1)S(1)}, bf16[7168,384]{1,0:T(8,128)(2,1)}, u32[]{:S(2)}, u32[]{:S(2)}) collective-permute-start(bf16[7168,384]{1,0:T(8,128)(2,1)S(1)} %bitcast.229), channel_id=1, source_target_pairs={{0,2},{1,3},{2,0},{3,1},{4,6},{5,7},{6,4},{7,5}} | collective-permute-start | bytes 16515080 | tf_op jit(solution)/shard_map/ppermute | solution.py:187
  1241.5 165.3 %collective-permute-start.37 = (f32[1024,512]{1,0:T(8,128)}, f32[1024,512]{1,0:T(8,128)}, u32[]{:S(2)}, u32[]{:S(2)}) collective-permute-start(f32[1024,512]{1,0:T(8,128)} %fusion.119), channel_id=1, source_target_pairs={{0,4},{4,0},{1,5},{5,1},{2,6},{6,2},{3,7},{7,3}} | collective-permute-start | bytes 6291464 | tf_op jit(solution)/shard_map/ppermute | solution.py:193
  1243.0 209.4 %collective-permute-start.39 = (f32[1024,512]{1,0:T(8,128)}, f32[1024,512]{1,0:T(8,128)S(1)}, u32[]{:S(2)}, u32[]{:S(2)}) collective-permute-start(f32[1024,512]{1,0:T(8,128)} %fusion.111), channel_id=1, source_target_pairs={{0,4},{4,0},{1,5},{5,1},{2,6},{6,2},{3,7},{7,3}} | collective-permute-start | bytes 6291464 | tf_op jit(solution)/shard_map/ppermute | solution.py:193
  1394.8 91.3 %collective-permute-start.40 = (f32[1024,384]{1,0:T(8,128)}, f32[1024,384]{1,0:T(8,128)}, u32[]{:S(2)}, u32[]{:S(2)}) collective-permute-start(f32[1024,384]{1,0:T(8,128)} %fusion.115), channel_id=1, source_target_pairs={{0,4},{4,0},{1,5},{5,1},{2,6},{6,2},{3,7},{7,3}} | collective-permute-start | bytes 4718600 | tf_op jit(solution)/shard_map/ppermute | solution.py:193
  1406.8 124.1 %collective-permute-start.41 = (f32[1024,512]{1,0:T(8,128)}, f32[1024,512]{1,0:T(8,128)S(1)}, u32[]{:S(2)}, u32[]{:S(2)}) collective-permute-start(f32[1024,512]{1,0:T(8,128)} %fusion.112), channel_id=1, source_target_pairs={{0,4},{4,0},{1,5},{5,1},{2,6},{6,2},{3,7},{7,3}} | collective-permute-start | bytes 6291464 | tf_op jit(solution)/shard_map/ppermute | solution.py:193
  1419.3 153.2 %collective-permute-start.44 = (bf16[896,2048]{1,0:T(8,128)(2,1)}, bf16[896,2048]{1,0:T(8,128)(2,1)}, u32[]{:S(2)}, u32[]{:S(2)}) collective-permute-start(bf16[896,2048]{1,0:T(8,128)(2,1)} %bitcast.61.refs_0_), channel_id=1, source_target_pairs={{0,2},{1,3},{2,0},{3,1},{4,6},{5,7},{6,4},{7,5}} | collective-permute-start | bytes 11010056 | tf_op jit(solution)/shard_map/ppermute | solution.py:187
  1452.4 128.1 %collective-permute-start.43 = (bf16[896,2048]{1,0:T(8,128)(2,1)}, bf16[896,2048]{1,0:T(8,128)(2,1)}, u32[]{:S(2)}, u32[]{:S(2)}) collective-permute-start(bf16[896,2048]{1,0:T(8,128)(2,1)} %bitcast.61.refs_0_), channel_id=1, source_target_pairs={{0,1},{1,0},{2,3},{3,2},{4,5},{5,4},{6,7},{7,6}} | collective-permute-start | bytes 11010056 | tf_op jit(solution)/shard_map/ppermute | solution.py:190
  1452.4 128.1 %collective-permute-start.47 = (bf16[896,2048]{1,0:T(8,128)(2,1)}, bf16[896,2048]{1,0:T(8,128)(2,1)}, u32[]{:S(2)}, u32[]{:S(2)}) collective-permute-start(bf16[896,2048]{1,0:T(8,128)(2,1)} %constant_dynamic-update-slice_fusion.2.refs_0_), channel_id=1, source_target_pairs={{0,2},{1,3},{2,0},{3,1},{4,6},{5,7},{6,4},{7,5}} | collective-permute-start | bytes 11010056 | tf_op jit(solution)/shard_map/ppermute | solution.py:187
  1570.8 161.2 %collective-permute-start.49 = (bf16[1024,3584]{1,0:T(8,128)(2,1)}, bf16[1024,3584]{1,0:T(8,128)(2,1)}, u32[]{:S(2)}, u32[]{:S(2)}) collective-permute-start(bf16[1024,3584]{1,0:T(8,128)(2,1)} %pad_maximum_fusion.6.h_ref), channel_id=1, source_target_pairs={{0,4},{4,0},{1,5},{5,1},{2,6},{6,2},{3,7},{7,3}} | collective-permute-start | bytes 22020104 | tf_op jit(solution)/shard_map/ppermute | solution.py:193
  1572.5 84.5 %collective-permute-start.51 = (bf16[2048,896]{1,0:T(8,128)(2,1)}, bf16[2048,896]{1,0:T(8,128)(2,1)}, u32[]{:S(2)}, u32[]{:S(2)}) collective-permute-start(bf16[2048,896]{1,0:T(8,128)(2,1)} %bitcast.25), channel_id=1, source_target_pairs={{0,2},{1,3},{2,0},{3,1},{4,6},{5,7},{6,4},{7,5}} | collective-permute-start | bytes 11010056 | tf_op jit(solution)/shard_map/ppermute | solution.py:187
  1580.5 78.3 %collective-permute-start.46 = (bf16[896,2048]{1,0:T(8,128)(2,1)}, bf16[896,2048]{1,0:T(8,128)(2,1)}, u32[]{:S(2)}, u32[]{:S(2)}) collective-permute-start(bf16[896,2048]{1,0:T(8,128)(2,1)} %constant_dynamic-update-slice_fusion.2.refs_0_), channel_id=1, source_target_pairs={{0,1},{1,0},{2,3},{3,2},{4,5},{5,4},{6,7},{7,6}} | collective-permute-start | bytes 11010056 | tf_op jit(solution)/shard_map/ppermute | solution.py:190
  1588.7 262.8 %collective-permute-start.50 = (bf16[2048,896]{1,0:T(8,128)(2,1)}, bf16[2048,896]{1,0:T(8,128)(2,1)}, u32[]{:S(2)}, u32[]{:S(2)}) collective-permute-start(bf16[2048,896]{1,0:T(8,128)(2,1)} %bitcast.25), channel_id=1, source_target_pairs={{0,1},{1,0},{2,3},{3,2},{4,5},{5,4},{6,7},{7,6}} | collective-permute-start | bytes 11010056 | tf_op jit(solution)/shard_map/ppermute | solution.py:190
  1657.0 186.2 %collective-permute-start.54 = (bf16[2048,896]{1,0:T(8,128)(2,1)}, bf16[2048,896]{1,0:T(8,128)(2,1)}, u32[]{:S(2)}, u32[]{:S(2)}) collective-permute-start(bf16[2048,896]{1,0:T(8,128)(2,1)} %bitcast.25), channel_id=1, source_target_pairs={{0,4},{4,0},{1,5},{5,1},{2,6},{6,2},{3,7},{7,3}} | collective-permute-start | bytes 11010056 | tf_op jit(solution)/shard_map/ppermute | solution.py:193
  1658.8 186.1 %collective-permute-start.52 = (bf16[2048,896]{1,0:T(8,128)(2,1)}, bf16[2048,896]{1,0:T(8,128)(2,1)}, u32[]{:S(2)}, u32[]{:S(2)}) collective-permute-start(bf16[2048,896]{1,0:T(8,128)(2,1)} %collective-permute-done.51), channel_id=1, source_target_pairs={{0,1},{1,0},{2,3},{3,2},{4,5},{5,4},{6,7},{7,6}} | collective-permute-start | bytes 11010056 | tf_op jit(solution)/shard_map/ppermute | solution.py:190
  1801.0 185.6 %collective-permute-start.53 = (bf16[2,512,2048]{2,1,0:T(8,128)(2,1)}, bf16[2,512,2048]{2,1,0:T(8,128)(2,1)}, u32[]{:S(2)}, u32[]{:S(2)}) collective-permute-start(bf16[2,512,2048]{2,1,0:T(8,128)(2,1)} %shard_map.128), channel_id=1, source_target_pairs={{0,4},{4,0},{1,5},{5,1},{2,6},{6,2},{3,7},{7,3}} | collective-permute-start | bytes 12582920 | tf_op jit(solution)/shard_map/ppermute | solution.py:193
  1802.7 175.2 %collective-permute-start.56 = (bf16[2048,896]{1,0:T(8,128)(2,1)}, bf16[2048,896]{1,0:T(8,128)(2,1)}, u32[]{:S(2)}, u32[]{:S(2)}) collective-permute-start(bf16[2048,896]{1,0:T(8,128)(2,1)} %collective-permute-done.51), channel_id=1, source_target_pairs={{0,4},{4,0},{1,5},{5,1},{2,6},{6,2},{3,7},{7,3}} | collective-permute-start | bytes 11010056 | tf_op jit(solution)/shard_map/ppermute | solution.py:193
  1843.2 182.1 %collective-permute-start.60 = (bf16[896,4096]{1,0:T(8,128)(2,1)}, bf16[896,4096]{1,0:T(8,128)(2,1)}, u32[]{:S(2)}, u32[]{:S(2)}) collective-permute-start(bf16[896,4096]{1,0:T(8,128)(2,1)} %pad_maximum_fusion.8.refs_0_.refs_4_), channel_id=1, source_target_pairs={{0,2},{1,3},{2,0},{3,1},{4,6},{5,7},{6,4},{7,5}} | collective-permute-start | bytes 22020104 | tf_op jit(solution)/shard_map/ppermute | solution.py:187
  1844.9 158.2 %collective-permute-start.55 = (bf16[2048,896]{1,0:T(8,128)(2,1)}, bf16[2048,896]{1,0:T(8,128)(2,1)S(1)}, u32[]{:S(2)}, u32[]{:S(2)}) collective-permute-start(bf16[2048,896]{1,0:T(8,128)(2,1)} %collective-permute-done.54), channel_id=1, source_target_pairs={{0,1},{1,0},{2,3},{3,2},{4,5},{5,4},{6,7},{7,6}} | collective-permute-start | bytes 11010056 | tf_op jit(solution)/shard_map/ppermute | solution.py:190
  1851.5 181.8 %collective-permute-start.59 = (bf16[896,4096]{1,0:T(8,128)(2,1)}, bf16[896,4096]{1,0:T(8,128)(2,1)}, u32[]{:S(2)}, u32[]{:S(2)}) collective-permute-start(bf16[896,4096]{1,0:T(8,128)(2,1)} %pad_maximum_fusion.8.refs_0_.refs_4_), channel_id=1, source_target_pairs={{0,1},{1,0},{2,3},{3,2},{4,5},{5,4},{6,7},{7,6}} | collective-permute-start | bytes 22020104 | tf_op jit(solution)/shard_map/ppermute | solution.py:190
  2031.7 160.2 %collective-permute-start.63 = (bf16[896,4096]{1,0:T(8,128)(2,1)}, bf16[896,4096]{1,0:T(8,128)(2,1)}, u32[]{:S(2)}, u32[]{:S(2)}) collective-permute-start(bf16[896,4096]{1,0:T(8,128)(2,1)} %pad_maximum_fusion.9.refs_0_.refs_4_), channel_id=1, source_target_pairs={{0,2},{1,3},{2,0},{3,1},{4,6},{5,7},{6,4},{7,5}} | collective-permute-start | bytes 22020104 | tf_op jit(solution)/shard_map/ppermute | solution.py:187
  2033.4 167.8 %collective-permute-start.62 = (bf16[896,4096]{1,0:T(8,128)(2,1)}, bf16[896,4096]{1,0:T(8,128)(2,1)}, u32[]{:S(2)}, u32[]{:S(2)}) collective-permute-start(bf16[896,4096]{1,0:T(8,128)(2,1)} %pad_maximum_fusion.9.refs_0_.refs_4_), channel_id=1, source_target_pairs={{0,1},{1,0},{2,3},{3,2},{4,5},{5,4},{6,7},{7,6}} | collective-permute-start | bytes 22020104 | tf_op jit(solution)/shard_map/ppermute | solution.py:190
  2191.9 160.7 %collective-permute-start.58 = (bf16[1024,3584]{1,0:T(8,128)(2,1)}, bf16[1024,3584]{1,0:T(8,128)(2,1)}, u32[]{:S(2)}, u32[]{:S(2)}) collective-permute-start(bf16[1024,3584]{1,0:T(8,128)(2,1)} %pad_maximum_fusion.7.h_ref), channel_id=1, source_target_pairs={{0,4},{4,0},{1,5},{5,1},{2,6},{6,2},{3,7},{7,3}} | collective-permute-start | bytes 22020104 | tf_op jit(solution)/shard_map/ppermute | solution.py:193
  2199.7 228.3 %collective-permute-start.66 = (bf16[896,3072]{1,0:T(8,128)(2,1)}, bf16[896,3072]{1,0:T(8,128)(2,1)}, u32[]{:S(2)}, u32[]{:S(2)}) collective-permute-start(bf16[896,3072]{1,0:T(8,128)(2,1)} %pad_maximum_fusion.10.refs_0_.refs_4_), channel_id=1, source_target_pairs={{0,2},{1,3},{2,0},{3,1},{4,6},{5,7},{6,4},{7,5}} | collective-permute-start | bytes 16515080 | tf_op jit(solution)/shard_map/ppermute | solution.py:187
  2201.2 231.3 %collective-permute-start.65 = (bf16[896,3072]{1,0:T(8,128)(2,1)}, bf16[896,3072]{1,0:T(8,128)(2,1)}, u32[]{:S(2)}, u32[]{:S(2)}) collective-permute-start(bf16[896,3072]{1,0:T(8,128)(2,1)} %pad_maximum_fusion.10.refs_0_.refs_4_), channel_id=1, source_target_pairs={{0,1},{1,0},{2,3},{3,2},{4,5},{5,4},{6,7},{7,6}} | collective-permute-start | bytes 16515080 | tf_op jit(solution)/shard_map/ppermute | solution.py:190
  2430.6 81.9 %collective-permute-start.69 = (bf16[896,2048]{1,0:T(8,128)(2,1)S(1)}, bf16[896,2048]{1,0:T(8,128)(2,1)}, u32[]{:S(2)}, u32[]{:S(2)}) collective-permute-start(bf16[896,2048]{1,0:T(8,128)(2,1)S(1)} %pad_maximum_fusion.16.refs_0_.refs_4_), channel_id=1, source_target_pairs={{0,2},{1,3},{2,0},{3,1},{4,6},{5,7},{6,4},{7,5}} | collective-permute-start | bytes 11010056 | tf_op jit(solution)/shard_map/ppermute | solution.py:187
  2432.3 85.5 %collective-permute-start.68 = (bf16[896,2048]{1,0:T(8,128)(2,1)S(1)}, bf16[896,2048]{1,0:T(8,128)(2,1)}, u32[]{:S(2)}, u32[]{:S(2)}) collective-permute-start(bf16[896,2048]{1,0:T(8,128)(2,1)S(1)} %pad_maximum_fusion.16.refs_0_.refs_4_), channel_id=1, source_target_pairs={{0,1},{1,0},{2,3},{3,2},{4,5},{5,4},{6,7},{7,6}} | collective-permute-start | bytes 11010056 | tf_op jit(solution)/shard_map/ppermute | solution.py:190
  2517.4 159.2 %collective-permute-start.74 = (bf16[7168,384]{1,0:T(8,128)(2,1)}, bf16[7168,384]{1,0:T(8,128)(2,1)}, u32[]{:S(2)}, u32[]{:S(2)}) collective-permute-start(bf16[7168,384]{1,0:T(8,128)(2,1)} %get-tuple-element.175), channel_id=1, source_target_pairs={{0,2},{1,3},{2,0},{3,1},{4,6},{5,7},{6,4},{7,5}} | collective-permute-start | bytes 16515080 | tf_op jit(solution)/shard_map/ppermute | solution.py:187
  2517.8 201.7 %collective-permute-start.79 = (bf16[7168,384]{1,0:T(8,128)(2,1)}, bf16[7168,384]{1,0:T(8,128)(2,1)}, u32[]{:S(2)}, u32[]{:S(2)}) collective-permute-start(bf16[7168,384]{1,0:T(8,128)(2,1)} %get-tuple-element.175), channel_id=1, source_target_pairs={{0,1},{1,0},{2,3},{3,2},{4,5},{5,4},{6,7},{7,6}} | collective-permute-start | bytes 16515080 | tf_op jit(solution)/shard_map/ppermute | solution.py:190
  2565.3 181.0 %collective-permute-start.80 = (bf16[7168,256]{1,0:T(8,128)(2,1)}, bf16[7168,256]{1,0:T(8,128)(2,1)}, u32[]{:S(2)}, u32[]{:S(2)}) collective-permute-start(bf16[7168,256]{1,0:T(8,128)(2,1)} %get-tuple-element.177), channel_id=1, source_target_pairs={{0,1},{1,0},{2,3},{3,2},{4,5},{5,4},{6,7},{7,6}} | collective-permute-start | bytes 11010056 | tf_op jit(solution)/shard_map/ppermute | solution.py:190
  2565.8 231.0 %collective-permute-start.78 = (bf16[7168,256]{1,0:T(8,128)(2,1)}, bf16[7168,256]{1,0:T(8,128)(2,1)}, u32[]{:S(2)}, u32[]{:S(2)}) collective-permute-start(bf16[7168,256]{1,0:T(8,128)(2,1)} %get-tuple-element.177), channel_id=1, source_target_pairs={{0,2},{1,3},{2,0},{3,1},{4,6},{5,7},{6,4},{7,5}} | collective-permute-start | bytes 11010056 | tf_op jit(solution)/shard_map/ppermute | solution.py:187
  2567.5 143.3 %collective-permute-start.81 = (bf16[7168,256]{1,0:T(8,128)(2,1)}, bf16[7168,256]{1,0:T(8,128)(2,1)}, u32[]{:S(2)}, u32[]{:S(2)}) collective-permute-start(bf16[7168,256]{1,0:T(8,128)(2,1)} %get-tuple-element.178), channel_id=1, source_target_pairs={{0,1},{1,0},{2,3},{3,2},{4,5},{5,4},{6,7},{7,6}} | collective-permute-start | bytes 11010056 | tf_op jit(solution)/shard_map/ppermute | solution.py:190
  2710.8 142.5 %collective-permute-start.77 = (bf16[7168,256]{1,0:T(8,128)(2,1)S(1)}, bf16[7168,256]{1,0:T(8,128)(2,1)}, u32[]{:S(2)}, u32[]{:S(2)}) collective-permute-start(bf16[7168,256]{1,0:T(8,128)(2,1)S(1)} %copy-done.36), channel_id=1, source_target_pairs={{0,2},{1,3},{2,0},{3,1},{4,6},{5,7},{6,4},{7,5}} | collective-permute-start | bytes 11010056 | tf_op jit(solution)/shard_map/ppermute | solution.py:187
  2719.4 180.4 %collective-permute-start.89 = (f32[1024,384]{1,0:T(8,128)}, f32[1024,384]{1,0:T(8,128)}, u32[]{:S(2)}, u32[]{:S(2)}) collective-permute-start(f32[1024,384]{1,0:T(8,128)} %fusion.121), channel_id=1, source_target_pairs={{0,4},{4,0},{1,5},{5,1},{2,6},{6,2},{3,7},{7,3}} | collective-permute-start | bytes 4718600 | tf_op jit(solution)/shard_map/ppermute | solution.py:193
  2731.9 167.4 %collective-permute-start.88 = (f32[1024,256]{1,0:T(8,128)}, f32[1024,256]{1,0:T(8,128)}, u32[]{:S(2)}, u32[]{:S(2)}) collective-permute-start(f32[1024,256]{1,0:T(8,128)} %fusion.136), channel_id=1, source_target_pairs={{0,4},{4,0},{1,5},{5,1},{2,6},{6,2},{3,7},{7,3}} | collective-permute-start | bytes 3145736 | tf_op jit(solution)/shard_map/ppermute | solution.py:193
  2746.3 245.5 %collective-permute-start.84 = (f32[1024,384]{1,0:T(8,128)}, f32[1024,384]{1,0:T(8,128)}, u32[]{:S(2)}, u32[]{:S(2)}) collective-permute-start(f32[1024,384]{1,0:T(8,128)} %fusion.134), channel_id=1, source_target_pairs={{0,4},{4,0},{1,5},{5,1},{2,6},{6,2},{3,7},{7,3}} | collective-permute-start | bytes 4718600 | tf_op jit(solution)/shard_map/ppermute | solution.py:193
  2832.5 159.8 %collective-permute-start.76 = (f32[1024,384]{1,0:T(8,128)}, f32[1024,384]{1,0:T(8,128)}, u32[]{:S(2)}, u32[]{:S(2)}) collective-permute-start(f32[1024,384]{1,0:T(8,128)} %fusion.99), channel_id=1, source_target_pairs={{0,4},{4,0},{1,5},{5,1},{2,6},{6,2},{3,7},{7,3}} | collective-permute-start | bytes 4718600 | tf_op jit(solution)/shard_map/ppermute | solution.py:193
  2945.3 112.5 %collective-permute-start.91 = (f32[1024,256]{1,0:T(8,128)}, f32[1024,256]{1,0:T(8,128)}, u32[]{:S(2)}, u32[]{:S(2)}) collective-permute-start(f32[1024,256]{1,0:T(8,128)} %fusion.126), channel_id=1, source_target_pairs={{0,4},{4,0},{1,5},{5,1},{2,6},{6,2},{3,7},{7,3}} | collective-permute-start | bytes 3145736 | tf_op jit(solution)/shard_map/ppermute | solution.py:193
  2991.8 87.7 %collective-permute-start.94 = (f32[1024,256]{1,0:T(8,128)}, f32[1024,256]{1,0:T(8,128)}, u32[]{:S(2)}, u32[]{:S(2)}) collective-permute-start(f32[1024,256]{1,0:T(8,128)} %fusion.131), channel_id=1, source_target_pairs={{0,4},{4,0},{1,5},{5,1},{2,6},{6,2},{3,7},{7,3}} | collective-permute-start | bytes 3145736 | tf_op jit(solution)/shard_map/ppermute | solution.py:193
  (127 other events, 3484.6 us)
